TPU v7x, 256 devices: a whole 4x4x8 slice. The times are simulated.
256 devices in a mesh: span: 64 (over y, z, core), depth: 4 (over x).
Axes of the slice: x: 4, y: 4, z: 8, core: 2. Of those that a mesh axis runs over, the one named last changes fastest.
Arguments:
- part_slab: int32 [4, 524288, 1], P('depth', 'span'), may hold values from 0 to 63; in each aligned block of 8192 rows (0 to 8191, 8192 to 16383, ..., all dimensions but the last counted through in order) at most 256 rows name the same one
- part_cell: int32 [4, 524288], P('depth', 'span'), may hold values from 0 to 65535
- part_volume: float32 [4, 524288], P('depth', 'span'), may hold values from 0.05 to 0.6
- part_drag: float32 [3, 4, 524288], P(None, 'depth', 'span'), may hold values from -6 to 6
- part_count: int32 [4, 64], P('depth', 'span'), may hold values from 7168 to 8192
- prior_solid: float32 [8, 1024, 2048], P(None, 'span', 'depth'), may hold values from 0 to 0.6
- prior_drag: float32 [3, 8, 1024, 2048], P(None, None, 'span', 'depth'), may hold values from -4 to 4
Outputs:
- fields: float32 [4, 8, 1024, 2048], P(None, None, 'span', 'depth')
- feedback: float32 [4, 4, 524288], P(None, 'depth', 'span')
Inputs may be any that keep to these rules, and one draw needn't show every extreme that they name: `part_slab`: among the 8192 particle slots of one owner device, live or not, no slab is named more than 256 times; in every draw some device names a slab exactly 256 times.
All inputs are finite; a program needn't handle non-finite values.
Results may differ from a plain program's by a relative error of at most 0.0003.
Values sent between devices are 32-bit elements; how exact they have to be, the bound alone decides.
No kernel may reach another device: no remote copies, remote signals or barrier semaphores. Data moves between devices by JAX's collectives and lax.ppermute only.
A program may use at most 128 MiB of HBM per device.

v0:
```python
import math

import jax
import jax.numpy as jnp
from jax import lax
from jax.sharding import PartitionSpec as P

SWEEPS = 6


NU_WEIGHT = 1.0
PHI_LIMIT = 0.6


def padded_2(array, sides, width):
    for axis, dim in sides:
        count, length = (lax.axis_size(axis), array.shape[dim])
        up = [(i, (i + 1) % count) for i in range(count - 1)]
        down = [(j, i) for i, j in up]
        last = lax.slice_in_dim(array, length - width, length, axis=dim)
        first = lax.slice_in_dim(array, 0, width, axis=dim)
        before = lax.ppermute(last, axis, up)
        after = lax.ppermute(first, axis, down)
        array = jnp.concatenate([before, array, after], axis=dim)
    return array


def relax_once(source, padded):
    beside = padded[:, :, 2:, 1:-1] + padded[:, :, :-2, 1:-1]
    beside = beside + padded[:, :, 1:-1, 2:] + padded[:, :, 1:-1, :-2]
    return (source + NU_WEIGHT * beside) / (1.0 + 4.0 * NU_WEIGHT)


def exact_inner(left, right):
    return lax.dot_general(
        left,
        right,
        (((0,), (0,)), ((), ())),
        precision=lax.Precision.HIGH,
        preferred_element_type=jnp.float32,
    )


def on_device(part_slab, part_cell, part_volume, part_drag, part_count, prior_solid, prior_drag):
    span_size = lax.axis_size("span")
    depth_size = lax.axis_size("depth")
    part_rows = part_cell.shape[1]
    capacity = 2 * part_rows // span_size
    total_slots = span_size * capacity
    layers, width_x, width_y = prior_solid.shape
    cell_total = layers * width_x * width_y
    low_count = math.gcd(cell_total, 128)
    high_count = cell_total // low_count
    part_block = math.gcd(part_rows, 512)
    part_blocks = part_rows // part_block
    slot_block = math.gcd(total_slots, 1024)
    slot_blocks = total_slots // slot_block
    owners = jnp.arange(span_size, dtype=jnp.int32)
    slot_range = jnp.arange(capacity, dtype=jnp.int32)
    high_range = jnp.arange(high_count, dtype=jnp.int32)
    low_range = jnp.arange(low_count, dtype=jnp.int32)
    row_local = jnp.arange(part_block, dtype=jnp.int32)
    lower_tri = (row_local[:, None] > row_local[None, :]).astype(jnp.bfloat16)
    within = jnp.arange(part_rows, dtype=jnp.int32)
    live_flag = within < part_count[0, 0]
    slab_blocks = part_slab[0, :, 0].reshape(part_blocks, part_block)
    live_blocks = live_flag.reshape(part_blocks, part_block)
    payload = jnp.concatenate(
        [part_cell[0].astype(jnp.float32)[None], part_volume, part_drag[:, 0, :]], axis=0
    )
    payload_blocks = payload.reshape(5, part_blocks, part_block).transpose(1, 0, 2)

    def pack_step(carry, inputs):
        offset, packed = carry
        slab_piece, live_piece, load_piece = inputs
        member = (slab_piece[:, None] == owners[None, :]) & live_piece[:, None]
        member_f = member.astype(jnp.float32)
        before = jnp.dot(lower_tri, member.astype(jnp.bfloat16), preferred_element_type=jnp.float32)
        position = jnp.sum((before + offset[None, :]) * member_f, axis=1).astype(jnp.int32)
        slot_hot = (position[:, None] == slot_range[None, :]).astype(jnp.float32)
        pieces = [exact_inner(member_f * load_piece[comp][:, None], slot_hot) for comp in range(5)]
        packed = packed + jnp.stack(pieces, axis=0)
        offset = offset + jnp.sum(member_f, axis=0)
        return ((offset, packed), position)

    start_carry = (
        jnp.zeros((span_size,), jnp.float32),
        jnp.zeros((5, span_size, capacity), jnp.float32),
    )
    (final_offset, packed), positions = lax.scan(
        pack_step, start_carry, (slab_blocks, live_blocks, payload_blocks)
    )
    send_ids = packed[0].astype(jnp.int32).reshape(1, span_size, capacity)
    send_loads = packed[1:]
    recv_ids, recv_loads = (
        lax.all_to_all(send_ids, "span", split_axis=1, concat_axis=1, tiled=True),
        lax.all_to_all(send_loads, "span", split_axis=1, concat_axis=1, tiled=True),
    )
    slot_cells = recv_ids.reshape(slot_blocks, slot_block)
    load_blocks = recv_loads.reshape(4, slot_blocks, slot_block).transpose(1, 0, 2)

    def deposit_step(total, inputs):
        cells, loads = inputs
        high_hot = ((cells // low_count)[:, None] == high_range[None, :]).astype(jnp.float32)
        low_hot = ((cells % low_count)[:, None] == low_range[None, :]).astype(jnp.float32)
        pieces = [exact_inner(high_hot * loads[comp][:, None], low_hot) for comp in range(4)]
        return (total + jnp.stack(pieces, axis=0), 0)

    deposit, unused = lax.scan(
        deposit_step, jnp.zeros((4, high_count, low_count), jnp.float32), (slot_cells, load_blocks)
    )
    deposit = deposit.reshape(4, layers, width_x, width_y)
    target = jnp.concatenate([jnp.minimum(deposit[:1], PHI_LIMIT), deposit[1:]], axis=0)
    smooth = jnp.concatenate([prior_solid[None], prior_drag], axis=0)
    rim_width = 3
    row_ids = (
        lax.axis_index("span") * width_x
        - rim_width
        + jnp.arange(width_x + 2 * rim_width, dtype=jnp.int32)
    )
    col_ids = (
        lax.axis_index("depth") * width_y
        - rim_width
        + jnp.arange(width_y + 2 * rim_width, dtype=jnp.int32)
    )
    row_inside = (row_ids >= 0) & (row_ids < span_size * width_x)
    col_inside = (col_ids >= 0) & (col_ids < depth_size * width_y)
    inside = (row_inside[:, None] & col_inside[None, :]).astype(jnp.float32)
    stacked = padded_2(
        jnp.concatenate([smooth, target], axis=0), (("span", 2), ("depth", 3)), rim_width
    )
    padded = stacked[:4]
    target_wide = stacked[4:]
    for round_index in range(SWEEPS // rim_width):
        if round_index > 0:
            padded = padded_2(smooth, (("span", 2), ("depth", 3)), rim_width)
        for inner_step in range(rim_width):
            edge_offset = inner_step + 1
            size_x = width_x + 2 * (rim_width - edge_offset)
            size_y = width_y + 2 * (rim_width - edge_offset)
            region = target_wide[
                :, :, edge_offset : edge_offset + size_x, edge_offset : edge_offset + size_y
            ]
            keeper = inside[edge_offset : edge_offset + size_x, edge_offset : edge_offset + size_y]
            padded = relax_once(region, padded) * keeper[None, None]
        smooth = padded
    void_fraction = 1.0 - smooth[0]
    fields = jnp.concatenate([void_fraction[None], -smooth[1:] / void_fraction[None]], axis=0)
    field_table = fields.reshape(4, cell_total)
    slot_index = recv_ids.reshape(total_slots).astype(jnp.int32)
    values = field_table[:, slot_index].reshape(4, span_size, capacity)
    returned = lax.all_to_all(values, "span", split_axis=1, concat_axis=1, tiled=True)
    flat_returned = returned.reshape(4, total_slots)
    slab_flat = part_slab[0, :, 0]
    position_flat = jnp.clip(positions.reshape(part_rows), 0, capacity - 1)
    back_index = slab_flat * capacity + position_flat
    picked = flat_returned[:, back_index] * live_flag.astype(jnp.float32)[None, :]
    return (fields, picked.reshape(4, 1, part_rows))


def solution(mesh):
    in_specs = (
        P("depth", "span", None),
        P("depth", "span"),
        P("depth", "span"),
        P(None, "depth", "span"),
        P("depth", "span"),
        P(None, "span", "depth"),
        P(None, None, "span", "depth"),
    )
    out_specs = (P(None, None, "span", "depth"), P(None, "depth", "span"))
    return jax.shard_map(
        on_device, mesh=mesh, in_specs=in_specs, out_specs=out_specs, check_vma=False
    )
```

profile of v0, /device:TPU:1, one launch (start us, length us, event | category | flops | bytes accessed | tf_op | source)
XLA Modules:
  0.0 424.5 jit_solution(14079696404201102471)
XLA Ops:
  6.2 35.9 %while.30 = (s32[]{:T(128)}, f32[64]{0:T(128)S(1)}, f32[5,64,256]{2,1,0:T(8,128)S(1)}, s32[16,512]{1,0:T(8,128)S(1)}, s32[16,512]{1,0:T(8,128)S(1)}, /*index=5*/pred[16,512]{1,0:T(8,128)(4,1)S(1)}, f32[16,5,512]{2,0,1:T(8,128)S(1)}) while((s32[]{:T(128)}, f32[64]{0:T(128)S(1)}, f32[5,64,256]{2,1,0:T(8,128)S(1)}, ...), condition=%wide.region_3.4_spmd.clone.clone, body=%wide.region_0.3_spmd.clone.sunk.clone | while | flops 287408192 | bytes 1386664 | solution.py:90
  42.8 13.1 %all-to-all-start = ((s32[1,64,256]{2,0,1:T(1,128)}), s32[1,64,256]{2,0,1:T(1,128)S(1)}, u32[]{:S(2)}, u32[]{:S(2)}) async-start(s32[1,64,256]{2,0,1:T(1,128)} %copy.34), calls=%async_computation | async-start | bytes 131072 | tf_op jit(solution)/shard_map/all_to_all | solution.py:96
  56.9 8.8 %all-to-all-done = s32[1,64,256]{2,0,1:T(1,128)S(1)} async-done(((s32[1,64,256]{2,0,1:T(1,128)}), s32[1,64,256]{2,0,1:T(1,128)S(1)}, u32[]{:S(2)}, u32[]{:S(2)}) %all-to-all-start) | async-done | bytes 65568 | tf_op jit(solution)/shard_map/all_to_all | solution.py:96
  65.7 4.5 %all-to-all-start.1 = ((f32[4,64,256]{2,0,1:T(4,128)}), f32[4,64,256]{2,0,1:T(4,128)S(1)}, u32[]{:S(2)}, u32[]{:S(2)}) async-start(f32[4,64,256]{2,0,1:T(4,128)} %slice.257), calls=%async_computation.1 | async-start | bytes 524288 | tf_op jit(solution)/shard_map/all_to_all | solution.py:97
  71.2 11.0 %all-to-all-done.1 = f32[4,64,256]{2,0,1:T(4,128)S(1)} async-done(((f32[4,64,256]{2,0,1:T(4,128)}), f32[4,64,256]{2,0,1:T(4,128)S(1)}, u32[]{:S(2)}, u32[]{:S(2)}) %all-to-all-start.1) | async-done | bytes 262176 | tf_op jit(solution)/shard_map/all_to_all | solution.py:97
  82.3 113.6 %while.31 = (s32[]{:T(128)}, f32[4,512,128]{2,1,0:T(8,128)S(1)}, s32[16,1024]{1,0:T(8,128)S(1)}, f32[16,4,1024]{2,0,1:T(8,128)S(1)}) while((s32[]{:T(128)}, f32[4,512,128]{2,1,0:T(8,128)S(1)}, s32[16,1024]{1,0:T(8,128)S(1)}, f32[16,4,1024]{2,0,1:T(8,128)S(1)}) %tuple.99), condition=%wide.region_5.6_spmd.clone.clone, body=%wide.region_4.5_spmd.clone.sunk.clone | while | flops 1616661504 | bytes 4296823 | solution.py:109
  94.5 1.7 fusion.192
  96.6 1.7 fusion.193
  98.3 1.7 fusion.194
  101.6 1.7 fusion.192
  103.7 1.7 fusion.193
  105.4 1.7 fusion.194
  107.0 1.7 fusion.195
  108.7 1.7 fusion.192
  110.8 1.7 fusion.193
  133.8 1.7 fusion.194
  135.4 1.7 fusion.195
  151.3 1.7 fusion.192
  153.4 1.7 fusion.193
  197.4 3.5 collective-permute-start
  201.1 2.1 collective-permute-start.1
  205.9 4.3 %collective-permute-done.1 = f32[8,8,3,512]{3,1,2,0:T(8,128)S(1)} collective-permute-done((f32[8,8,3,512]{3,1,2,0:T(8,128)S(1)}, f32[8,8,3,512]{3,1,2,0:T(8,128)S(1)}, u32[]{:S(2)}, u32[]{:S(2)}) %collective-permute-start.1) | collective-permute-done | bytes 393248 | tf_op jit(solution)/shard_map/ppermute | solution.py:23
  212.1 2.3 copy.42
  214.3 3.7 collective-permute-start.2
  218.1 2.2 copy.43
  221.7 2.3 copy.44
  224.0 2.0 collective-permute-done.3
  226.0 2.3 copy.45
  228.2 5.1 %pad_maximum_fusion = f32[8,8,22,518]{3,2,1,0:T(8,128)S(1)} fusion(f32[8,8,22,3]{3,2,1,0:T(8,128)} %copy.45, f32[8,8,3,512]{3,2,1,0:T(4,128)} %copy-done.1, f32[3,8,16,512]{3,2,1,0:T(8,128)S(1)} %slice.204, f32[1,8,16,512]{3,2,1,0:T(8,128)S(1)} %min.29, f32[3,8,16,512]{3,2,1,0:T(8,128)S(1)} %copy-done, f32[1,8,16,512]{3,2,1,0:T(8,128)} %bitcast.178, ...), kind=kLoop, calls=%fused_computation.122 | loop fusion | flops 5105408 | bytes 5834752 | tf_op jit(solution)/shard_map/concatenate | solution.py:24
  233.4 2.5 fusion.117
  235.9 2.5 fusion.115
  239.6 3.9 collective-permute-start.4
  243.4 1.9 collective-permute-start.5
  246.7 4.4 %collective-permute-done.5 = f32[4,8,3,512]{3,2,1,0:T(4,128)S(1)} collective-permute-done((f32[4,8,3,512]{3,2,1,0:T(4,128)S(1)}, f32[4,8,3,512]{3,2,1,0:T(4,128)S(1)}, u32[]{:S(2)}, u32[]{:S(2)}) %collective-permute-start.5) | collective-permute-done | bytes 196640 | tf_op jit(solution)/shard_map/ppermute | solution.py:23
  251.4 2.5 collective-permute-start.6
  255.4 3.6 collective-permute-done.6
  259.0 4.1 collective-permute-done.7
  264.3 2.5 fusion.113
  266.8 2.5 fusion.111
  271.9 16.0 %copy.46 = f32[4,65536]{0,1:T(8,128)} copy(f32[4,65536]{1,0:T(4,128)S(1)} %pad_maximum_fusion.3) | data formatting | bytes 2097152 | tf_op jit(solution)/shard_map/concatenate | solution.py:148
  287.9 65.3 %gather_fusion = f32[16384,4]{1,0:T(8,128)} fusion(f32[4,65536]{0,1:T(8,128)} %copy.46, s32[16384]{0:T(1024)S(1)} %broadcast_clamp_fusion), kind=kCustom, calls=%fused_computation | custom fusion | bytes 589824 | tf_op jit(solution)/shard_map/gather | solution.py:151
  353.1 5.9 %copy.47 = f32[4,64,256]{2,0,1:T(4,128)} copy(f32[4,64,256]{0,2,1:T(8,128)} %bitcast.175) | data formatting | bytes 524288 | tf_op jit(solution)/shard_map/reshape | solution.py:151
  359.1 9.8 %all-to-all-start.2 = ((f32[4,64,256]{2,0,1:T(4,128)}), f32[4,64,256]{2,0,1:T(4,128)S(1)}, u32[]{:S(2)}, u32[]{:S(2)}) async-start(f32[4,64,256]{2,0,1:T(4,128)} %copy.47), calls=%async_computation.2 | async-start | bytes 524288 | tf_op jit(solution)/shard_map/all_to_all | solution.py:152
  370.0 10.8 %all-to-all-done.2 = f32[4,64,256]{2,0,1:T(4,128)S(1)} async-done(((f32[4,64,256]{2,0,1:T(4,128)}), f32[4,64,256]{2,0,1:T(4,128)S(1)}, u32[]{:S(2)}, u32[]{:S(2)}) %all-to-all-start.2) | async-done | bytes 262176 | tf_op jit(solution)/shard_map/all_to_all | solution.py:152
  380.8 4.8 %copy.48 = f32[4,64,256]{0,2,1:T(8,128)} copy(f32[4,64,256]{2,0,1:T(4,128)S(1)} %all-to-all-done.2) | data formatting | bytes 524288 | tf_op jit(solution)/shard_map/all_to_all | solution.py:152
  385.6 31.2 %gather_fusion.1 = f32[8192,4]{1,0:T(8,128)} fusion(f32[4,16384]{0,1:T(8,128)} %bitcast.174, s32[8192]{0:T(1024)S(1)} %broadcast_clamp_fusion.1), kind=kCustom, calls=%fused_computation.1 | custom fusion | bytes 294912 | tf_op jit(solution)/shard_map/gather | solution.py:157
  416.9 4.2 bitcast_multiply_fusion
  421.0 3.5 copy.49
  (418 shorter events, 149.1 us)
Async XLA Ops:
  42.8 22.9 %all-to-all-start = ((s32[1,64,256]{2,0,1:T(1,128)}), s32[1,64,256]{2,0,1:T(1,128)S(1)}, u32[]{:S(2)}, u32[]{:S(2)}) async-start(s32[1,64,256]{2,0,1:T(1,128)} %copy.34), calls=%async_computation | async-start | bytes 131072 | tf_op jit(solution)/shard_map/all_to_all | solution.py:96
  65.7 16.5 %all-to-all-start.1 = ((f32[4,64,256]{2,0,1:T(4,128)}), f32[4,64,256]{2,0,1:T(4,128)S(1)}, u32[]{:S(2)}, u32[]{:S(2)}) async-start(f32[4,64,256]{2,0,1:T(4,128)} %slice.257), calls=%async_computation.1 | async-start | bytes 524288 | tf_op jit(solution)/shard_map/all_to_all | solution.py:97
  195.9 1.1 copy-start
  195.9 1.2 copy-start.2
  197.4 13.0 %copy-start.3 = (f32[8,16,512]{2,1,0:T(8,128)S(1)}, f32[8,16,512]{2,1,0:T(8,128)}, u32[]{:S(2)}) copy-start(f32[8,16,512]{2,1,0:T(8,128)} %param.16) | copy-start | bytes 786436
  197.4 8.2 %collective-permute-start = (f32[8,8,3,512]{3,1,2,0:T(8,128)S(1)}, f32[8,8,3,512]{3,1,2,0:T(8,128)S(1)}, u32[]{:S(2)}, u32[]{:S(2)}) collective-permute-start(f32[8,8,3,512]{3,1,2,0:T(8,128)S(1)} %copy.38), channel_id=1, source_target_pairs={{0,4},{4,8},{8,12},{12,16},{16,20},{20,24},{24,28},{28,32},{32,36}... | collective-permute-start | bytes 1179656 | tf_op jit(solution)/shard_map/ppermute | solution.py:22
  201.1 9.1 %collective-permute-start.1 = (f32[8,8,3,512]{3,1,2,0:T(8,128)S(1)}, f32[8,8,3,512]{3,1,2,0:T(8,128)S(1)}, u32[]{:S(2)}, u32[]{:S(2)}) collective-permute-start(f32[8,8,3,512]{3,1,2,0:T(8,128)S(1)} %copy.39), channel_id=1, source_target_pairs={{4,0},{8,4},{12,8},{16,12},{20,16},{24,20},{28,24},{32,28},{36,32}... | collective-permute-start | bytes 1179656 | tf_op jit(solution)/shard_map/ppermute | solution.py:23
  210.5 1.6 copy-start.1
  214.3 7.4 %collective-permute-start.2 = (f32[8,8,22,3]{2,1,3,0:T(8,128)}, f32[8,8,22,3]{2,1,3,0:T(8,128)}, u32[]{:S(2)}, u32[]{:S(2)}) collective-permute-start(f32[8,8,22,3]{2,1,3,0:T(8,128)} %copy.42), channel_id=1, source_target_pairs={{0,1},{1,2},{2,3},{4,5},{5,6},{6,7},{8,9},{9,10},{10,11},{12,13},{... | collective-permute-start | bytes 50696 | tf_op jit(solution)/shard_map/ppermute | solution.py:22
  220.3 5.7 %collective-permute-start.3 = (f32[8,8,22,3]{2,1,3,0:T(8,128)}, f32[8,8,22,3]{2,1,3,0:T(8,128)}, u32[]{:S(2)}, u32[]{:S(2)}) collective-permute-start(f32[8,8,22,3]{2,1,3,0:T(8,128)} %copy.43), channel_id=1, source_target_pairs={{1,0},{2,1},{3,2},{5,4},{6,5},{7,6},{9,8},{10,9},{11,10},{13,12},{... | collective-permute-start | bytes 50696 | tf_op jit(solution)/shard_map/ppermute | solution.py:23
  233.3 2.5 copy-start.4
  235.9 2.5 copy-start.5
  239.6 7.2 %collective-permute-start.4 = (f32[4,8,3,512]{3,2,1,0:T(4,128)S(1)}, f32[4,8,3,512]{3,2,1,0:T(4,128)S(1)}, u32[]{:S(2)}, u32[]{:S(2)}) collective-permute-start(f32[4,8,3,512]{3,2,1,0:T(4,128)S(1)} %get-tuple-element.271), channel_id=1, source_target_pairs={{0,4},{4,8},{8,12},{12,16},{16,20},{20,24},{24,28},{28,32},{32,36}... | collective-permute-start | bytes 589832 | tf_op jit(solution)/shard_map/ppermute | solution.py:22
  243.4 7.7 %collective-permute-start.5 = (f32[4,8,3,512]{3,2,1,0:T(4,128)S(1)}, f32[4,8,3,512]{3,2,1,0:T(4,128)S(1)}, u32[]{:S(2)}, u32[]{:S(2)}) collective-permute-start(f32[4,8,3,512]{3,2,1,0:T(4,128)S(1)} %get-tuple-element.272), channel_id=1, source_target_pairs={{4,0},{8,4},{12,8},{16,12},{20,16},{24,20},{28,24},{32,28},{36,32}... | collective-permute-start | bytes 589832 | tf_op jit(solution)/shard_map/ppermute | solution.py:23
  251.4 7.6 %collective-permute-start.6 = (f32[4,8,22,3]{3,2,1,0:T(8,128)S(1)}, f32[4,8,22,3]{3,2,1,0:T(8,128)S(1)}, u32[]{:S(2)}, u32[]{:S(2)}) collective-permute-start(f32[4,8,22,3]{3,2,1,0:T(8,128)S(1)} %get-tuple-element.267), channel_id=1, source_target_pairs={{0,1},{1,2},{2,3},{4,5},{5,6},{6,7},{8,9},{9,10},{10,11},{12,13},{... | collective-permute-start | bytes 25352 | tf_op jit(solution)/shard_map/ppermute | solution.py:22
  253.9 9.2 %collective-permute-start.7 = (f32[4,8,22,3]{3,2,1,0:T(8,128)S(1)}, f32[4,8,22,3]{3,2,1,0:T(8,128)S(1)}, u32[]{:S(2)}, u32[]{:S(2)}) collective-permute-start(f32[4,8,22,3]{3,2,1,0:T(8,128)S(1)} %get-tuple-element.268), channel_id=1, source_target_pairs={{1,0},{2,1},{3,2},{5,4},{6,5},{7,6},{9,8},{10,9},{11,10},{13,12},{... | collective-permute-start | bytes 25352 | tf_op jit(solution)/shard_map/ppermute | solution.py:23
  353.1 15.7 %copy-start.6 = (s32[1,8192,1]{1,2,0:T(1,128)S(1)}, s32[1,8192,1]{1,2,0:T(1,128)}, u32[]{:S(2)}) copy-start(s32[1,8192,1]{1,2,0:T(1,128)} %param.11) | copy-start | bytes 98308
  353.1 15.7 %copy-start.7 = (s32[1,1,16,512]{3,1,2,0:T(1,128)S(1)}, s32[1,1,16,512]{3,1,2,0:T(1,128)}, u32[]{:S(2)}) copy-start(s32[1,1,16,512]{3,1,2,0:T(1,128)} %copy.64) | copy-start | bytes 98308
  359.1 21.7 %all-to-all-start.2 = ((f32[4,64,256]{2,0,1:T(4,128)}), f32[4,64,256]{2,0,1:T(4,128)S(1)}, u32[]{:S(2)}, u32[]{:S(2)}) async-start(f32[4,64,256]{2,0,1:T(4,128)} %copy.47), calls=%async_computation.2 | async-start | bytes 524288 | tf_op jit(solution)/shard_map/all_to_all | solution.py:152
where the time goes:
time: 426 us; the launch traced here: 425 us
  local copies, waits for them, and re-layouts  145 us (34%)
  matrix products  136 us (32%)
  waiting for transfers between devices  51.2 us (12%)
  starting transfers between devices  47.8 us (11%)
  other arithmetic  39.6 us (9%)
    dot_general x144, matrix products, exact_inner(): lax.dot_general(left, right, (((0,), (0,)), ((), ())), precision=lax.Prec...  132 us
    gather x1, local copies, waits for them, and re-layouts, on_device(): values = field_table[:, slot_index].reshape(4, span_size, capacity)  65.3 us
    gather x1, local copies, waits for them, and re-layouts, on_device(): flat_returned[:, back_index] * live_flag.astype(jnp.float32)[None, :]  31.2 us
    concatenate x1, local copies, waits for them, and re-layouts, on_device(): jnp.concatenate([void_fraction[None], -smooth[1:] / void_fraction[None]],...  16 us
    ppermute x4, waiting for transfers between devices, padded_2(): after = lax.ppermute(first, axis, down)  14.8 us
    ppermute x4, starting transfers between devices, padded_2(): before = lax.ppermute(last, axis, up)  13.6 us
    mul x9, other arithmetic, on_device(): padded = relax_once(region, padded) * keeper[None, None]  13.6 us
    all_to_all x1, starting transfers between devices, on_device(): lax.all_to_all(send_ids, 'span', split_axis=1, concat_axis=1, tiled=True)  13.1 us
  transfers between devices with their start and end apart: 11, of which 10 were waited for; matrix products, arithmetic and copies ran while one was open for 2% of the time, Pallas kernels for 0%

commit v1 on v0

v1 whole, which is shorter than its diff:
```python
import jax
import jax.numpy as jnp
from jax import lax
from jax.experimental import pallas as pl
from jax.experimental.pallas import tpu as pltpu
from jax.sharding import PartitionSpec as P

F32, BF16, I32 = jnp.float32, jnp.bfloat16, jnp.int32
OWNERS = 64
CAP = 256
LAYERS, CX, CY = 8, 16, 512
PARTS = 8192
HI, LO = 256, 256
ROWS = 2 * 5
BACK_ROWS = 8
SWEEPS = 6
PRIOR_RIM, TARGET_RIM = SWEEPS, SWEEPS - 1
PHI_LIMIT = 0.6


def halves(value):
    high = value.astype(BF16)
    return high, (value - high.astype(F32)).astype(BF16)


def spread(row, size):
    n = row.shape[1]
    packed = jnp.broadcast_to(row, (16, n)).astype(BF16)
    return jnp.broadcast_to(packed[None], (size // 16, 16, n)).reshape(size, n)


def index_rows(size, n):
    return lax.broadcasted_iota(I32, (size, n), 0).astype(F32).astype(BF16)


def row_is(row, size):
    return index_rows(size, row.shape[1]) == spread(row, size)


def one_hot(row, size):
    return jnp.where(row_is(row, size), jnp.ones((), BF16), jnp.zeros((), BF16))


def dot_nt(left, right):
    return lax.dot_general(left, right, (((1,), (1,)), ((), ())), preferred_element_type=F32)


def dot_nn(left, right):
    return lax.dot_general(left, right, (((1,), (0,)), ((), ())), preferred_element_type=F32)


PACK_BLOCK = 1024
SUB = 256


def pack_kernel(count_ref, slab_ref, cell_ref, volume_ref, drag_ref, out_ref, position_ref, acc):
    count = count_ref[0, 0]
    acc[...] = jnp.zeros_like(acc)
    before_mask = lax.broadcasted_iota(I32, (SUB, SUB + 128), 0)
    after_mask = lax.broadcasted_iota(I32, (SUB, SUB + 128), 1)
    upper = jnp.where((before_mask < after_mask) | (after_mask >= SUB), 1.0, 0.0).astype(BF16)

    def step(block, offset):
        hots, lefts = [], []
        for sub in range(PACK_BLOCK // SUB):
            start = pl.multiple_of(block * PACK_BLOCK + sub * SUB, SUB)
            spot = pl.ds(start, SUB)
            lane = lax.broadcasted_iota(I32, (1, SUB), 1) + start
            slab = jnp.where(lane < count, slab_ref[0:1, spot], OWNERS).astype(F32)
            member = row_is(slab, OWNERS)
            member_one = jnp.where(member, jnp.ones((), BF16), jnp.zeros((), BF16))
            ranks = dot_nn(member_one, upper)
            place = ranks[:, :SUB] + jnp.concatenate([offset, offset], axis=1)
            position = jnp.sum(place * member_one.astype(F32), axis=0, keepdims=True)
            offset = offset + ranks[:, SUB:]
            position_ref[0:1, spot] = position
            hots.append(one_hot(position, CAP))
            cell = cell_ref[0:1, spot]
            cell_high = lax.shift_right_logical(cell, 8)
            rows = [cell_high.astype(F32), (cell - cell_high * 256).astype(F32)]
            for value in [volume_ref[0:1, spot]] + [drag_ref[k, 0:1, spot] for k in range(3)]:
                high = value.astype(BF16).astype(F32)
                rows += [high, value - high]
            zero = jnp.zeros((), BF16)
            lefts.append(
                jnp.concatenate([jnp.where(member, spread(row, OWNERS), zero) for row in rows], axis=0)
            )
        acc[...] += dot_nt(jnp.concatenate(lefts, axis=1), jnp.concatenate(hots, axis=1))
        return offset

    lax.fori_loop(0, PARTS // PACK_BLOCK, step, jnp.zeros((OWNERS, 128), F32))
    for comp in range(5):
        high = acc[2 * comp * OWNERS : (2 * comp + 1) * OWNERS, :]
        low = acc[(2 * comp + 1) * OWNERS : (2 * comp + 2) * OWNERS, :]
        whole = high * 256.0 + low if comp == 0 else high + low
        for half in range(2):
            out_ref[pl.ds(2 * comp + half, OWNERS, stride=ROWS), :] = whole[:, half * 128 : (half + 1) * 128]


def pack(count, slab, cell, volume, drag):
    vmem = pl.BlockSpec(memory_space=pltpu.VMEM)
    return pl.pallas_call(
        pack_kernel,
        out_shape=(
            jax.ShapeDtypeStruct((OWNERS * ROWS, 128), F32),
            jax.ShapeDtypeStruct((1, PARTS), F32),
        ),
        in_specs=[pl.BlockSpec(memory_space=pltpu.SMEM), vmem, vmem, vmem, vmem],
        out_specs=(vmem, vmem),
        scratch_shapes=[pltpu.VMEM((10 * OWNERS, CAP), F32)],
        name="pack",
    )(count, slab, cell, volume, drag)


SOURCES_AT_ONCE = 4


def cell_split(cell):
    cell = cell.astype(I32)
    layer_x = lax.shift_right_logical(cell, 9)
    layer = lax.shift_right_logical(cell, 13)
    x = layer_x - layer * 16
    y_half = lax.shift_right_logical(cell, 8) - layer_x * 2
    high = (y_half * 16 + x) * 8 + layer
    low = cell - lax.shift_right_logical(cell, 8) * 256
    return high.astype(F32), low.astype(F32)


def source_row(ref, source, comp):
    base = source * ROWS + 2 * comp
    return jnp.concatenate([ref[pl.ds(base, 1), :], ref[pl.ds(base + 1, 1), :]], axis=1)


def deposit_kernel(recv_ref, out_ref, first_ref, last_ref):
    out_ref[...] = jnp.zeros_like(out_ref)
    zero = jnp.zeros((), BF16)

    def step(block, carry):
        lows, members, values = [], [], []
        for sub in range(SOURCES_AT_ONCE):
            source = block * SOURCES_AT_ONCE + sub
            high, low = cell_split(source_row(recv_ref, source, 0))
            lows.append(one_hot(low, LO))
            members.append(row_is(high, HI))
            parts = []
            for comp in range(4):
                value = source_row(recv_ref, source, comp + 1)
                top = value.astype(BF16).astype(F32)
                parts.append((top, value - top))
            values.append(parts)
        right = jnp.concatenate(lows, axis=1)
        right2 = jnp.concatenate([right, right], axis=1)
        for comp in range(4):
            left = [
                jnp.where(members[sub], spread(values[sub][comp][part], HI), zero)
                for part in range(2)
                for sub in range(SOURCES_AT_ONCE)
            ]
            out_ref[comp] += dot_nt(jnp.concatenate(left, axis=1), right2)
        return carry

    lax.fori_loop(0, OWNERS // SOURCES_AT_ONCE, step, 0)
    out_ref[0] = jnp.minimum(out_ref[0], PHI_LIMIT)
    for comp in range(4):
        for step_x in range(TARGET_RIM):
            spot = pl.ds((comp * TARGET_RIM + step_x) * LAYERS, LAYERS)
            for half in range(2):
                lanes = pl.ds(half * LO, LO)
                first_ref[spot, lanes] = out_ref[comp, pl.ds((half * CX + step_x) * LAYERS, LAYERS), :]
                x = CX - TARGET_RIM + step_x
                last_ref[spot, lanes] = out_ref[comp, pl.ds((half * CX + x) * LAYERS, LAYERS), :]


def deposit(received):
    vmem = pl.BlockSpec(memory_space=pltpu.VMEM)
    edge = jax.ShapeDtypeStruct((4 * TARGET_RIM * LAYERS, CY), F32)
    return pl.pallas_call(
        deposit_kernel,
        out_shape=(jax.ShapeDtypeStruct((4, HI, LO), F32), edge, edge),
        in_specs=[vmem],
        out_specs=(vmem, vmem, vmem),
        name="deposit",
    )(received)


GATHER_SOURCES = 2


def gather_kernel(table_ref, recv_ref, out_ref, tops, bottoms):
    for comp in range(4):
        tops[comp], bottoms[comp] = halves(table_ref[comp])

    def step(block, carry):
        highs, lows = [], []
        for sub in range(GATHER_SOURCES):
            high, low = cell_split(source_row(recv_ref, block * GATHER_SOURCES + sub, 0))
            highs.append(high)
            lows.append(one_hot(low, LO))
        low_hot = jnp.concatenate(lows, axis=1)
        high_row = jnp.concatenate(highs, axis=1)
        n = high_row.shape[1]
        member = lax.broadcasted_iota(I32, (HI, n), 0).astype(F32) == high_row
        rows = []
        for comp in range(4):
            value = dot_nn(tops[comp], low_hot) + dot_nn(bottoms[comp], low_hot)
            rows.append(jnp.sum(jnp.where(member, value, 0.0), axis=0, keepdims=True))
        for sub in range(GATHER_SOURCES):
            pieces = [
                row[:, sub * CAP + half * 128 : sub * CAP + (half + 1) * 128] for row in rows for half in range(2)
            ]
            start = pl.multiple_of((block * GATHER_SOURCES + sub) * BACK_ROWS, BACK_ROWS)
            out_ref[pl.ds(start, BACK_ROWS), :] = jnp.concatenate(pieces, axis=0)
        return carry

    lax.fori_loop(0, OWNERS // GATHER_SOURCES, step, 0)


def gather(table, received):
    vmem = pl.BlockSpec(memory_space=pltpu.VMEM)
    return pl.pallas_call(
        gather_kernel,
        out_shape=jax.ShapeDtypeStruct((OWNERS * BACK_ROWS, 128), F32),
        in_specs=[vmem, vmem],
        out_specs=vmem,
        scratch_shapes=[pltpu.VMEM((4, HI, LO), BF16)] * 2,
        name="gather",
    )(table, received)


PICK_BLOCK = 1024


def pick_kernel(count_ref, slab_ref, position_ref, back_ref, out_ref, tops, bottoms):
    count = count_ref[0, 0]
    for comp in range(4):
        tile = jnp.concatenate(
            [back_ref[pl.ds(2 * comp + half, OWNERS, stride=BACK_ROWS), :] for half in range(2)], axis=1
        )
        high, low = halves(tile)
        tops[comp * OWNERS : (comp + 1) * OWNERS, :] = high
        bottoms[comp * OWNERS : (comp + 1) * OWNERS, :] = low

    def step(block, carry):
        start = pl.multiple_of(block * PICK_BLOCK, PICK_BLOCK)
        spot = pl.ds(start, PICK_BLOCK)
        lane = lax.broadcasted_iota(I32, (1, PICK_BLOCK), 1) + start
        slab = jnp.where(lane < count, slab_ref[0:1, spot], OWNERS)
        position_hot = one_hot(position_ref[0:1, spot], CAP)
        value = dot_nn(tops[...], position_hot) + dot_nn(bottoms[...], position_hot)
        member = lax.broadcasted_iota(I32, (OWNERS, PICK_BLOCK), 0) == slab
        for comp in range(4):
            piece = value[comp * OWNERS : (comp + 1) * OWNERS, :]
            out_ref[comp, 0:1, spot] = jnp.sum(jnp.where(member, piece, 0.0), axis=0, keepdims=True)
        return carry

    lax.fori_loop(0, PARTS // PICK_BLOCK, step, 0)


def pick(count, slab, position, back):
    vmem = pl.BlockSpec(memory_space=pltpu.VMEM)
    return pl.pallas_call(
        pick_kernel,
        out_shape=jax.ShapeDtypeStruct((4, 1, PARTS), F32),
        in_specs=[pl.BlockSpec(memory_space=pltpu.SMEM), vmem, vmem, vmem],
        out_specs=vmem,
        scratch_shapes=[pltpu.VMEM((4 * OWNERS, CAP), BF16)] * 2,
        name="pick",
    )(count, slab, position, back)


def prior_kernel(solid_ref, drag_ref, rows_ref, first_ref, last_ref):
    for comp in range(4):
        for x in range(CX):
            row = solid_ref[:, x, :] if comp == 0 else drag_ref[comp - 1, :, x, :]
            rows_ref[pl.ds((comp * CX + x) * LAYERS, LAYERS), :] = row
            if x < PRIOR_RIM:
                first_ref[pl.ds((comp * PRIOR_RIM + x) * LAYERS, LAYERS), :] = row
            if x >= CX - PRIOR_RIM:
                spot = (comp * PRIOR_RIM + x - CX + PRIOR_RIM) * LAYERS
                last_ref[pl.ds(spot, LAYERS), :] = row


def prior(solid, drag):
    vmem = pl.BlockSpec(memory_space=pltpu.VMEM)
    edge = jax.ShapeDtypeStruct((4 * PRIOR_RIM * LAYERS, CY), F32)
    return pl.pallas_call(
        prior_kernel,
        out_shape=(jax.ShapeDtypeStruct((4 * CX * LAYERS, CY), F32), edge, edge),
        in_specs=[vmem, vmem],
        out_specs=(vmem, vmem, vmem),
        name="prior",
    )(solid, drag)


def row_list():
    rows = []
    for comp in range(4):
        rows += [(comp, False, x) for x in range(-PRIOR_RIM, CX + PRIOR_RIM)]
        rows += [(comp, True, x) for x in range(-TARGET_RIM, CX + TARGET_RIM)]
    return rows


SIDE_ROWS = -(-len(row_list()) // 16)


def row_piece(refs, row, start, size):
    target, target_above, target_below, prior_rows, prior_above, prior_below = refs
    comp, is_target, x = row
    above, below, rim = (target_above, target_below, TARGET_RIM) if is_target else (prior_above, prior_below, PRIOR_RIM)
    lanes = pl.ds(start, size)
    if x < 0:
        return above[pl.ds((comp * rim + x + rim) * LAYERS, LAYERS), lanes]
    if x >= CX:
        return below[pl.ds((comp * rim + x - CX) * LAYERS, LAYERS), lanes]
    if is_target:
        half = start // LO
        return target[comp, pl.ds((half * CX + x) * LAYERS, LAYERS), pl.ds(start - half * LO, size)]
    return prior_rows[pl.ds((comp * CX + x) * LAYERS, LAYERS), lanes]


def sides_kernel(*refs):
    ins, (left_ref, right_ref) = refs[:6], refs[6:]
    lane = lax.broadcasted_iota(I32, (LAYERS, 128), 1)
    rows = row_list()
    for group in range(SIDE_ROWS):
        left = jnp.zeros((LAYERS, 128), F32)
        right = jnp.zeros((LAYERS, 128), F32)
        for place, row in enumerate(rows[16 * group : 16 * group + 16]):
            here = (lane >= 8 * place) & (lane < 8 * place + 8)
            first = row_piece(ins, row, 0, 128)
            last = row_piece(ins, row, CY - 128, 128)
            left = jnp.where(here, pltpu.roll(first, 8 * place, 1) if place else first, left)
            shift = (8 * place + 8) % 128
            right = jnp.where(here, pltpu.roll(last, shift, 1) if shift else last, right)
        spot = pl.ds(group * LAYERS, LAYERS)
        left_ref[spot, :] = left
        right_ref[spot, :] = right


def sides(*arrays):
    vmem = pl.BlockSpec(memory_space=pltpu.VMEM)
    side = jax.ShapeDtypeStruct((SIDE_ROWS * LAYERS, 128), F32)
    return pl.pallas_call(
        sides_kernel,
        out_shape=(side, side),
        in_specs=[vmem] * 6,
        out_specs=(vmem, vmem),
        name="sides",
    )(*arrays)


WIDE = CY + 128


def relax_kernel(inside_ref, *refs):
    ins, (before_ref, after_ref), (fields_ref, table_ref), (state, source) = refs[:6], refs[6:8], refs[8:10], refs[10:]
    lane = lax.broadcasted_iota(I32, (LAYERS, 128), 1)
    for number, row in enumerate(row_list()):
        comp, is_target, x = row
        group, place = number // 16, number % 16
        spot = pl.ds(group * LAYERS, LAYERS)
        after = after_ref[spot, :]
        before = before_ref[spot, :]
        after = pltpu.roll(after, 128 - 8 * place, 1) if place else after
        shift = (120 - 8 * place) % 128
        before = pltpu.roll(before, shift, 1) if shift else before
        rim = jnp.where(lane < 8, after, jnp.where(lane >= 120, before, 0.0))
        into, at = (source, x + TARGET_RIM) if is_target else (state, x + PRIOR_RIM)
        for half in range(2):
            into[comp, at, :, pl.ds(half * LO, LO)] = row_piece(ins, row, half * LO, LO)
        into[comp, at, :, pl.ds(CY, 128)] = rim

    wide_lane = lax.broadcasted_iota(I32, (LAYERS, WIDE), 1)
    outside = ((wide_lane >= CY + 64) & (inside_ref[2] == 0)) | (
        (wide_lane >= CY) & (wide_lane < CY + 64) & (inside_ref[3] == 0)
    )
    factor = jnp.where(outside, 0.0, 0.2)
    above_factor = jnp.where(inside_ref[0] == 0, 0.0, factor)
    below_factor = jnp.where(inside_ref[1] == 0, 0.0, factor)

    def comp_step(comp, carry):
        for sweep in range(SWEEPS):
            rim = PRIOR_RIM - 1 - sweep
            above = state[comp, PRIOR_RIM - rim - 1]
            here = state[comp, PRIOR_RIM - rim]
            for x in range(-rim, CX + rim):
                below = state[comp, x + 1 + PRIOR_RIM]
                beside = above + below + pltpu.roll(here, 1, 1) + pltpu.roll(here, WIDE - 1, 1)
                scale = above_factor if x < 0 else below_factor if x >= CX else factor
                state[comp, x + PRIOR_RIM] = (source[comp, x + TARGET_RIM] + beside) * scale
                above, here = here, below
        return carry

    lax.fori_loop(0, 4, comp_step, 0)
    for x in range(CX):
        void = 1.0 - state[0, x + PRIOR_RIM, :, 0:CY]
        for comp in range(4):
            value = void if comp == 0 else -state[comp, x + PRIOR_RIM, :, 0:CY] / void
            fields_ref[comp, :, x, :] = value
            for half in range(2):
                table_ref[comp, pl.ds((half * CX + x) * LAYERS, LAYERS), :] = value[:, half * LO : (half + 1) * LO]


def relax(inside, *arrays):
    vmem = pl.BlockSpec(memory_space=pltpu.VMEM)
    return pl.pallas_call(
        relax_kernel,
        out_shape=(
            jax.ShapeDtypeStruct((4, LAYERS, CX, CY), F32),
            jax.ShapeDtypeStruct((4, HI, LO), F32),
        ),
        in_specs=[pl.BlockSpec(memory_space=pltpu.SMEM)] + [vmem] * 8,
        out_specs=(vmem, vmem),
        scratch_shapes=[
            pltpu.VMEM((4, CX + 2 * PRIOR_RIM, LAYERS, WIDE), F32),
            pltpu.VMEM((4, CX + 2 * TARGET_RIM, LAYERS, WIDE), F32),
        ],
        name="relax",
    )(inside, *arrays)


def shifted(array, axis, step):
    count = lax.axis_size(axis)
    pairs = [(i, i + step) for i in range(count) if 0 <= i + step < count]
    return lax.ppermute(array, axis, pairs)


def on_device(part_slab, part_cell, part_volume, part_drag, part_count, prior_solid, prior_drag):
    slab = part_slab.reshape(1, PARTS)
    prior_rows, prior_first, prior_last = prior(prior_solid, prior_drag)
    prior_above = shifted(prior_last, "span", 1)
    prior_below = shifted(prior_first, "span", -1)
    sent, position = pack(part_count, slab, part_cell, part_volume, part_drag)
    received = lax.all_to_all(sent.reshape(OWNERS, 5, 2, 128), "span", 0, 0, tiled=True)
    received = received.reshape(OWNERS * ROWS, 128)
    target, target_first, target_last = deposit(received)
    target_above = shifted(target_last, "span", 1)
    target_below = shifted(target_first, "span", -1)
    arrays = (target, target_above, target_below, prior_rows, prior_above, prior_below)
    side_first, side_last = sides(*arrays)
    before = shifted(side_last, "depth", 1)
    after = shifted(side_first, "depth", -1)
    row, col = lax.axis_index("span"), lax.axis_index("depth")
    inside = jnp.stack(
        [row > 0, row < lax.axis_size("span") - 1, col > 0, col < lax.axis_size("depth") - 1]
    ).astype(I32)
    fields, table = relax(inside, *arrays, before, after)
    returned = gather(table, received)
    back = lax.all_to_all(returned.reshape(OWNERS, BACK_ROWS, 128), "span", 0, 0, tiled=True)
    feedback = pick(part_count, slab, position, back.reshape(OWNERS * BACK_ROWS, 128))
    return fields, feedback


def solution(mesh):
    in_specs = (
        P("depth", "span", None),
        P("depth", "span"),
        P("depth", "span"),
        P(None, "depth", "span"),
        P("depth", "span"),
        P(None, "span", "depth"),
        P(None, None, "span", "depth"),
    )
    out_specs = (P(None, None, "span", "depth"), P(None, "depth", "span"))
    return jax.shard_map(on_device, mesh=mesh, in_specs=in_specs, out_specs=out_specs, check_vma=False)
```

time: 426 us -> 147 us (0.35)
  local copies, waits for them, and re-layouts: 145 us -> 2.09 us
  matrix products: 136 us -> 0 us
  Pallas kernels: 0 us -> 77.4 us
  other arithmetic: 39.6 us -> 0.6 us
  waiting for transfers between devices: 51.2 us -> 15.2 us
  blocking collectives: 0 us -> 20.7 us
  starting transfers between devices: 47.8 us -> 28.7 us
    dot_general x160 -> x0, matrix products: 136 us -> none  [the longest x144 132 us: exact_inner(): lax.dot_general(left, right, (((0,), (0,)), ((), ())), precision=lax.Prec...]
    gather x2 -> x0, local copies, waits for them, and re-layouts: 96.5 us -> none  [the longest x1 65.3 us: on_device(): values = field_table[:, slot_index].reshape(4, span_size, capacity)]
    pallas_call x0 -> x7, Pallas kernels: none -> 77.4 us  [the longest x1 25.6 us: gather(): pl.pallas_call(gather_kernel, out_shape=jax.ShapeDtypeStruct((OWNERS * BA...]
    all_to_all x3 -> x1, waiting for transfers between devices: 30.5 us -> 5.34 us  [on_device(): lax.all_to_all(sent.reshape(OWNERS, 5, 2, 128), 'span', 0, 0, tiled=True)]
    all_to_all x0 -> x1, blocking collectives: none -> 20.7 us  [on_device(): lax.all_to_all(returned.reshape(OWNERS, BACK_ROWS, 128), 'span', 0, 0, ti...]
    mul x10 -> x0, other arithmetic: 17.7 us -> none  [the longest x9 13.6 us: on_device(): padded = relax_once(region, padded) * keeper[None, None]]
    concatenate x3 -> x0, local copies, waits for them, and re-layouts: 16.1 us -> none  [the longest x1 16 us: on_device(): jnp.concatenate([void_fraction[None], -smooth[1:] / void_fraction[None]],...]
    all_to_all x3 -> x1, starting transfers between devices: 27.4 us -> 13.1 us  [on_device(): lax.all_to_all(sent.reshape(OWNERS, 5, 2, 128), 'span', 0, 0, tiled=True)]
  transfers between devices with their start and end apart: 11 -> 7, of which waited for: 10 -> 4; matrix products, arithmetic and copies ran while one was open for 2% -> 0% of each run, Pallas kernels for 0% -> 18%
where the time goes in v1:
time: 147 us; the launch traced here: 146 us
  Pallas kernels  77.4 us (53%)
  starting transfers between devices  28.7 us (20%)
  blocking collectives  20.7 us (14%)
  waiting for transfers between devices  15.2 us (10%)
  local copies, waits for them, and re-layouts  2.09 us (1%)
    pallas_call x1, Pallas kernels, gather(): pl.pallas_call(gather_kernel, out_shape=jax.ShapeDtypeStruct((OWNERS * BA...  25.6 us
    pallas_call x1, Pallas kernels, deposit(): pl.pallas_call(deposit_kernel, out_shape=(jax.ShapeDtypeStruct((4, HI, LO...  23 us
    all_to_all x1, blocking collectives, on_device(): lax.all_to_all(returned.reshape(OWNERS, BACK_ROWS, 128), 'span', 0, 0, ti...  20.7 us
    ppermute x6, starting transfers between devices, shifted(): return lax.ppermute(array, axis, pairs)  15.5 us
    all_to_all x1, starting transfers between devices, on_device(): lax.all_to_all(sent.reshape(OWNERS, 5, 2, 128), 'span', 0, 0, tiled=True)  13.1 us
    pallas_call x1, Pallas kernels, relax(): pl.pallas_call(relax_kernel, out_shape=(jax.ShapeDtypeStruct((4, LAYERS,...  9.93 us
    ppermute x6, waiting for transfers between devices, shifted(): return lax.ppermute(array, axis, pairs)  9.85 us
    pallas_call x1, Pallas kernels, pack(): pl.pallas_call(pack_kernel, out_shape=(jax.ShapeDtypeStruct((OWNERS * ROW...  7.86 us
  transfers between devices with their start and end apart: 7, of which 4 were waited for; matrix products, arithmetic and copies ran while one was open for 0% of the time, Pallas kernels for 18%

profile of v1, /device:TPU:1, one launch (start us, length us, event | category | flops | bytes accessed | tf_op | source)
XLA Modules:
  0.0 146.0 jit_solution(14984775126298467150)
XLA Ops:
  1.3 7.9 %pack.1 = (f32[640,128]{1,0:T(8,128)}, f32[1,8192]{1,0:T(1,128)}) custom-call(s32[1,1]{1,0:T(1,128)S(6)} %copy.9.count_ref, s32[1,8192]{1,0:T(1,128)} %bitcast.14, s32[1,8192]{1,0:T(1,128)} %cell_ref.1, f32[1,8192]{1,0:T(1,128)} %volume_ref.1, f32[3,1,8192]{2,1,0:T(1,128)} %drag_ref.2), custom_call_target="tpu_custom_call" | custom-call | tf_op jit(solution)/shard_map/pack/pallas_call | solution.py:102
  9.1 13.1 %all-to-all-start = ((f32[64,5,2,128]{3,2,1,0:T(2,128)}), f32[64,5,2,128]{3,2,1,0:T(2,128)S(1)}, u32[]{:S(2)}, u32[]{:S(2)}) async-start(f32[64,5,2,128]{3,2,1,0:T(2,128)} %bitcast.13), calls=%async_computation | async-start | bytes 655360 | tf_op jit(solution)/shard_map/all_to_all | solution.py:434
  22.3 2.6 %prior.1 = (f32[512,512]{1,0:T(8,128)}, f32[192,512]{1,0:T(8,128)}, f32[192,512]{1,0:T(8,128)}) custom-call(f32[8,16,512]{2,1,0:T(8,128)} %solid_ref.1, f32[3,8,16,512]{3,2,1,0:T(8,128)} %drag_ref.3), custom_call_target="tpu_custom_call" | custom-call | tf_op jit(solution)/shard_map/prior/pallas_call | solution.py:286
  24.9 3.5 %collective-permute-start.2 = (f32[192,512]{1,0:T(8,128)}, f32[192,512]{1,0:T(8,128)S(1)}, u32[]{:S(2)}, u32[]{:S(2)}) collective-permute-start(f32[192,512]{1,0:T(8,128)} %get-tuple-element.19), channel_id=1, source_target_pairs={{0,4},{4,8},{8,12},{12,16},{16,20},{20,24},{24,28},{28,32},{32,36}... | collective-permute-start | bytes 1179656 | tf_op jit(solution)/shard_map/ppermute | solution.py:425
  28.4 1.9 %collective-permute-start.3 = (f32[192,512]{1,0:T(8,128)}, f32[192,512]{1,0:T(8,128)S(1)}, u32[]{:S(2)}, u32[]{:S(2)}) collective-permute-start(f32[192,512]{1,0:T(8,128)} %get-tuple-element.20), channel_id=1, source_target_pairs={{4,0},{8,4},{12,8},{16,12},{20,16},{24,20},{28,24},{32,28},{36,32}... | collective-permute-start | bytes 1179656 | tf_op jit(solution)/shard_map/ppermute | solution.py:425
  30.3 5.3 %all-to-all-done = f32[64,5,2,128]{3,2,1,0:T(2,128)S(1)} async-done(((f32[64,5,2,128]{3,2,1,0:T(2,128)}), f32[64,5,2,128]{3,2,1,0:T(2,128)S(1)}, u32[]{:S(2)}, u32[]{:S(2)}) %all-to-all-start) | async-done | bytes 327712 | tf_op jit(solution)/shard_map/all_to_all | solution.py:434
  35.7 0.0 copy-start
  35.7 0.7 copy-done
  36.4 23.0 %deposit.1 = (f32[4,256,256]{2,1,0:T(8,128)}, f32[160,512]{1,0:T(8,128)}, f32[160,512]{1,0:T(8,128)}) custom-call(f32[640,128]{1,0:T(8,128)} %bitcast.9), custom_call_target="tpu_custom_call" | custom-call | tf_op jit(solution)/shard_map/deposit/pallas_call | solution.py:177
  59.4 3.8 %collective-permute-start = (f32[160,512]{1,0:T(8,128)}, f32[160,512]{1,0:T(8,128)S(1)}, u32[]{:S(2)}, u32[]{:S(2)}) collective-permute-start(f32[160,512]{1,0:T(8,128)} %get-tuple-element.16), channel_id=1, source_target_pairs={{0,4},{4,8},{8,12},{12,16},{16,20},{20,24},{24,28},{28,32},{32,36}... | collective-permute-start | bytes 983048 | tf_op jit(solution)/shard_map/ppermute | solution.py:425
  63.2 1.9 %collective-permute-start.1 = (f32[160,512]{1,0:T(8,128)}, f32[160,512]{1,0:T(8,128)S(1)}, u32[]{:S(2)}, u32[]{:S(2)}) collective-permute-start(f32[160,512]{1,0:T(8,128)} %get-tuple-element.17), channel_id=1, source_target_pairs={{4,0},{8,4},{12,8},{16,12},{20,16},{24,20},{28,24},{32,28},{36,32}... | collective-permute-start | bytes 983048 | tf_op jit(solution)/shard_map/ppermute | solution.py:425
  65.1 0.0 collective-permute-done.2.refs_4_
  65.1 0.0 copy-start.1
  65.1 0.0 collective-permute-done.3.refs_5_
  65.2 0.0 copy-start.2
  65.2 2.3 %collective-permute-done.refs_1_ = f32[160,512]{1,0:T(8,128)S(1)} collective-permute-done((f32[160,512]{1,0:T(8,128)}, f32[160,512]{1,0:T(8,128)S(1)}, u32[]{:S(2)}, u32[]{:S(2)}) %collective-permute-start) | collective-permute-done | bytes 327712 | tf_op jit(solution)/shard_map/ppermute | solution.py:425
  67.5 0.0 copy-start.3
  67.5 4.3 %collective-permute-done.1.refs_2_ = f32[160,512]{1,0:T(8,128)S(1)} collective-permute-done((f32[160,512]{1,0:T(8,128)}, f32[160,512]{1,0:T(8,128)S(1)}, u32[]{:S(2)}, u32[]{:S(2)}) %collective-permute-start.1) | collective-permute-done | bytes 327712 | tf_op jit(solution)/shard_map/ppermute | solution.py:425
  71.8 0.0 copy-start.4
  71.8 0.0 copy-done.1
  71.8 0.0 copy-done.2
  71.8 0.0 copy-done.3
  71.8 0.7 copy-done.4
  72.5 3.1 %sides.1 = (f32[112,128]{1,0:T(8,128)}, f32[112,128]{1,0:T(8,128)}) custom-call(f32[4,256,256]{2,1,0:T(8,128)} %get-tuple-element.15.refs_0_, f32[160,512]{1,0:T(8,128)} %copy-done.3, f32[160,512]{1,0:T(8,128)} %copy-done.4, f32[512,512]{1,0:T(8,128)} %get-tuple-element.18.refs_3_, f32[192,512]{1,0:T(8,128)} %copy-done.1, f32[192,512]{1,0:T(8,128)} %copy-done.2), custom_call_target="tpu_custom_call" | custom-call | tf_op jit(solution)/shard_map/sides/pallas_call | solution.py:343
  75.6 3.1 %collective-permute-start.4 = (f32[112,128]{1,0:T(8,128)}, f32[112,128]{1,0:T(8,128)S(1)}, u32[]{:S(2)}, u32[]{:S(2)}) collective-permute-start(f32[112,128]{1,0:T(8,128)} %get-tuple-element.21), channel_id=1, source_target_pairs={{0,1},{1,2},{2,3},{4,5},{5,6},{6,7},{8,9},{9,10},{10,11},{12,13},{... | collective-permute-start | bytes 172040 | tf_op jit(solution)/shard_map/ppermute | solution.py:425
  78.7 1.3 collective-permute-start.5
  80.0 0.6 add_convert_fusion.inside_ref
  80.6 0.0 collective-permute-done.4.refs_6_
  80.6 0.0 copy-start.5
  80.6 3.2 %collective-permute-done.5.refs_7_ = f32[112,128]{1,0:T(8,128)S(1)} collective-permute-done((f32[112,128]{1,0:T(8,128)}, f32[112,128]{1,0:T(8,128)S(1)}, u32[]{:S(2)}, u32[]{:S(2)}) %collective-permute-start.5) | collective-permute-done | bytes 57376 | tf_op jit(solution)/shard_map/ppermute | solution.py:425
  83.8 0.0 copy-done.5
  83.8 0.0 copy-start.6
  83.8 0.6 copy-done.6
  84.5 9.9 %relax.1 = (f32[4,8,16,512]{3,2,1,0:T(8,128)}, f32[4,256,256]{2,1,0:T(8,128)}) custom-call(s32[4]{0:T(128)} %add_convert_fusion.inside_ref, f32[4,256,256]{2,1,0:T(8,128)} %get-tuple-element.15.refs_0_, f32[160,512]{1,0:T(8,128)} %copy-done.3, f32[160,512]{1,0:T(8,128)} %copy-done.4, f32[512,512]{1,0:T(8,128)} %get-tuple-element.18.refs_3_, ...), custom_call_target="tpu_custom_call" | custom-call | tf_op jit(solution)/shard_map/relax/pallas_call | solution.py:406
  94.4 25.6 %gather.1 = f32[512,128]{1,0:T(8,128)} custom-call(f32[4,256,256]{2,1,0:T(8,128)} %get-tuple-element.25.table_ref, f32[640,128]{1,0:T(8,128)} %bitcast.10), custom_call_target="tpu_custom_call" | custom-call | tf_op jit(solution)/shard_map/gather/pallas_call | solution.py:220
  120.0 20.7 %all_to_all.10 = f32[64,8,128]{2,1,0:T(8,128)} all-to-all(f32[64,8,128]{2,1,0:T(8,128)} %bitcast.11), channel_id=1, replica_groups=mesh['span'=64,'depth'=4] {'span'}, dimensions={0} | all-to-all | bytes 524288 | tf_op jit(solution)/shard_map/all_to_all | solution.py:449
  140.7 5.4 %pick.1 = f32[4,1,8192]{2,1,0:T(1,128)} custom-call(s32[1,1]{1,0:T(1,128)S(6)} %copy.9.count_ref, s32[1,8192]{1,0:T(1,128)} %bitcast.15, f32[1,8192]{1,0:T(1,128)} %get-tuple-element.24.position_ref, f32[512,128]{1,0:T(8,128)} %bitcast.12), custom_call_target="tpu_custom_call" | custom-call | tf_op jit(solution)/shard_map/pick/pallas_call | solution.py:261
Async XLA Ops:
  9.1 26.5 %all-to-all-start = ((f32[64,5,2,128]{3,2,1,0:T(2,128)}), f32[64,5,2,128]{3,2,1,0:T(2,128)S(1)}, u32[]{:S(2)}, u32[]{:S(2)}) async-start(f32[64,5,2,128]{3,2,1,0:T(2,128)} %bitcast.13), calls=%async_computation | async-start | bytes 655360 | tf_op jit(solution)/shard_map/all_to_all | solution.py:434
  24.9 40.3 %collective-permute-start.2 = (f32[192,512]{1,0:T(8,128)}, f32[192,512]{1,0:T(8,128)S(1)}, u32[]{:S(2)}, u32[]{:S(2)}) collective-permute-start(f32[192,512]{1,0:T(8,128)} %get-tuple-element.19), channel_id=1, source_target_pairs={{0,4},{4,8},{8,12},{12,16},{16,20},{20,24},{24,28},{28,32},{32,36}... | collective-permute-start | bytes 1179656 | tf_op jit(solution)/shard_map/ppermute | solution.py:425
  28.4 36.8 %collective-permute-start.3 = (f32[192,512]{1,0:T(8,128)}, f32[192,512]{1,0:T(8,128)S(1)}, u32[]{:S(2)}, u32[]{:S(2)}) collective-permute-start(f32[192,512]{1,0:T(8,128)} %get-tuple-element.20), channel_id=1, source_target_pairs={{4,0},{8,4},{12,8},{16,12},{20,16},{24,20},{28,24},{32,28},{36,32}... | collective-permute-start | bytes 1179656 | tf_op jit(solution)/shard_map/ppermute | solution.py:425
  35.7 0.7 copy-start
  59.4 8.1 %collective-permute-start = (f32[160,512]{1,0:T(8,128)}, f32[160,512]{1,0:T(8,128)S(1)}, u32[]{:S(2)}, u32[]{:S(2)}) collective-permute-start(f32[160,512]{1,0:T(8,128)} %get-tuple-element.16), channel_id=1, source_target_pairs={{0,4},{4,8},{8,12},{12,16},{16,20},{20,24},{24,28},{28,32},{32,36}... | collective-permute-start | bytes 983048 | tf_op jit(solution)/shard_map/ppermute | solution.py:425
  63.2 8.6 %collective-permute-start.1 = (f32[160,512]{1,0:T(8,128)}, f32[160,512]{1,0:T(8,128)S(1)}, u32[]{:S(2)}, u32[]{:S(2)}) collective-permute-start(f32[160,512]{1,0:T(8,128)} %get-tuple-element.17), channel_id=1, source_target_pairs={{4,0},{8,4},{12,8},{16,12},{20,16},{24,20},{28,24},{32,28},{36,32}... | collective-permute-start | bytes 983048 | tf_op jit(solution)/shard_map/ppermute | solution.py:425
  65.1 6.7 %copy-start.1 = (f32[192,512]{1,0:T(8,128)}, f32[192,512]{1,0:T(8,128)S(1)}, u32[]{:S(2)}) copy-start(f32[192,512]{1,0:T(8,128)S(1)} %collective-permute-done.2.refs_4_) | copy-start | bytes 1179652
  65.2 6.6 %copy-start.2 = (f32[192,512]{1,0:T(8,128)}, f32[192,512]{1,0:T(8,128)S(1)}, u32[]{:S(2)}) copy-start(f32[192,512]{1,0:T(8,128)S(1)} %collective-permute-done.3.refs_5_) | copy-start | bytes 1179652
  67.5 4.3 %copy-start.3 = (f32[160,512]{1,0:T(8,128)}, f32[160,512]{1,0:T(8,128)S(1)}, u32[]{:S(2)}) copy-start(f32[160,512]{1,0:T(8,128)S(1)} %collective-permute-done.refs_1_) | copy-start | bytes 983044
  71.8 0.7 copy-start.4
  75.6 5.0 %collective-permute-start.4 = (f32[112,128]{1,0:T(8,128)}, f32[112,128]{1,0:T(8,128)S(1)}, u32[]{:S(2)}, u32[]{:S(2)}) collective-permute-start(f32[112,128]{1,0:T(8,128)} %get-tuple-element.21), channel_id=1, source_target_pairs={{0,1},{1,2},{2,3},{4,5},{5,6},{6,7},{8,9},{9,10},{10,11},{12,13},{... | collective-permute-start | bytes 172040 | tf_op jit(solution)/shard_map/ppermute | solution.py:425
  78.7 5.1 %collective-permute-start.5 = (f32[112,128]{1,0:T(8,128)}, f32[112,128]{1,0:T(8,128)S(1)}, u32[]{:S(2)}, u32[]{:S(2)}) collective-permute-start(f32[112,128]{1,0:T(8,128)} %get-tuple-element.22), channel_id=1, source_target_pairs={{1,0},{2,1},{3,2},{5,4},{6,5},{7,6},{9,8},{10,9},{11,10},{13,12},{... | collective-permute-start | bytes 172040 | tf_op jit(solution)/shard_map/ppermute | solution.py:425
  80.6 3.2 %copy-start.5 = (f32[112,128]{1,0:T(8,128)}, f32[112,128]{1,0:T(8,128)S(1)}, u32[]{:S(2)}) copy-start(f32[112,128]{1,0:T(8,128)S(1)} %collective-permute-done.4.refs_6_) | copy-start | bytes 172036
  83.8 0.6 copy-start.6

commit v2 on v1

--- a/solution.py
+++ b/solution.py
@@ -14,7 +14,8 @@
 ROWS = 2 * 5
 BACK_ROWS = 8
 SWEEPS = 6
-PRIOR_RIM, TARGET_RIM = SWEEPS, SWEEPS - 1
+RIM = SWEEPS
+SIDE_ROWS = 4 * CX // 16 * LAYERS
 PHI_LIMIT = 0.6
 
 
@@ -47,6 +48,32 @@
 
 def dot_nn(left, right):
     return lax.dot_general(left, right, (((1,), (0,)), ((), ())), preferred_element_type=F32)
+
+
+def fold_sides(pieces, left_ref, right_ref):
+    lane = lax.broadcasted_iota(I32, (LAYERS, 128), 1)
+    for group in range(4 * CX // 16):
+        left = jnp.zeros((LAYERS, 128), F32)
+        right = jnp.zeros((LAYERS, 128), F32)
+        for place in range(16):
+            first, last = pieces(group * 16 + place)
+            here = (lane >= 8 * place) & (lane < 8 * place + 8)
+            left = jnp.where(here, pltpu.roll(first, 8 * place, 1) if place else first, left)
+            shift = (8 * place + 8) % 128
+            right = jnp.where(here, pltpu.roll(last, shift, 1) if shift else last, right)
+        left_ref[group * LAYERS : (group + 1) * LAYERS, :] = left
+        right_ref[group * LAYERS : (group + 1) * LAYERS, :] = right
+
+
+def unfold_side(row, before_ref, after_ref):
+    lane = lax.broadcasted_iota(I32, (LAYERS, 128), 1)
+    group, place = row // 16, row % 16
+    after = after_ref[group * LAYERS : (group + 1) * LAYERS, :]
+    before = before_ref[group * LAYERS : (group + 1) * LAYERS, :]
+    after = pltpu.roll(after, 128 - 8 * place, 1) if place else after
+    shift = (120 - 8 * place) % 128
+    before = pltpu.roll(before, shift, 1) if shift else before
+    return jnp.where(lane < 8, after, jnp.where(lane >= 120, before, 0.0))
 
 
 PACK_BLOCK = 1024
@@ -161,22 +188,22 @@
 
     lax.fori_loop(0, OWNERS // SOURCES_AT_ONCE, step, 0)
     out_ref[0] = jnp.minimum(out_ref[0], PHI_LIMIT)
-    for comp in range(4):
-        for step_x in range(TARGET_RIM):
-            spot = pl.ds((comp * TARGET_RIM + step_x) * LAYERS, LAYERS)
-            for half in range(2):
-                lanes = pl.ds(half * LO, LO)
-                first_ref[spot, lanes] = out_ref[comp, pl.ds((half * CX + step_x) * LAYERS, LAYERS), :]
-                x = CX - TARGET_RIM + step_x
-                last_ref[spot, lanes] = out_ref[comp, pl.ds((half * CX + x) * LAYERS, LAYERS), :]
+
+    def pieces(row):
+        comp, x = row // CX, row % CX
+        first = out_ref[comp, x * LAYERS : (x + 1) * LAYERS, 0:128]
+        last = out_ref[comp, (CX + x) * LAYERS : (CX + x + 1) * LAYERS, LO - 128 : LO]
+        return first, last
+
+    fold_sides(pieces, first_ref, last_ref)
 
 
 def deposit(received):
     vmem = pl.BlockSpec(memory_space=pltpu.VMEM)
-    edge = jax.ShapeDtypeStruct((4 * TARGET_RIM * LAYERS, CY), F32)
+    side = jax.ShapeDtypeStruct((SIDE_ROWS, 128), F32)
     return pl.pallas_call(
         deposit_kernel,
-        out_shape=(jax.ShapeDtypeStruct((4, HI, LO), F32), edge, edge),
+        out_shape=(jax.ShapeDtypeStruct((4, HI, LO), F32), side, side),
         in_specs=[vmem],
         out_specs=(vmem, vmem, vmem),
         name="deposit",
@@ -186,9 +213,26 @@
 GATHER_SOURCES = 2
 
 
-def gather_kernel(table_ref, recv_ref, out_ref, tops, bottoms):
-    for comp in range(4):
-        tops[comp], bottoms[comp] = halves(table_ref[comp])
+def gather_kernel(own_ref, above_ref, below_ref, recv_ref, fields_ref, out_ref, tops, bottoms):
+    def smooth(comp, x):
+        row = own_ref[pl.ds((comp * CX + x) * LAYERS, LAYERS), :]
+        if x < RIM:
+            row = row + above_ref[pl.ds((comp * RIM + x) * LAYERS, LAYERS), :]
+        if x >= CX - RIM:
+            row = row + below_ref[pl.ds((comp * RIM + x - CX + RIM) * LAYERS, LAYERS), :]
+        return row
+
+    for pair in range(0, CX, 2):
+        void = [1.0 - smooth(0, x) for x in (pair, pair + 1)]
+        for comp in range(4):
+            rows = void if comp == 0 else [-smooth(comp, x) / v for x, v in zip((pair, pair + 1), void)]
+            for x, row in zip((pair, pair + 1), rows):
+                fields_ref[comp, :, x, :] = row
+            high, low = halves(jnp.concatenate(rows, axis=0))
+            for half in range(2):
+                spot = pl.ds((half * CX + pair) * LAYERS, 2 * LAYERS)
+                tops[comp, spot, :] = high[:, half * LO : (half + 1) * LO]
+                bottoms[comp, spot, :] = low[:, half * LO : (half + 1) * LO]
 
     def step(block, carry):
         highs, lows = [], []
@@ -215,16 +259,19 @@
     lax.fori_loop(0, OWNERS // GATHER_SOURCES, step, 0)
 
 
-def gather(table, received):
+def gather(own, above, below, received):
     vmem = pl.BlockSpec(memory_space=pltpu.VMEM)
     return pl.pallas_call(
         gather_kernel,
-        out_shape=jax.ShapeDtypeStruct((OWNERS * BACK_ROWS, 128), F32),
-        in_specs=[vmem, vmem],
-        out_specs=vmem,
+        out_shape=(
+            jax.ShapeDtypeStruct((4, LAYERS, CX, CY), F32),
+            jax.ShapeDtypeStruct((OWNERS * BACK_ROWS, 128), F32),
+        ),
+        in_specs=[vmem] * 4,
+        out_specs=(vmem, vmem),
         scratch_shapes=[pltpu.VMEM((4, HI, LO), BF16)] * 2,
         name="gather",
-    )(table, received)
+    )(own, above, below, received)
 
 
 PICK_BLOCK = 1024
@@ -268,111 +315,59 @@
     )(count, slab, position, back)
 
 
-def prior_kernel(solid_ref, drag_ref, rows_ref, first_ref, last_ref):
+def prior_row(solid_ref, drag_ref, row):
+    comp, x = row // CX, row % CX
+    return solid_ref[:, x, :] if comp == 0 else drag_ref[comp - 1, :, x, :]
+
+
+def prior_kernel(solid_left, drag_left, solid_right, drag_right, first_ref, last_ref):
+    def pieces(row):
+        return prior_row(solid_left, drag_left, row), prior_row(solid_right, drag_right, row)
+
+    fold_sides(pieces, first_ref, last_ref)
+
+
+def prior_sides(solid, drag):
+    vmem = pl.BlockSpec(memory_space=pltpu.VMEM)
+    side = jax.ShapeDtypeStruct((SIDE_ROWS, 128), F32)
+    edges = []
+    for block in (0, CY // 128 - 1):
+        edges.append(pl.BlockSpec((LAYERS, CX, 128), lambda i, block=block: (0, 0, block)))
+        edges.append(pl.BlockSpec((3, LAYERS, CX, 128), lambda i, block=block: (0, 0, 0, block)))
+    return pl.pallas_call(
+        prior_kernel,
+        grid=(1,),
+        out_shape=(side, side),
+        in_specs=edges,
+        out_specs=(pl.BlockSpec((SIDE_ROWS, 128), lambda i: (0, 0)),) * 2,
+        name="prior_sides",
+    )(solid, drag, solid, drag)
+
+
+WIDE = CY + 128
+
+
+def relax_kernel(
+    inside_ref, target_ref, solid_ref, drag_ref, before, after, prior_before, prior_after,
+    own_ref, up_ref, down_ref, state, source,
+):
+    blank = jnp.zeros((LAYERS, WIDE), F32)
     for comp in range(4):
+        for x in range(RIM):
+            state[comp, x] = blank
+            state[comp, RIM + CX + x] = blank
         for x in range(CX):
-            row = solid_ref[:, x, :] if comp == 0 else drag_ref[comp - 1, :, x, :]
-            rows_ref[pl.ds((comp * CX + x) * LAYERS, LAYERS), :] = row
-            if x < PRIOR_RIM:
-                first_ref[pl.ds((comp * PRIOR_RIM + x) * LAYERS, LAYERS), :] = row
-            if x >= CX - PRIOR_RIM:
-                spot = (comp * PRIOR_RIM + x - CX + PRIOR_RIM) * LAYERS
-                last_ref[pl.ds(spot, LAYERS), :] = row
-
-
-def prior(solid, drag):
-    vmem = pl.BlockSpec(memory_space=pltpu.VMEM)
-    edge = jax.ShapeDtypeStruct((4 * PRIOR_RIM * LAYERS, CY), F32)
-    return pl.pallas_call(
-        prior_kernel,
-        out_shape=(jax.ShapeDtypeStruct((4 * CX * LAYERS, CY), F32), edge, edge),
-        in_specs=[vmem, vmem],
-        out_specs=(vmem, vmem, vmem),
-        name="prior",
-    )(solid, drag)
-
-
-def row_list():
-    rows = []
-    for comp in range(4):
-        rows += [(comp, False, x) for x in range(-PRIOR_RIM, CX + PRIOR_RIM)]
-        rows += [(comp, True, x) for x in range(-TARGET_RIM, CX + TARGET_RIM)]
-    return rows
-
-
-SIDE_ROWS = -(-len(row_list()) // 16)
-
-
-def row_piece(refs, row, start, size):
-    target, target_above, target_below, prior_rows, prior_above, prior_below = refs
-    comp, is_target, x = row
-    above, below, rim = (target_above, target_below, TARGET_RIM) if is_target else (prior_above, prior_below, PRIOR_RIM)
-    lanes = pl.ds(start, size)
-    if x < 0:
-        return above[pl.ds((comp * rim + x + rim) * LAYERS, LAYERS), lanes]
-    if x >= CX:
-        return below[pl.ds((comp * rim + x - CX) * LAYERS, LAYERS), lanes]
-    if is_target:
-        half = start // LO
-        return target[comp, pl.ds((half * CX + x) * LAYERS, LAYERS), pl.ds(start - half * LO, size)]
-    return prior_rows[pl.ds((comp * CX + x) * LAYERS, LAYERS), lanes]
-
-
-def sides_kernel(*refs):
-    ins, (left_ref, right_ref) = refs[:6], refs[6:]
-    lane = lax.broadcasted_iota(I32, (LAYERS, 128), 1)
-    rows = row_list()
-    for group in range(SIDE_ROWS):
-        left = jnp.zeros((LAYERS, 128), F32)
-        right = jnp.zeros((LAYERS, 128), F32)
-        for place, row in enumerate(rows[16 * group : 16 * group + 16]):
-            here = (lane >= 8 * place) & (lane < 8 * place + 8)
-            first = row_piece(ins, row, 0, 128)
-            last = row_piece(ins, row, CY - 128, 128)
-            left = jnp.where(here, pltpu.roll(first, 8 * place, 1) if place else first, left)
-            shift = (8 * place + 8) % 128
-            right = jnp.where(here, pltpu.roll(last, shift, 1) if shift else last, right)
-        spot = pl.ds(group * LAYERS, LAYERS)
-        left_ref[spot, :] = left
-        right_ref[spot, :] = right
-
-
-def sides(*arrays):
-    vmem = pl.BlockSpec(memory_space=pltpu.VMEM)
-    side = jax.ShapeDtypeStruct((SIDE_ROWS * LAYERS, 128), F32)
-    return pl.pallas_call(
-        sides_kernel,
-        out_shape=(side, side),
-        in_specs=[vmem] * 6,
-        out_specs=(vmem, vmem),
-        name="sides",
-    )(*arrays)
-
-
-WIDE = CY + 128
-
-
-def relax_kernel(inside_ref, *refs):
-    ins, (before_ref, after_ref), (fields_ref, table_ref), (state, source) = refs[:6], refs[6:8], refs[8:10], refs[10:]
-    lane = lax.broadcasted_iota(I32, (LAYERS, 128), 1)
-    for number, row in enumerate(row_list()):
-        comp, is_target, x = row
-        group, place = number // 16, number % 16
-        spot = pl.ds(group * LAYERS, LAYERS)
-        after = after_ref[spot, :]
-        before = before_ref[spot, :]
-        after = pltpu.roll(after, 128 - 8 * place, 1) if place else after
-        shift = (120 - 8 * place) % 128
-        before = pltpu.roll(before, shift, 1) if shift else before
-        rim = jnp.where(lane < 8, after, jnp.where(lane >= 120, before, 0.0))
-        into, at = (source, x + TARGET_RIM) if is_target else (state, x + PRIOR_RIM)
-        for half in range(2):
-            into[comp, at, :, pl.ds(half * LO, LO)] = row_piece(ins, row, half * LO, LO)
-        into[comp, at, :, pl.ds(CY, 128)] = rim
-
-    wide_lane = lax.broadcasted_iota(I32, (LAYERS, WIDE), 1)
-    outside = ((wide_lane >= CY + 64) & (inside_ref[2] == 0)) | (
-        (wide_lane >= CY) & (wide_lane < CY + 64) & (inside_ref[3] == 0)
+            row = comp * CX + x
+            for half in range(2):
+                spot = pl.ds((half * CX + x) * LAYERS, LAYERS)
+                source[comp, x, :, half * LO : (half + 1) * LO] = target_ref[comp, spot, :]
+            source[comp, x, :, CY:WIDE] = unfold_side(row, before, after)
+            state[comp, RIM + x, :, 0:CY] = prior_row(solid_ref, drag_ref, row)
+            state[comp, RIM + x, :, CY:WIDE] = unfold_side(row, prior_before, prior_after)
+
+    lane = lax.broadcasted_iota(I32, (LAYERS, WIDE), 1)
+    outside = ((lane >= CY + 64) & (inside_ref[2] == 0)) | (
+        (lane >= CY) & (lane < CY + 64) & (inside_ref[3] == 0)
     )
     factor = jnp.where(outside, 0.0, 0.2)
     above_factor = jnp.where(inside_ref[0] == 0, 0.0, factor)
@@ -380,40 +375,41 @@
 
     def comp_step(comp, carry):
         for sweep in range(SWEEPS):
-            rim = PRIOR_RIM - 1 - sweep
-            above = state[comp, PRIOR_RIM - rim - 1]
-            here = state[comp, PRIOR_RIM - rim]
+            rim = sweep + 1
+            above, here = blank, blank
             for x in range(-rim, CX + rim):
-                below = state[comp, x + 1 + PRIOR_RIM]
-                beside = above + below + pltpu.roll(here, 1, 1) + pltpu.roll(here, WIDE - 1, 1)
+                below = state[comp, x + 1 + RIM] if x + 1 < CX + sweep else blank
+                total = above + below
+                if -sweep <= x < CX + sweep:
+                    total = total + pltpu.roll(here, 1, 1) + pltpu.roll(here, WIDE - 1, 1)
+                if 0 <= x < CX:
+                    total = total + source[comp, x]
                 scale = above_factor if x < 0 else below_factor if x >= CX else factor
-                state[comp, x + PRIOR_RIM] = (source[comp, x + TARGET_RIM] + beside) * scale
+                state[comp, x + RIM] = total * scale
                 above, here = here, below
         return carry
 
     lax.fori_loop(0, 4, comp_step, 0)
-    for x in range(CX):
-        void = 1.0 - state[0, x + PRIOR_RIM, :, 0:CY]
-        for comp in range(4):
-            value = void if comp == 0 else -state[comp, x + PRIOR_RIM, :, 0:CY] / void
-            fields_ref[comp, :, x, :] = value
-            for half in range(2):
-                table_ref[comp, pl.ds((half * CX + x) * LAYERS, LAYERS), :] = value[:, half * LO : (half + 1) * LO]
+    for comp in range(4):
+        for x in range(CX):
+            own_ref[pl.ds((comp * CX + x) * LAYERS, LAYERS), :] = state[comp, RIM + x, :, 0:CY]
+        for x in range(RIM):
+            spot = pl.ds((comp * RIM + x) * LAYERS, LAYERS)
+            up_ref[spot, :] = state[comp, x, :, 0:CY]
+            down_ref[spot, :] = state[comp, RIM + CX + x, :, 0:CY]
 
 
 def relax(inside, *arrays):
     vmem = pl.BlockSpec(memory_space=pltpu.VMEM)
+    rim = jax.ShapeDtypeStruct((4 * RIM * LAYERS, CY), F32)
     return pl.pallas_call(
         relax_kernel,
-        out_shape=(
-            jax.ShapeDtypeStruct((4, LAYERS, CX, CY), F32),
-            jax.ShapeDtypeStruct((4, HI, LO), F32),
-        ),
-        in_specs=[pl.BlockSpec(memory_space=pltpu.SMEM)] + [vmem] * 8,
-        out_specs=(vmem, vmem),
+        out_shape=(jax.ShapeDtypeStruct((4 * CX * LAYERS, CY), F32), rim, rim),
+        in_specs=[pl.BlockSpec(memory_space=pltpu.SMEM)] + [vmem] * 7,
+        out_specs=(vmem, vmem, vmem),
         scratch_shapes=[
-            pltpu.VMEM((4, CX + 2 * PRIOR_RIM, LAYERS, WIDE), F32),
-            pltpu.VMEM((4, CX + 2 * TARGET_RIM, LAYERS, WIDE), F32),
+            pltpu.VMEM((4, CX + 2 * RIM, LAYERS, WIDE), F32),
+            pltpu.VMEM((4, CX, LAYERS, WIDE), F32),
         ],
         name="relax",
     )(inside, *arrays)
@@ -427,25 +423,25 @@
 
 def on_device(part_slab, part_cell, part_volume, part_drag, part_count, prior_solid, prior_drag):
     slab = part_slab.reshape(1, PARTS)
-    prior_rows, prior_first, prior_last = prior(prior_solid, prior_drag)
-    prior_above = shifted(prior_last, "span", 1)
-    prior_below = shifted(prior_first, "span", -1)
-    sent, position = pack(part_count, slab, part_cell, part_volume, part_drag)
-    received = lax.all_to_all(sent.reshape(OWNERS, 5, 2, 128), "span", 0, 0, tiled=True)
-    received = received.reshape(OWNERS * ROWS, 128)
-    target, target_first, target_last = deposit(received)
-    target_above = shifted(target_last, "span", 1)
-    target_below = shifted(target_first, "span", -1)
-    arrays = (target, target_above, target_below, prior_rows, prior_above, prior_below)
-    side_first, side_last = sides(*arrays)
-    before = shifted(side_last, "depth", 1)
-    after = shifted(side_first, "depth", -1)
     row, col = lax.axis_index("span"), lax.axis_index("depth")
     inside = jnp.stack(
         [row > 0, row < lax.axis_size("span") - 1, col > 0, col < lax.axis_size("depth") - 1]
     ).astype(I32)
-    fields, table = relax(inside, *arrays, before, after)
-    returned = gather(table, received)
+    sent, position = pack(part_count, slab, part_cell, part_volume, part_drag)
+    received = lax.all_to_all(sent.reshape(OWNERS, 5, 2, 128), "span", 0, 0, tiled=True)
+    received = received.reshape(OWNERS * ROWS, 128)
+    prior_first, prior_last = prior_sides(prior_solid, prior_drag)
+    prior_before = shifted(prior_last, "depth", 1)
+    prior_after = shifted(prior_first, "depth", -1)
+    target, first, last = deposit(received)
+    before = shifted(last, "depth", 1)
+    after = shifted(first, "depth", -1)
+    own, up, down = relax(
+        inside, target, prior_solid, prior_drag, before, after, prior_before, prior_after
+    )
+    from_above = shifted(down, "span", 1)
+    from_below = shifted(up, "span", -1)
+    fields, returned = gather(own, from_above, from_below, received)
     back = lax.all_to_all(returned.reshape(OWNERS, BACK_ROWS, 128), "span", 0, 0, tiled=True)
     feedback = pick(part_count, slab, position, back.reshape(OWNERS * BACK_ROWS, 128))
     return fields, feedback

time: 147 us -> 145 us (0.986)
  Pallas kernels: 77.4 us -> 73.4 us
  waiting for transfers between devices: 15.2 us -> 16.9 us
    pallas_call x4 -> x3, Pallas kernels: 41.1 us -> 37.4 us  [the longest x1 26.1 us: gather(): pl.pallas_call(gather_kernel, out_shape=(jax.ShapeDtypeStruct((4, LAYERS,...]
  transfers between devices with their start and end apart: 7 -> 7, of which waited for: 4 -> 4; matrix products, arithmetic and copies ran while one was open for 0% -> 0% of each run, Pallas kernels for 18% -> 17%
where the time goes in v2:
time: 145 us; the launch traced here: 144 us
  Pallas kernels  73.4 us (51%)
  starting transfers between devices  28.6 us (20%)
  blocking collectives  21 us (14%)
  waiting for transfers between devices  16.9 us (12%)
  local copies, waits for them, and re-layouts  2.09 us (1%)
    pallas_call x1, Pallas kernels, gather(): pl.pallas_call(gather_kernel, out_shape=(jax.ShapeDtypeStruct((4, LAYERS,...  26.1 us
    pallas_call x1, Pallas kernels, deposit(): pl.pallas_call(deposit_kernel, out_shape=(jax.ShapeDtypeStruct((4, HI, LO...  22.9 us
    all_to_all x1, blocking collectives, on_device(): lax.all_to_all(returned.reshape(OWNERS, BACK_ROWS, 128), 'span', 0, 0, ti...  21 us
    ppermute x6, starting transfers between devices, shifted(): return lax.ppermute(array, axis, pairs)  15.4 us
    all_to_all x1, starting transfers between devices, on_device(): lax.all_to_all(sent.reshape(OWNERS, 5, 2, 128), 'span', 0, 0, tiled=True)  13.1 us
    ppermute x6, waiting for transfers between devices, shifted(): return lax.ppermute(array, axis, pairs)  10.1 us
    pallas_call x1, Pallas kernels, relax(): pl.pallas_call(relax_kernel, out_shape=(jax.ShapeDtypeStruct((4 * CX * LA...  9.2 us
    pallas_call x1, Pallas kernels, pack(): pl.pallas_call(pack_kernel, out_shape=(jax.ShapeDtypeStruct((OWNERS * ROW...  7.85 us
  transfers between devices with their start and end apart: 7, of which 4 were waited for; matrix products, arithmetic and copies ran while one was open for 0% of the time, Pallas kernels for 17%

profile of v2, /device:TPU:1, one launch (start us, length us, event | category | flops | bytes accessed | tf_op | source)
XLA Modules:
  0.0 144.0 jit_solution(1142723102842754383)
XLA Ops:
  1.3 7.9 %pack.1 = (f32[640,128]{1,0:T(8,128)}, f32[1,8192]{1,0:T(1,128)}) custom-call(s32[1,1]{1,0:T(1,128)S(6)} %copy.9.count_ref, s32[1,8192]{1,0:T(1,128)} %bitcast.14, s32[1,8192]{1,0:T(1,128)} %cell_ref.1, f32[1,8192]{1,0:T(1,128)} %volume_ref.1, f32[3,1,8192]{2,1,0:T(1,128)} %drag_ref.2), custom_call_target="tpu_custom_call" | custom-call | tf_op jit(solution)/shard_map/pack/pallas_call | solution.py:129
  9.1 13.1 %all-to-all-start = ((f32[64,5,2,128]{3,2,1,0:T(2,128)}), f32[64,5,2,128]{3,2,1,0:T(2,128)S(1)}, u32[]{:S(2)}, u32[]{:S(2)}) async-start(f32[64,5,2,128]{3,2,1,0:T(2,128)} %bitcast.12), calls=%async_computation | async-start | bytes 655360 | tf_op jit(solution)/shard_map/all_to_all | solution.py:431
  22.3 2.1 %prior_sides.1 = (f32[32,128]{1,0:T(8,128)}, f32[32,128]{1,0:T(8,128)}) custom-call(f32[8,16,512]{2,1,0:T(8,128)} %solid_ref.1, f32[3,8,16,512]{3,2,1,0:T(8,128)} %drag_ref.3, f32[8,16,512]{2,1,0:T(8,128)} %solid_ref.1, f32[3,8,16,512]{3,2,1,0:T(8,128)} %drag_ref.3), custom_call_target="tpu_custom_call" | custom-call | tf_op jit(solution)/shard_map/prior_sides/pallas_call | solution.py:337
  24.3 3.1 %collective-permute-start.2 = (f32[32,128]{1,0:T(8,128)}, f32[32,128]{1,0:T(8,128)S(1)}, u32[]{:S(2)}, u32[]{:S(2)}) collective-permute-start(f32[32,128]{1,0:T(8,128)} %get-tuple-element.18), channel_id=1, source_target_pairs={{0,1},{1,2},{2,3},{4,5},{5,6},{6,7},{8,9},{9,10},{10,11},{12,13},{... | collective-permute-start | bytes 49160 | tf_op jit(solution)/shard_map/ppermute | solution.py:421
  27.5 1.3 collective-permute-start.3
  28.8 6.8 %all-to-all-done = f32[64,5,2,128]{3,2,1,0:T(2,128)S(1)} async-done(((f32[64,5,2,128]{3,2,1,0:T(2,128)}), f32[64,5,2,128]{3,2,1,0:T(2,128)S(1)}, u32[]{:S(2)}, u32[]{:S(2)}) %all-to-all-start) | async-done | bytes 327712 | tf_op jit(solution)/shard_map/all_to_all | solution.py:431
  35.5 0.0 copy-start
  35.5 0.7 copy-done
  36.3 22.9 %deposit.1 = (f32[4,256,256]{2,1,0:T(8,128)}, f32[32,128]{1,0:T(8,128)}, f32[32,128]{1,0:T(8,128)}) custom-call(f32[640,128]{1,0:T(8,128)} %bitcast.9), custom_call_target="tpu_custom_call" | custom-call | tf_op jit(solution)/shard_map/deposit/pallas_call | solution.py:204
  59.1 3.1 %collective-permute-start = (f32[32,128]{1,0:T(8,128)}, f32[32,128]{1,0:T(8,128)S(1)}, u32[]{:S(2)}, u32[]{:S(2)}) collective-permute-start(f32[32,128]{1,0:T(8,128)} %get-tuple-element.16), channel_id=1, source_target_pairs={{0,1},{1,2},{2,3},{4,5},{5,6},{6,7},{8,9},{9,10},{10,11},{12,13},{... | collective-permute-start | bytes 49160 | tf_op jit(solution)/shard_map/ppermute | solution.py:421
  62.3 1.3 collective-permute-start.1
  63.6 0.6 add_convert_fusion.inside_ref
  64.2 0.0 collective-permute-done.2.prior_before
  64.2 0.0 copy-start.3
  64.2 0.0 collective-permute-done.3.prior_after
  64.2 0.0 copy-start.4
  64.2 0.0 collective-permute-done.before
  64.2 0.0 copy-start.5
  64.2 2.7 %collective-permute-done.1.after = f32[32,128]{1,0:T(8,128)S(1)} collective-permute-done((f32[32,128]{1,0:T(8,128)}, f32[32,128]{1,0:T(8,128)S(1)}, u32[]{:S(2)}, u32[]{:S(2)}) %collective-permute-start.1) | collective-permute-done | bytes 16416 | tf_op jit(solution)/shard_map/ppermute | solution.py:421
  67.0 0.0 copy-start.6
  67.0 0.0 copy-done.3
  67.0 0.0 copy-done.4
  67.0 0.0 copy-done.5
  67.0 0.6 copy-done.6
  67.6 9.2 %relax.1 = (f32[512,512]{1,0:T(8,128)}, f32[192,512]{1,0:T(8,128)}, f32[192,512]{1,0:T(8,128)}) custom-call(s32[4]{0:T(128)} %add_convert_fusion.inside_ref, f32[4,256,256]{2,1,0:T(8,128)} %get-tuple-element.15.target_ref, f32[8,16,512]{2,1,0:T(8,128)} %solid_ref.1, f32[3,8,16,512]{3,2,1,0:T(8,128)} %drag_ref.3, f32[32,128]{1,0:T(8,128)} %copy-done.5, ...), custom_call_target="tpu_custom_call" | custom-call | tf_op jit(solution)/shard_map/relax/pallas_call | solution.py:405
  76.8 4.7 %collective-permute-start.4 = (f32[192,512]{1,0:T(8,128)}, f32[192,512]{1,0:T(8,128)S(1)}, u32[]{:S(2)}, u32[]{:S(2)}) collective-permute-start(f32[192,512]{1,0:T(8,128)} %get-tuple-element.21), channel_id=1, source_target_pairs={{0,4},{4,8},{8,12},{12,16},{16,20},{20,24},{24,28},{28,32},{32,36}... | collective-permute-start | bytes 1179656 | tf_op jit(solution)/shard_map/ppermute | solution.py:421
  81.5 1.9 %collective-permute-start.5 = (f32[192,512]{1,0:T(8,128)}, f32[192,512]{1,0:T(8,128)S(1)}, u32[]{:S(2)}, u32[]{:S(2)}) collective-permute-start(f32[192,512]{1,0:T(8,128)} %get-tuple-element.22), channel_id=1, source_target_pairs={{4,0},{8,4},{12,8},{16,12},{20,16},{24,20},{28,24},{32,28},{36,32}... | collective-permute-start | bytes 1179656 | tf_op jit(solution)/shard_map/ppermute | solution.py:421
  83.4 3.1 %collective-permute-done.4.above_ref = f32[192,512]{1,0:T(8,128)S(1)} collective-permute-done((f32[192,512]{1,0:T(8,128)}, f32[192,512]{1,0:T(8,128)S(1)}, u32[]{:S(2)}, u32[]{:S(2)}) %collective-permute-start.4) | collective-permute-done | bytes 393248 | tf_op jit(solution)/shard_map/ppermute | solution.py:421
  86.5 0.0 copy-start.1
  86.5 4.3 %collective-permute-done.5.below_ref = f32[192,512]{1,0:T(8,128)S(1)} collective-permute-done((f32[192,512]{1,0:T(8,128)}, f32[192,512]{1,0:T(8,128)S(1)}, u32[]{:S(2)}, u32[]{:S(2)}) %collective-permute-start.5) | collective-permute-done | bytes 393248 | tf_op jit(solution)/shard_map/ppermute | solution.py:421
  90.8 0.0 copy-start.2
  90.8 0.0 copy-done.1
  90.8 0.8 copy-done.2
  91.6 26.1 %gather.1 = (f32[4,8,16,512]{3,2,1,0:T(8,128)}, f32[512,128]{1,0:T(8,128)}) custom-call(f32[512,512]{1,0:T(8,128)} %get-tuple-element.20.own_ref, f32[192,512]{1,0:T(8,128)} %copy-done.1, f32[192,512]{1,0:T(8,128)} %copy-done.2, f32[640,128]{1,0:T(8,128)} %bitcast.10), custom_call_target="tpu_custom_call" | custom-call | tf_op jit(solution)/shard_map/gather/pallas_call | solution.py:264
  117.7 21.0 %all_to_all.10 = f32[64,8,128]{2,1,0:T(8,128)} all-to-all(f32[64,8,128]{2,1,0:T(8,128)} %bitcast.13), channel_id=1, replica_groups=mesh['span'=64,'depth'=4] {'span'}, dimensions={0} | all-to-all | bytes 524288 | tf_op jit(solution)/shard_map/all_to_all | solution.py:445
  138.6 5.4 %pick.1 = f32[4,1,8192]{2,1,0:T(1,128)} custom-call(s32[1,1]{1,0:T(1,128)S(6)} %copy.9.count_ref, s32[1,8192]{1,0:T(1,128)} %bitcast.15, f32[1,8192]{1,0:T(1,128)} %get-tuple-element.24.position_ref, f32[512,128]{1,0:T(8,128)} %bitcast.11), custom_call_target="tpu_custom_call" | custom-call | tf_op jit(solution)/shard_map/pick/pallas_call | solution.py:308
Async XLA Ops:
  9.1 26.4 %all-to-all-start = ((f32[64,5,2,128]{3,2,1,0:T(2,128)}), f32[64,5,2,128]{3,2,1,0:T(2,128)S(1)}, u32[]{:S(2)}, u32[]{:S(2)}) async-start(f32[64,5,2,128]{3,2,1,0:T(2,128)} %bitcast.12), calls=%async_computation | async-start | bytes 655360 | tf_op jit(solution)/shard_map/all_to_all | solution.py:431
  24.3 39.8 %collective-permute-start.2 = (f32[32,128]{1,0:T(8,128)}, f32[32,128]{1,0:T(8,128)S(1)}, u32[]{:S(2)}, u32[]{:S(2)}) collective-permute-start(f32[32,128]{1,0:T(8,128)} %get-tuple-element.18), channel_id=1, source_target_pairs={{0,1},{1,2},{2,3},{4,5},{5,6},{6,7},{8,9},{9,10},{10,11},{12,13},{... | collective-permute-start | bytes 49160 | tf_op jit(solution)/shard_map/ppermute | solution.py:421
  27.5 36.7 %collective-permute-start.3 = (f32[32,128]{1,0:T(8,128)}, f32[32,128]{1,0:T(8,128)S(1)}, u32[]{:S(2)}, u32[]{:S(2)}) collective-permute-start(f32[32,128]{1,0:T(8,128)} %get-tuple-element.19), channel_id=1, source_target_pairs={{1,0},{2,1},{3,2},{5,4},{6,5},{7,6},{9,8},{10,9},{11,10},{13,12},{... | collective-permute-start | bytes 49160 | tf_op jit(solution)/shard_map/ppermute | solution.py:421
  35.5 0.7 copy-start
  59.1 5.1 %collective-permute-start = (f32[32,128]{1,0:T(8,128)}, f32[32,128]{1,0:T(8,128)S(1)}, u32[]{:S(2)}, u32[]{:S(2)}) collective-permute-start(f32[32,128]{1,0:T(8,128)} %get-tuple-element.16), channel_id=1, source_target_pairs={{0,1},{1,2},{2,3},{4,5},{5,6},{6,7},{8,9},{9,10},{10,11},{12,13},{... | collective-permute-start | bytes 49160 | tf_op jit(solution)/shard_map/ppermute | solution.py:421
  62.3 4.7 %collective-permute-start.1 = (f32[32,128]{1,0:T(8,128)}, f32[32,128]{1,0:T(8,128)S(1)}, u32[]{:S(2)}, u32[]{:S(2)}) collective-permute-start(f32[32,128]{1,0:T(8,128)} %get-tuple-element.17), channel_id=1, source_target_pairs={{1,0},{2,1},{3,2},{5,4},{6,5},{7,6},{9,8},{10,9},{11,10},{13,12},{... | collective-permute-start | bytes 49160 | tf_op jit(solution)/shard_map/ppermute | solution.py:421
  64.2 2.8 %copy-start.3 = (f32[32,128]{1,0:T(8,128)}, f32[32,128]{1,0:T(8,128)S(1)}, u32[]{:S(2)}) copy-start(f32[32,128]{1,0:T(8,128)S(1)} %collective-permute-done.2.prior_before) | copy-start | bytes 49156
  64.2 2.8 %copy-start.4 = (f32[32,128]{1,0:T(8,128)}, f32[32,128]{1,0:T(8,128)S(1)}, u32[]{:S(2)}) copy-start(f32[32,128]{1,0:T(8,128)S(1)} %collective-permute-done.3.prior_after) | copy-start | bytes 49156
  64.2 2.8 %copy-start.5 = (f32[32,128]{1,0:T(8,128)}, f32[32,128]{1,0:T(8,128)S(1)}, u32[]{:S(2)}) copy-start(f32[32,128]{1,0:T(8,128)S(1)} %collective-permute-done.before) | copy-start | bytes 49156
  67.0 0.6 copy-start.6
  76.8 9.7 %collective-permute-start.4 = (f32[192,512]{1,0:T(8,128)}, f32[192,512]{1,0:T(8,128)S(1)}, u32[]{:S(2)}, u32[]{:S(2)}) collective-permute-start(f32[192,512]{1,0:T(8,128)} %get-tuple-element.21), channel_id=1, source_target_pairs={{0,4},{4,8},{8,12},{12,16},{16,20},{20,24},{24,28},{28,32},{32,36}... | collective-permute-start | bytes 1179656 | tf_op jit(solution)/shard_map/ppermute | solution.py:421
  81.5 9.3 %collective-permute-start.5 = (f32[192,512]{1,0:T(8,128)}, f32[192,512]{1,0:T(8,128)S(1)}, u32[]{:S(2)}, u32[]{:S(2)}) collective-permute-start(f32[192,512]{1,0:T(8,128)} %get-tuple-element.22), channel_id=1, source_target_pairs={{4,0},{8,4},{12,8},{16,12},{20,16},{24,20},{28,24},{32,28},{36,32}... | collective-permute-start | bytes 1179656 | tf_op jit(solution)/shard_map/ppermute | solution.py:421
  86.5 4.3 %copy-start.1 = (f32[192,512]{1,0:T(8,128)}, f32[192,512]{1,0:T(8,128)S(1)}, u32[]{:S(2)}) copy-start(f32[192,512]{1,0:T(8,128)S(1)} %collective-permute-done.4.above_ref) | copy-start | bytes 1179652
  90.8 0.8 copy-start.2

commit v3 on v2

--- a/solution.py
+++ b/solution.py
@@ -6,6 +6,7 @@
 from jax.sharding import PartitionSpec as P
 
 F32, BF16, I32 = jnp.float32, jnp.bfloat16, jnp.int32
+MIB = 1 << 20
 OWNERS = 64
 CAP = 256
 LAYERS, CX, CY = 8, 16, 512
@@ -15,7 +16,7 @@
 BACK_ROWS = 8
 SWEEPS = 6
 RIM = SWEEPS
-SIDE_ROWS = 4 * CX // 16 * LAYERS
+SIDE_ROWS = 2 * 4 * CX // 16 * LAYERS
 PHI_LIMIT = 0.6
 
 
@@ -50,9 +51,14 @@
     return lax.dot_general(left, right, (((1,), (0,)), ((), ())), preferred_element_type=F32)
 
 
+def at_edge(axis):
+    place = lax.axis_index(axis)
+    return place == 0, place == lax.axis_size(axis) - 1
+
+
 def fold_sides(pieces, left_ref, right_ref):
     lane = lax.broadcasted_iota(I32, (LAYERS, 128), 1)
-    for group in range(4 * CX // 16):
+    for group in range(SIDE_ROWS // LAYERS):
         left = jnp.zeros((LAYERS, 128), F32)
         right = jnp.zeros((LAYERS, 128), F32)
         for place in range(16):
@@ -65,15 +71,19 @@
         right_ref[group * LAYERS : (group + 1) * LAYERS, :] = right
 
 
-def unfold_side(row, before_ref, after_ref):
-    lane = lax.broadcasted_iota(I32, (LAYERS, 128), 1)
+def unfold_side(row, before_ref, after_ref, is_before, is_after):
     group, place = row // 16, row % 16
     after = after_ref[group * LAYERS : (group + 1) * LAYERS, :]
     before = before_ref[group * LAYERS : (group + 1) * LAYERS, :]
     after = pltpu.roll(after, 128 - 8 * place, 1) if place else after
     shift = (120 - 8 * place) % 128
     before = pltpu.roll(before, shift, 1) if shift else before
-    return jnp.where(lane < 8, after, jnp.where(lane >= 120, before, 0.0))
+    return jnp.where(is_after, after, jnp.where(is_before, before, 0.0))
+
+
+def prior_row(solid_ref, drag_ref, row, lanes):
+    comp, x = row // CX, row % CX
+    return solid_ref[:, x, lanes] if comp == 0 else drag_ref[comp - 1, :, x, lanes]
 
 
 PACK_BLOCK = 1024
@@ -136,6 +146,7 @@
         out_specs=(vmem, vmem),
         scratch_shapes=[pltpu.VMEM((10 * OWNERS, CAP), F32)],
         name="pack",
+        compiler_params=pltpu.CompilerParams(vmem_limit_bytes=8 * MIB),
     )(count, slab, cell, volume, drag)
 
 
@@ -158,7 +169,7 @@
     return jnp.concatenate([ref[pl.ds(base, 1), :], ref[pl.ds(base + 1, 1), :]], axis=1)
 
 
-def deposit_kernel(recv_ref, out_ref, first_ref, last_ref):
+def deposit_kernel(recv_ref, solid_ref, drag_ref, out_ref, first_ref, last_ref):
     out_ref[...] = jnp.zeros_like(out_ref)
     zero = jnp.zeros((), BF16)
 
@@ -190,6 +201,9 @@
     out_ref[0] = jnp.minimum(out_ref[0], PHI_LIMIT)
 
     def pieces(row):
+        if row >= 4 * CX:
+            row -= 4 * CX
+            return tuple(prior_row(solid_ref, drag_ref, row, pl.ds(at, 128)) for at in (0, CY - 128))
         comp, x = row // CX, row % CX
         first = out_ref[comp, x * LAYERS : (x + 1) * LAYERS, 0:128]
         last = out_ref[comp, (CX + x) * LAYERS : (CX + x + 1) * LAYERS, LO - 128 : LO]
@@ -198,28 +212,31 @@
     fold_sides(pieces, first_ref, last_ref)
 
 
-def deposit(received):
+def deposit(received, solid, drag):
     vmem = pl.BlockSpec(memory_space=pltpu.VMEM)
     side = jax.ShapeDtypeStruct((SIDE_ROWS, 128), F32)
     return pl.pallas_call(
         deposit_kernel,
         out_shape=(jax.ShapeDtypeStruct((4, HI, LO), F32), side, side),
-        in_specs=[vmem],
+        in_specs=[vmem] * 3,
         out_specs=(vmem, vmem, vmem),
         name="deposit",
-    )(received)
+        compiler_params=pltpu.CompilerParams(vmem_limit_bytes=12 * MIB),
+    )(received, solid, drag)
 
 
 GATHER_SOURCES = 2
 
 
 def gather_kernel(own_ref, above_ref, below_ref, recv_ref, fields_ref, out_ref, tops, bottoms):
+    top, bottom = at_edge("span")
+
     def smooth(comp, x):
         row = own_ref[pl.ds((comp * CX + x) * LAYERS, LAYERS), :]
         if x < RIM:
-            row = row + above_ref[pl.ds((comp * RIM + x) * LAYERS, LAYERS), :]
+            row = row + jnp.where(top, 0.0, above_ref[pl.ds((comp * RIM + x) * LAYERS, LAYERS), :])
         if x >= CX - RIM:
-            row = row + below_ref[pl.ds((comp * RIM + x - CX + RIM) * LAYERS, LAYERS), :]
+            row = row + jnp.where(bottom, 0.0, below_ref[pl.ds((comp * RIM + x - CX + RIM) * LAYERS, LAYERS), :])
         return row
 
     for pair in range(0, CX, 2):
@@ -271,6 +288,7 @@
         out_specs=(vmem, vmem),
         scratch_shapes=[pltpu.VMEM((4, HI, LO), BF16)] * 2,
         name="gather",
+        compiler_params=pltpu.CompilerParams(vmem_limit_bytes=16 * MIB),
     )(own, above, below, received)
 
 
@@ -312,45 +330,21 @@
         out_specs=vmem,
         scratch_shapes=[pltpu.VMEM((4 * OWNERS, CAP), BF16)] * 2,
         name="pick",
+        compiler_params=pltpu.CompilerParams(vmem_limit_bytes=8 * MIB),
     )(count, slab, position, back)
 
 
-def prior_row(solid_ref, drag_ref, row):
-    comp, x = row // CX, row % CX
-    return solid_ref[:, x, :] if comp == 0 else drag_ref[comp - 1, :, x, :]
-
-
-def prior_kernel(solid_left, drag_left, solid_right, drag_right, first_ref, last_ref):
-    def pieces(row):
-        return prior_row(solid_left, drag_left, row), prior_row(solid_right, drag_right, row)
-
-    fold_sides(pieces, first_ref, last_ref)
-
-
-def prior_sides(solid, drag):
-    vmem = pl.BlockSpec(memory_space=pltpu.VMEM)
-    side = jax.ShapeDtypeStruct((SIDE_ROWS, 128), F32)
-    edges = []
-    for block in (0, CY // 128 - 1):
-        edges.append(pl.BlockSpec((LAYERS, CX, 128), lambda i, block=block: (0, 0, block)))
-        edges.append(pl.BlockSpec((3, LAYERS, CX, 128), lambda i, block=block: (0, 0, 0, block)))
-    return pl.pallas_call(
-        prior_kernel,
-        grid=(1,),
-        out_shape=(side, side),
-        in_specs=edges,
-        out_specs=(pl.BlockSpec((SIDE_ROWS, 128), lambda i: (0, 0)),) * 2,
-        name="prior_sides",
-    )(solid, drag, solid, drag)
-
-
 WIDE = CY + 128
 
 
 def relax_kernel(
-    inside_ref, target_ref, solid_ref, drag_ref, before, after, prior_before, prior_after,
-    own_ref, up_ref, down_ref, state, source,
+    target_ref, solid_ref, drag_ref, before, after, own_ref, up_ref, down_ref, state, source
 ):
+    top, bottom = at_edge("span")
+    first, last = at_edge("depth")
+    near = lax.broadcasted_iota(I32, (LAYERS, 128), 1)
+    is_before = (near >= 120) & jnp.logical_not(first)
+    is_after = (near < 8) & jnp.logical_not(last)
     blank = jnp.zeros((LAYERS, WIDE), F32)
     for comp in range(4):
         for x in range(RIM):
@@ -361,17 +355,15 @@
             for half in range(2):
                 spot = pl.ds((half * CX + x) * LAYERS, LAYERS)
                 source[comp, x, :, half * LO : (half + 1) * LO] = target_ref[comp, spot, :]
-            source[comp, x, :, CY:WIDE] = unfold_side(row, before, after)
-            state[comp, RIM + x, :, 0:CY] = prior_row(solid_ref, drag_ref, row)
-            state[comp, RIM + x, :, CY:WIDE] = unfold_side(row, prior_before, prior_after)
+            source[comp, x, :, CY:WIDE] = unfold_side(row, before, after, is_before, is_after)
+            state[comp, RIM + x, :, 0:CY] = prior_row(solid_ref, drag_ref, row, slice(None))
+            state[comp, RIM + x, :, CY:WIDE] = unfold_side(4 * CX + row, before, after, is_before, is_after)
 
     lane = lax.broadcasted_iota(I32, (LAYERS, WIDE), 1)
-    outside = ((lane >= CY + 64) & (inside_ref[2] == 0)) | (
-        (lane >= CY) & (lane < CY + 64) & (inside_ref[3] == 0)
-    )
+    outside = ((lane >= CY + 64) & first) | ((lane >= CY) & (lane < CY + 64) & last)
     factor = jnp.where(outside, 0.0, 0.2)
-    above_factor = jnp.where(inside_ref[0] == 0, 0.0, factor)
-    below_factor = jnp.where(inside_ref[1] == 0, 0.0, factor)
+    above_factor = jnp.where(top, 0.0, factor)
+    below_factor = jnp.where(bottom, 0.0, factor)
 
     def comp_step(comp, carry):
         for sweep in range(SWEEPS):
@@ -399,46 +391,37 @@
             down_ref[spot, :] = state[comp, RIM + CX + x, :, 0:CY]
 
 
-def relax(inside, *arrays):
+def relax(*arrays):
     vmem = pl.BlockSpec(memory_space=pltpu.VMEM)
     rim = jax.ShapeDtypeStruct((4 * RIM * LAYERS, CY), F32)
     return pl.pallas_call(
         relax_kernel,
         out_shape=(jax.ShapeDtypeStruct((4 * CX * LAYERS, CY), F32), rim, rim),
-        in_specs=[pl.BlockSpec(memory_space=pltpu.SMEM)] + [vmem] * 7,
+        in_specs=[vmem] * 5,
         out_specs=(vmem, vmem, vmem),
         scratch_shapes=[
             pltpu.VMEM((4, CX + 2 * RIM, LAYERS, WIDE), F32),
             pltpu.VMEM((4, CX, LAYERS, WIDE), F32),
         ],
         name="relax",
-    )(inside, *arrays)
+        compiler_params=pltpu.CompilerParams(vmem_limit_bytes=16 * MIB),
+    )(*arrays)
 
 
 def shifted(array, axis, step):
     count = lax.axis_size(axis)
-    pairs = [(i, i + step) for i in range(count) if 0 <= i + step < count]
-    return lax.ppermute(array, axis, pairs)
+    return lax.ppermute(array, axis, [(i, (i + step) % count) for i in range(count)])
 
 
 def on_device(part_slab, part_cell, part_volume, part_drag, part_count, prior_solid, prior_drag):
     slab = part_slab.reshape(1, PARTS)
-    row, col = lax.axis_index("span"), lax.axis_index("depth")
-    inside = jnp.stack(
-        [row > 0, row < lax.axis_size("span") - 1, col > 0, col < lax.axis_size("depth") - 1]
-    ).astype(I32)
     sent, position = pack(part_count, slab, part_cell, part_volume, part_drag)
     received = lax.all_to_all(sent.reshape(OWNERS, 5, 2, 128), "span", 0, 0, tiled=True)
     received = received.reshape(OWNERS * ROWS, 128)
-    prior_first, prior_last = prior_sides(prior_solid, prior_drag)
-    prior_before = shifted(prior_last, "depth", 1)
-    prior_after = shifted(prior_first, "depth", -1)
-    target, first, last = deposit(received)
+    target, first, last = deposit(received, prior_solid, prior_drag)
     before = shifted(last, "depth", 1)
     after = shifted(first, "depth", -1)
-    own, up, down = relax(
-        inside, target, prior_solid, prior_drag, before, after, prior_before, prior_after
-    )
+    own, up, down = relax(target, prior_solid, prior_drag, before, after)
     from_above = shifted(down, "span", 1)
     from_below = shifted(up, "span", -1)
     fields, returned = gather(own, from_above, from_below, received)

time: 145 us -> 130 us (0.90)
  blocking collectives: 21 us -> 47 us
  starting transfers between devices: 28.6 us -> 5.61 us
  Pallas kernels: 73.4 us -> 62.1 us
  waiting for transfers between devices: 16.9 us -> 8.84 us
  local copies, waits for them, and re-layouts: 2.09 us -> 4.12 us
    all_to_all x0 -> x1, blocking collectives: none -> 26.2 us  [on_device(): lax.all_to_all(sent.reshape(OWNERS, 5, 2, 128), 'span', 0, 0, tiled=True)]
    all_to_all x1 -> x0, starting transfers between devices: 13.1 us -> none  [on_device(): lax.all_to_all(sent.reshape(OWNERS, 5, 2, 128), 'span', 0, 0, tiled=True)]
    ppermute x6 -> x4, starting transfers between devices: 15.4 us -> 5.61 us  [shifted(): lax.ppermute(array, axis, [(i, (i + step) % count) for i in range(count)])]
    all_to_all x1 -> x0, waiting for transfers between devices: 6.78 us -> none  [on_device(): lax.all_to_all(sent.reshape(OWNERS, 5, 2, 128), 'span', 0, 0, tiled=True)]
    pallas_call x1, Pallas kernels: 9.2 us -> 6.22 us  [relax(): pl.pallas_call(relax_kernel, out_shape=(jax.ShapeDtypeStruct((4 * CX * LA...]
    pallas_call x1 -> x0, Pallas kernels: 2.05 us -> none  [prior_sides(): pl.pallas_call(prior_kernel, grid=(1,), out_shape=(side, side), in_specs=...]
    unnamed x14 -> x16, local copies, waits for them, and re-layouts: 2.09 us -> 4.12 us
    pallas_call x1, Pallas kernels: 26.1 us -> 24.1 us  [gather(): pl.pallas_call(gather_kernel, out_shape=(jax.ShapeDtypeStruct((4, LAYERS,...]
  transfers between devices with their start and end apart: 7 -> 4, of which waited for: 4 -> 3; matrix products, arithmetic and copies ran while one was open for 0% -> 0% of each run, Pallas kernels for 17% -> 0%
where the time goes in v3:
time: 130 us; the launch traced here: 129 us
  Pallas kernels  62.1 us (48%)
  blocking collectives  47 us (36%)
  waiting for transfers between devices  8.84 us (7%)
  starting transfers between devices  5.61 us (4%)
  local copies, waits for them, and re-layouts  4.12 us (3%)
  between operations  1.4 us (1%)
    all_to_all x1, blocking collectives, on_device(): lax.all_to_all(sent.reshape(OWNERS, 5, 2, 128), 'span', 0, 0, tiled=True)  26.2 us
    pallas_call x1, Pallas kernels, gather(): pl.pallas_call(gather_kernel, out_shape=(jax.ShapeDtypeStruct((4, LAYERS,...  24.1 us
    pallas_call x1, Pallas kernels, deposit(): pl.pallas_call(deposit_kernel, out_shape=(jax.ShapeDtypeStruct((4, HI, LO...  21.2 us
    all_to_all x1, blocking collectives, on_device(): lax.all_to_all(returned.reshape(OWNERS, BACK_ROWS, 128), 'span', 0, 0, ti...  20.8 us
    ppermute x4, waiting for transfers between devices, shifted(): lax.ppermute(array, axis, [(i, (i + step) % count) for i in range(count)])  8.84 us
    pallas_call x1, Pallas kernels, relax(): pl.pallas_call(relax_kernel, out_shape=(jax.ShapeDtypeStruct((4 * CX * LA...  6.22 us
    pallas_call x1, Pallas kernels, pack(): pl.pallas_call(pack_kernel, out_shape=(jax.ShapeDtypeStruct((OWNERS * ROW...  6.17 us
    ppermute x4, starting transfers between devices, shifted(): lax.ppermute(array, axis, [(i, (i + step) % count) for i in range(count)])  5.61 us
  transfers between devices with their start and end apart: 4, of which 3 were waited for; matrix products, arithmetic and copies ran while one was open for 0% of the time, Pallas kernels for 0%

profile of v3, /device:TPU:1, one launch (start us, length us, event | category | flops | bytes accessed | tf_op | source)
XLA Modules:
  0.0 129.1 jit_solution(2526309939702529615)
XLA Ops:
  0.6 0.0 copy-start
  1.4 0.0 copy-start.3
  1.4 0.7 copy-done.3
  2.1 0.0 copy-start.5
  2.1 0.9 copy-done.5
  3.0 0.0 copy-start.6
  3.0 0.8 copy-done.6
  3.8 0.0 copy-start.7
  3.8 0.8 copy-done.7
  4.5 6.2 %pack.1 = (f32[640,128]{1,0:T(8,128)S(1)}, f32[1,8192]{1,0:T(1,128)S(1)}) custom-call(s32[1,1]{1,0:T(1,128)S(6)} %copy.9.count_ref, s32[1,8192]{1,0:T(1,128)S(1)} %bitcast.10, s32[1,8192]{1,0:T(1,128)S(1)} %copy-done.6, f32[1,8192]{1,0:T(1,128)S(1)} %copy-done.7, f32[3,1,8192]{2,1,0:T(1,128)S(1)} %copy-done.5), custom_call_target="tpu_custom_call" | custom-call | tf_op jit(solution)/shard_map/pack/pallas_call | solution.py:139
  10.7 26.2 %all_to_all.10 = f32[64,5,2,128]{3,2,1,0:T(2,128)S(1)} all-to-all(f32[64,5,2,128]{3,2,1,0:T(2,128)S(1)} %bitcast.8), channel_id=1, replica_groups=mesh['span'=64,'depth'=4] {'span'}, dimensions={0} | all-to-all | bytes 655360 | tf_op jit(solution)/shard_map/all_to_all | solution.py:419
  36.9 0.0 copy-done
  36.9 0.0 copy-start.1
  36.9 0.9 copy-done.1
  37.9 0.0 copy-start.2
  37.9 21.2 %deposit.1 = (f32[4,256,256]{2,1,0:T(8,128)S(1)}, f32[64,128]{1,0:T(8,128)S(1)}, f32[64,128]{1,0:T(8,128)S(1)}) custom-call(f32[640,128]{1,0:T(8,128)S(1)} %bitcast.5, f32[8,16,512]{2,1,0:T(8,128)S(1)} %copy-done.1, f32[3,8,16,512]{3,2,1,0:T(8,128)S(1)} %copy-done), custom_call_target="tpu_custom_call" | custom-call | tf_op jit(solution)/shard_map/deposit/pallas_call | solution.py:218
  59.1 1.3 %collective-permute-start = (f32[64,128]{1,0:T(8,128)S(1)}, f32[64,128]{1,0:T(8,128)S(1)}, u32[]{:S(2)}, u32[]{:S(2)}) collective-permute-start(f32[64,128]{1,0:T(8,128)S(1)} %get-tuple-element.14), channel_id=1, source_target_pairs={{0,1},{1,2},{2,3},{3,0},{4,5},{5,6},{6,7},{7,4},{8,9},{9,10},{10,1... | collective-permute-start | bytes 98312 | tf_op jit(solution)/shard_map/ppermute | solution.py:413
  60.4 1.4 %collective-permute-start.1 = (f32[64,128]{1,0:T(8,128)S(1)}, f32[64,128]{1,0:T(8,128)S(1)}, u32[]{:S(2)}, u32[]{:S(2)}) collective-permute-start(f32[64,128]{1,0:T(8,128)S(1)} %get-tuple-element.15), channel_id=1, source_target_pairs={{0,3},{1,0},{2,1},{3,2},{4,7},{5,4},{6,5},{7,6},{8,11},{9,8},{10,9... | collective-permute-start | bytes 98312 | tf_op jit(solution)/shard_map/ppermute | solution.py:413
  61.9 1.3 %collective-permute-done.before = f32[64,128]{1,0:T(8,128)S(1)} collective-permute-done((f32[64,128]{1,0:T(8,128)S(1)}, f32[64,128]{1,0:T(8,128)S(1)}, u32[]{:S(2)}, u32[]{:S(2)}) %collective-permute-start) | collective-permute-done | bytes 32800 | tf_op jit(solution)/shard_map/ppermute | solution.py:413
  63.1 0.0 collective-permute-done.1.after
  63.2 0.0 copy-done.2
  63.2 6.2 %relax.1 = (f32[512,512]{1,0:T(8,128)S(1)}, f32[192,512]{1,0:T(8,128)S(1)}, f32[192,512]{1,0:T(8,128)S(1)}) custom-call(f32[4,256,256]{2,1,0:T(8,128)S(1)} %get-tuple-element.13.target_ref, f32[8,16,512]{2,1,0:T(8,128)S(1)} %copy-done.2, f32[3,8,16,512]{3,2,1,0:T(8,128)S(1)} %copy-done, f32[64,128]{1,0:T(8,128)S(1)} %collective-permute-done.before, ...), custom_call_target="tpu_custom_call" | custom-call | tf_op jit(solution)/shard_map/relax/pallas_call | solution.py:397
  69.4 2.9 %collective-permute-start.2 = (f32[192,512]{1,0:T(8,128)S(1)}, f32[192,512]{1,0:T(8,128)S(1)}, u32[]{:S(2)}, u32[]{:S(2)}) collective-permute-start(f32[192,512]{1,0:T(8,128)S(1)} %get-tuple-element.17), channel_id=1, source_target_pairs={{0,4},{4,8},{8,12},{12,16},{16,20},{20,24},{24,28},{28,32},{32,36}... | collective-permute-start | bytes 1179656 | tf_op jit(solution)/shard_map/ppermute | solution.py:413
  72.3 0.0 collective-permute-start.3
  72.3 4.7 %collective-permute-done.2.above_ref = f32[192,512]{1,0:T(8,128)S(1)} collective-permute-done((f32[192,512]{1,0:T(8,128)S(1)}, f32[192,512]{1,0:T(8,128)S(1)}, u32[]{:S(2)}, u32[]{:S(2)}) %collective-permute-start.2) | collective-permute-done | bytes 393248 | tf_op jit(solution)/shard_map/ppermute | solution.py:413
  77.0 2.8 %collective-permute-done.3.below_ref = f32[192,512]{1,0:T(8,128)S(1)} collective-permute-done((f32[192,512]{1,0:T(8,128)S(1)}, f32[192,512]{1,0:T(8,128)S(1)}, u32[]{:S(2)}, u32[]{:S(2)}) %collective-permute-start.3) | collective-permute-done | bytes 393248 | tf_op jit(solution)/shard_map/ppermute | solution.py:413
  79.8 24.1 %gather.1 = (f32[4,8,16,512]{3,2,1,0:T(8,128)}, f32[512,128]{1,0:T(8,128)S(1)}) custom-call(f32[512,512]{1,0:T(8,128)S(1)} %get-tuple-element.16.own_ref, f32[192,512]{1,0:T(8,128)S(1)} %collective-permute-done.2.above_ref, f32[192,512]{1,0:T(8,128)S(1)} %collective-permute-done.3.below_ref, f32[640,128]{1,0:T(8,128)S(1)} %bitcast.6), custom_call_target="tpu_custom_call" | custom-call | tf_op jit(solution)/shard_map/gather/pallas_call | solution.py:281
  103.9 0.0 copy-start.4
  103.9 20.8 %all_to_all.11 = f32[64,8,128]{2,1,0:T(8,128)S(1)} all-to-all(f32[64,8,128]{2,1,0:T(8,128)S(1)} %bitcast.9), channel_id=1, replica_groups=mesh['span'=64,'depth'=4] {'span'}, dimensions={0} | all-to-all | bytes 524288 | tf_op jit(solution)/shard_map/all_to_all | solution.py:428
  124.7 0.0 copy-done.4
  124.7 4.4 %pick.1 = f32[4,1,8192]{2,1,0:T(1,128)} custom-call(s32[1,1]{1,0:T(1,128)S(6)} %copy.9.count_ref, s32[1,8192]{1,0:T(1,128)S(1)} %bitcast.11, f32[1,8192]{1,0:T(1,128)S(1)} %get-tuple-element.20.position_ref, f32[512,128]{1,0:T(8,128)S(1)} %bitcast.7), custom_call_target="tpu_custom_call" | custom-call | tf_op jit(solution)/shard_map/pick/pallas_call | solution.py:326
Async XLA Ops:
  0.6 36.3 %copy-start = (f32[3,8,16,512]{3,2,1,0:T(8,128)S(1)}, f32[3,8,16,512]{3,2,1,0:T(8,128)}, u32[]{:S(2)}) copy-start(f32[3,8,16,512]{3,2,1,0:T(8,128)} %drag_ref.5) | copy-start | bytes 2359300
  1.4 0.8 copy-start.3
  2.1 0.9 copy-start.5
  3.0 0.8 copy-start.6
  3.8 0.8 copy-start.7
  36.9 1.0 copy-start.1
  37.9 25.3 %copy-start.2 = (f32[8,16,512]{2,1,0:T(8,128)S(1)}, f32[8,16,512]{2,1,0:T(8,128)}, u32[]{:S(2)}) copy-start(f32[8,16,512]{2,1,0:T(8,128)} %solid_ref.3) | copy-start | bytes 786436
  59.1 4.1 %collective-permute-start = (f32[64,128]{1,0:T(8,128)S(1)}, f32[64,128]{1,0:T(8,128)S(1)}, u32[]{:S(2)}, u32[]{:S(2)}) collective-permute-start(f32[64,128]{1,0:T(8,128)S(1)} %get-tuple-element.14), channel_id=1, source_target_pairs={{0,1},{1,2},{2,3},{3,0},{4,5},{5,6},{6,7},{7,4},{8,9},{9,10},{10,1... | collective-permute-start | bytes 98312 | tf_op jit(solution)/shard_map/ppermute | solution.py:413
  60.4 2.8 %collective-permute-start.1 = (f32[64,128]{1,0:T(8,128)S(1)}, f32[64,128]{1,0:T(8,128)S(1)}, u32[]{:S(2)}, u32[]{:S(2)}) collective-permute-start(f32[64,128]{1,0:T(8,128)S(1)} %get-tuple-element.15), channel_id=1, source_target_pairs={{0,3},{1,0},{2,1},{3,2},{4,7},{5,4},{6,5},{7,6},{8,11},{9,8},{10,9... | collective-permute-start | bytes 98312 | tf_op jit(solution)/shard_map/ppermute | solution.py:413
  69.4 7.6 %collective-permute-start.2 = (f32[192,512]{1,0:T(8,128)S(1)}, f32[192,512]{1,0:T(8,128)S(1)}, u32[]{:S(2)}, u32[]{:S(2)}) collective-permute-start(f32[192,512]{1,0:T(8,128)S(1)} %get-tuple-element.17), channel_id=1, source_target_pairs={{0,4},{4,8},{8,12},{12,16},{16,20},{20,24},{24,28},{28,32},{32,36}... | collective-permute-start | bytes 1179656 | tf_op jit(solution)/shard_map/ppermute | solution.py:413
  72.3 7.5 %collective-permute-start.3 = (f32[192,512]{1,0:T(8,128)S(1)}, f32[192,512]{1,0:T(8,128)S(1)}, u32[]{:S(2)}, u32[]{:S(2)}) collective-permute-start(f32[192,512]{1,0:T(8,128)S(1)} %get-tuple-element.18), channel_id=1, source_target_pairs={{0,252},{4,0},{8,4},{12,8},{16,12},{20,16},{24,20},{28,24},{32,28}... | collective-permute-start | bytes 1179656 | tf_op jit(solution)/shard_map/ppermute | solution.py:413
  103.9 20.8 %copy-start.4 = (s32[1,8192,1]{1,2,0:T(1,128)S(1)}, s32[1,8192,1]{1,2,0:T(1,128)}, u32[]{:S(2)}) copy-start(s32[1,8192,1]{1,2,0:T(1,128)} %param.7) | copy-start | bytes 98308

commit v4 on v3

--- a/solution.py
+++ b/solution.py
@@ -88,28 +88,58 @@
 
 PACK_BLOCK = 1024
 SUB = 256
-
-
-def pack_kernel(count_ref, slab_ref, cell_ref, volume_ref, drag_ref, out_ref, position_ref, acc):
+CLASSES = 4
+
+
+def pack_kernel(
+    count_ref, slab_any, cell_any, volume_any, drag_any, out_ref, position_ref,
+    slab_ref, cell_ref, volume_ref, drag_ref, acc, sems,
+):
+    sources, targets = (slab_any, cell_any, volume_any, drag_any), (slab_ref, cell_ref, volume_ref, drag_ref)
+    copies = [pltpu.make_async_copy(f, t, sems.at[i]) for i, (f, t) in enumerate(zip(sources, targets))]
+    for copy in copies:
+        copy.start()
     count = count_ref[0, 0]
     acc[...] = jnp.zeros_like(acc)
-    before_mask = lax.broadcasted_iota(I32, (SUB, SUB + 128), 0)
-    after_mask = lax.broadcasted_iota(I32, (SUB, SUB + 128), 1)
-    upper = jnp.where((before_mask < after_mask) | (after_mask >= SUB), 1.0, 0.0).astype(BF16)
+    earlier = lax.broadcasted_iota(I32, (SUB, SUB), 0)
+    later = lax.broadcasted_iota(I32, (SUB, SUB), 1)
+    upper = jnp.where(earlier <= later, 1.0, 0.0).astype(BF16)
+    for copy in copies:
+        copy.wait()
+
+    def live_slab(start, size):
+        lane = lax.broadcasted_iota(I32, (1, size), 1) + start
+        return jnp.where(lane < count, slab_ref[0:1, pl.ds(start, size)], CLASSES * OWNERS)
+
+    def classes(start, size):
+        return lax.shift_right_logical(cell_ref[0:1, pl.ds(start, size)], 14)
+
+    def count_step(block, counts):
+        start = pl.multiple_of(block * PACK_BLOCK, PACK_BLOCK)
+        member = one_hot(live_slab(start, PACK_BLOCK).astype(F32), OWNERS)
+        kind = one_hot(classes(start, PACK_BLOCK).astype(F32), 128)
+        return counts + dot_nt(member, kind)
+
+    counts = lax.fori_loop(0, PARTS // PACK_BLOCK, count_step, jnp.zeros((OWNERS, 128), F32))
+    numbers = [jnp.broadcast_to(counts[:, kind : kind + 1], (OWNERS, 128)) for kind in range(CLASSES)]
+    starts, end = [], jnp.zeros((OWNERS, 128), F32)
+    for kind in range(CLASSES):
+        rest = sum(numbers[kind:])
+        starts.append(jnp.maximum(end, jnp.minimum(float(kind * CAP // CLASSES), CAP - rest)))
+        end = starts[-1] + numbers[kind]
 
     def step(block, offset):
         hots, lefts = [], []
         for sub in range(PACK_BLOCK // SUB):
             start = pl.multiple_of(block * PACK_BLOCK + sub * SUB, SUB)
             spot = pl.ds(start, SUB)
-            lane = lax.broadcasted_iota(I32, (1, SUB), 1) + start
-            slab = jnp.where(lane < count, slab_ref[0:1, spot], OWNERS).astype(F32)
-            member = row_is(slab, OWNERS)
-            member_one = jnp.where(member, jnp.ones((), BF16), jnp.zeros((), BF16))
-            ranks = dot_nn(member_one, upper)
-            place = ranks[:, :SUB] + jnp.concatenate([offset, offset], axis=1)
-            position = jnp.sum(place * member_one.astype(F32), axis=0, keepdims=True)
-            offset = offset + ranks[:, SUB:]
+            slab = live_slab(start, SUB)
+            member = row_is(slab.astype(F32), OWNERS)
+            sorted_one = one_hot((slab + classes(start, SUB) * OWNERS).astype(F32), CLASSES * OWNERS)
+            ranks = dot_nn(sorted_one, upper)
+            place = ranks + jnp.concatenate([offset, offset], axis=1)
+            position = jnp.sum(place * sorted_one.astype(F32), axis=0, keepdims=True) - 1.0
+            offset = offset + jnp.broadcast_to(ranks[:, SUB - 1 : SUB], offset.shape)
             position_ref[0:1, spot] = position
             hots.append(one_hot(position, CAP))
             cell = cell_ref[0:1, spot]
@@ -125,7 +155,7 @@
         acc[...] += dot_nt(jnp.concatenate(lefts, axis=1), jnp.concatenate(hots, axis=1))
         return offset
 
-    lax.fori_loop(0, PARTS // PACK_BLOCK, step, jnp.zeros((OWNERS, 128), F32))
+    lax.fori_loop(0, PARTS // PACK_BLOCK, step, jnp.concatenate(starts, axis=0))
     for comp in range(5):
         high = acc[2 * comp * OWNERS : (2 * comp + 1) * OWNERS, :]
         low = acc[(2 * comp + 1) * OWNERS : (2 * comp + 2) * OWNERS, :]
@@ -136,99 +166,181 @@
 
 def pack(count, slab, cell, volume, drag):
     vmem = pl.BlockSpec(memory_space=pltpu.VMEM)
+    hbm = pl.BlockSpec(memory_space=pltpu.HBM)
     return pl.pallas_call(
         pack_kernel,
         out_shape=(
             jax.ShapeDtypeStruct((OWNERS * ROWS, 128), F32),
             jax.ShapeDtypeStruct((1, PARTS), F32),
         ),
-        in_specs=[pl.BlockSpec(memory_space=pltpu.SMEM), vmem, vmem, vmem, vmem],
+        in_specs=[pl.BlockSpec(memory_space=pltpu.SMEM), hbm, hbm, hbm, hbm],
         out_specs=(vmem, vmem),
-        scratch_shapes=[pltpu.VMEM((10 * OWNERS, CAP), F32)],
+        scratch_shapes=[
+            pltpu.VMEM((1, PARTS), I32),
+            pltpu.VMEM((1, PARTS), I32),
+            pltpu.VMEM((1, PARTS), F32),
+            pltpu.VMEM((3, 1, PARTS), F32),
+            pltpu.VMEM((10 * OWNERS, CAP), F32),
+            pltpu.SemaphoreType.DMA((4,)),
+        ],
+        compiler_params=pltpu.CompilerParams(vmem_limit_bytes=8 * MIB),
         name="pack",
-        compiler_params=pltpu.CompilerParams(vmem_limit_bytes=8 * MIB),
     )(count, slab, cell, volume, drag)
 
 
-SOURCES_AT_ONCE = 4
-
-
-def cell_split(cell):
-    cell = cell.astype(I32)
-    layer_x = lax.shift_right_logical(cell, 9)
-    layer = lax.shift_right_logical(cell, 13)
-    x = layer_x - layer * 16
-    y_half = lax.shift_right_logical(cell, 8) - layer_x * 2
-    high = (y_half * 16 + x) * 8 + layer
-    low = cell - lax.shift_right_logical(cell, 8) * 256
-    return high.astype(F32), low.astype(F32)
-
-
-def source_row(ref, source, comp):
-    base = source * ROWS + 2 * comp
-    return jnp.concatenate([ref[pl.ds(base, 1), :], ref[pl.ds(base + 1, 1), :]], axis=1)
-
-
-def deposit_kernel(recv_ref, solid_ref, drag_ref, out_ref, first_ref, last_ref):
-    out_ref[...] = jnp.zeros_like(out_ref)
+CHUNKS, CHUNK = 16, 1024
+CLASS_HIGH = 64
+TABLE_ROWS = 4 * HI
+
+
+def target_row(comp, side, block):
+    return (comp * 2 + side) * HI + block * LAYERS
+
+
+def swap_halves(first, second):
+    lane = lax.broadcasted_iota(I32, (8, 128), 1)
+    return (
+        jnp.where(lane < 64, first, pltpu.roll(second, 64, 1)),
+        jnp.where(lane < 64, pltpu.roll(first, 64, 1), second),
+    )
+
+
+def fill_low_hot(low_hot, low_ref, chunk):
+    for r in range(8):
+        low_hot[:, r * 128 : (r + 1) * 128] = one_hot(low_ref[chunk, r : r + 1, :], LO)
+
+
+def deposit_kernel(
+    recv_ref, solid_any, drag_any,
+    out_ref, first_ref, last_ref, prior_ref, high_ref, low_ref, bounds_ref,
+    solid_ref, drag_ref, values, acc, low_hot, left, spreads, sems,
+):
+    copies = [
+        pltpu.make_async_copy(solid_any, solid_ref, sems.at[0]),
+        pltpu.make_async_copy(drag_any, drag_ref, sems.at[1]),
+    ]
+    for copy in copies:
+        copy.start()
+    acc[...] = jnp.zeros_like(acc)
     zero = jnp.zeros((), BF16)
 
-    def step(block, carry):
-        lows, members, values = [], [], []
-        for sub in range(SOURCES_AT_ONCE):
-            source = block * SOURCES_AT_ONCE + sub
-            high, low = cell_split(source_row(recv_ref, source, 0))
-            lows.append(one_hot(low, LO))
-            members.append(row_is(high, HI))
-            parts = []
-            for comp in range(4):
-                value = source_row(recv_ref, source, comp + 1)
-                top = value.astype(BF16).astype(F32)
-                parts.append((top, value - top))
-            values.append(parts)
-        right = jnp.concatenate(lows, axis=1)
-        right2 = jnp.concatenate([right, right], axis=1)
+    def chunked(comp):
+        tile = jnp.concatenate([recv_ref[pl.ds(2 * comp + half, OWNERS, stride=ROWS), :] for half in range(2)], axis=0)
+        slots = jnp.transpose(tile)
+        pairs = [swap_halves(slots[16 * m : 16 * m + 8], slots[16 * m + 8 : 16 * m + 16]) for m in range(8)]
+        return [pair[0] for pair in pairs] + [pair[1] for pair in pairs]
+
+    volumes = chunked(1)
+    for chunk, cell in enumerate(chunked(0)):
+        cell = cell.astype(I32)
+        layer = lax.shift_right_logical(cell, 13)
+        layer_x = lax.shift_right_logical(cell, 9)
+        layer_xy = lax.shift_right_logical(cell, 8)
+        high = layer * 32 + (layer_xy - layer_x * 2) * 16 + layer_x - layer * 16
+        high_ref[chunk] = high.astype(F32)
+        low_ref[chunk] = (cell - layer_xy * 256).astype(F32)
+        values[0, chunk] = volumes[chunk]
+        live = volumes[chunk] > 0.0
+        kind = lax.shift_right_logical(layer, 1).astype(F32)
+        bounds_ref[chunk, 0] = jnp.min(jnp.where(live, kind, float(CLASSES))).astype(I32)
+        bounds_ref[chunk, 1] = jnp.max(jnp.where(live, kind, -1.0)).astype(I32) + 1
+    for comp in range(1, 4):
+        for chunk, value in enumerate(chunked(comp + 1)):
+            values[comp, chunk] = value
+
+    def step(chunk, carry):
+        fill_low_hot(low_hot, low_ref, chunk)
         for comp in range(4):
-            left = [
-                jnp.where(members[sub], spread(values[sub][comp][part], HI), zero)
-                for part in range(2)
-                for sub in range(SOURCES_AT_ONCE)
-            ]
-            out_ref[comp] += dot_nt(jnp.concatenate(left, axis=1), right2)
+            value = values[comp, chunk]
+            top = value.astype(BF16).astype(F32)
+            for part, piece in enumerate((top, value - top)):
+                for r in range(8):
+                    row = jnp.broadcast_to(piece[r : r + 1], (16, 128)).astype(BF16)
+                    spreads[comp, :, part * CHUNK + r * 128 : part * CHUNK + (r + 1) * 128] = row
+
+        def class_step(kind, carry):
+            key = high_ref[chunk] - (kind * CLASS_HIGH).astype(F32)
+            for r in range(8):
+                member = row_is(key[r : r + 1], CLASS_HIGH)
+                for comp in range(4):
+                    for part in range(2):
+                        lanes = slice(part * CHUNK + r * 128, part * CHUNK + (r + 1) * 128)
+                        value = spreads[comp, :, lanes]
+                        value = jnp.broadcast_to(value[None], (CLASS_HIGH // 16, 16, 128)).reshape(CLASS_HIGH, 128)
+                        picked = jnp.where(member, value, zero)
+                        for layer in range(2):
+                            left[pl.ds(layer * 128 + comp * 32, 32), lanes] = picked[layer * 32 : layer * 32 + 32]
+            spot = pl.ds(pl.multiple_of(kind * 256, 256), 256)
+            acc[spot, :] += dot_nt(left[:, 0:CHUNK], low_hot[...]) + dot_nt(left[:, CHUNK : 2 * CHUNK], low_hot[...])
+            return carry
+
+        lax.fori_loop(bounds_ref[chunk, 0], bounds_ref[chunk, 1], class_step, 0)
         return carry
 
-    lax.fori_loop(0, OWNERS // SOURCES_AT_ONCE, step, 0)
-    out_ref[0] = jnp.minimum(out_ref[0], PHI_LIMIT)
+    lax.fori_loop(0, CHUNKS, step, 0)
+    for copy in copies:
+        copy.wait()
+    for comp in range(4):
+        for layer in range(LAYERS):
+            rows = acc[pl.ds(layer * 128 + comp * 32, 32), :]
+            if comp == 0:
+                rows = jnp.minimum(rows, PHI_LIMIT)
+            for side in range(2):
+                spot = pl.ds(target_row(comp, side, 0) + layer, 32, stride=LAYERS)
+                out_ref[spot, :] = rows[:, side * 128 : (side + 1) * 128]
+        for x in range(CX):
+            row = comp * CX + x
+            prior_ref[row * LAYERS : (row + 1) * LAYERS, :] = prior_row(solid_ref, drag_ref, row, slice(None))
 
     def pieces(row):
         if row >= 4 * CX:
             row -= 4 * CX
-            return tuple(prior_row(solid_ref, drag_ref, row, pl.ds(at, 128)) for at in (0, CY - 128))
+            spot = slice(row * LAYERS, (row + 1) * LAYERS)
+            return prior_ref[spot, 0:128], prior_ref[spot, CY - 128 : CY]
         comp, x = row // CX, row % CX
-        first = out_ref[comp, x * LAYERS : (x + 1) * LAYERS, 0:128]
-        last = out_ref[comp, (CX + x) * LAYERS : (CX + x + 1) * LAYERS, LO - 128 : LO]
-        return first, last
+        at = target_row(comp, 0, x), target_row(comp, 1, CX + x)
+        return out_ref[at[0] : at[0] + LAYERS, :], out_ref[at[1] : at[1] + LAYERS, :]
 
     fold_sides(pieces, first_ref, last_ref)
 
 
 def deposit(received, solid, drag):
     vmem = pl.BlockSpec(memory_space=pltpu.VMEM)
+    hbm = pl.BlockSpec(memory_space=pltpu.HBM)
     side = jax.ShapeDtypeStruct((SIDE_ROWS, 128), F32)
+    index = jax.ShapeDtypeStruct((CHUNKS, 8, 128), F32)
     return pl.pallas_call(
         deposit_kernel,
-        out_shape=(jax.ShapeDtypeStruct((4, HI, LO), F32), side, side),
-        in_specs=[vmem] * 3,
-        out_specs=(vmem, vmem, vmem),
+        out_shape=(
+            jax.ShapeDtypeStruct((4 * 2 * HI, 128), F32),
+            side,
+            side,
+            jax.ShapeDtypeStruct((4 * CX * LAYERS, CY), F32),
+            index,
+            index,
+            jax.ShapeDtypeStruct((CHUNKS, 2), I32),
+        ),
+        in_specs=[vmem, hbm, hbm],
+        out_specs=(vmem,) * 6 + (pl.BlockSpec(memory_space=pltpu.SMEM),),
+        scratch_shapes=[
+            pltpu.VMEM((LAYERS, CX, CY), F32),
+            pltpu.VMEM((3, LAYERS, CX, CY), F32),
+            pltpu.VMEM((4, CHUNKS, 8, 128), F32),
+            pltpu.VMEM((TABLE_ROWS, LO), F32),
+            pltpu.VMEM((LO, CHUNK), BF16),
+            pltpu.VMEM((256, 2 * CHUNK), BF16),
+            pltpu.VMEM((4, 16, 2 * CHUNK), BF16),
+            pltpu.SemaphoreType.DMA((2,)),
+        ],
+        compiler_params=pltpu.CompilerParams(vmem_limit_bytes=16 * MIB),
         name="deposit",
-        compiler_params=pltpu.CompilerParams(vmem_limit_bytes=12 * MIB),
     )(received, solid, drag)
 
 
-GATHER_SOURCES = 2
-
-
-def gather_kernel(own_ref, above_ref, below_ref, recv_ref, fields_ref, out_ref, tops, bottoms):
+def gather_kernel(
+    bounds_ref, own_ref, above_ref, below_ref, high_ref, low_ref, fields_any, out_ref,
+    fields, table, tops, bottoms, low_hot, found, sem,
+):
     top, bottom = at_edge("span")
 
     def smooth(comp, x):
@@ -239,44 +351,65 @@
             row = row + jnp.where(bottom, 0.0, below_ref[pl.ds((comp * RIM + x - CX + RIM) * LAYERS, LAYERS), :])
         return row
 
-    for pair in range(0, CX, 2):
-        void = [1.0 - smooth(0, x) for x in (pair, pair + 1)]
+    for x in range(CX):
+        void = 1.0 - smooth(0, x)
         for comp in range(4):
-            rows = void if comp == 0 else [-smooth(comp, x) / v for x, v in zip((pair, pair + 1), void)]
-            for x, row in zip((pair, pair + 1), rows):
-                fields_ref[comp, :, x, :] = row
-            high, low = halves(jnp.concatenate(rows, axis=0))
+            row = void if comp == 0 else -smooth(comp, x) / void
+            fields[comp, :, x, :] = row
             for half in range(2):
-                spot = pl.ds((half * CX + pair) * LAYERS, 2 * LAYERS)
-                tops[comp, spot, :] = high[:, half * LO : (half + 1) * LO]
-                bottoms[comp, spot, :] = low[:, half * LO : (half + 1) * LO]
-
-    def step(block, carry):
-        highs, lows = [], []
-        for sub in range(GATHER_SOURCES):
-            high, low = cell_split(source_row(recv_ref, block * GATHER_SOURCES + sub, 0))
-            highs.append(high)
-            lows.append(one_hot(low, LO))
-        low_hot = jnp.concatenate(lows, axis=1)
-        high_row = jnp.concatenate(highs, axis=1)
-        n = high_row.shape[1]
-        member = lax.broadcasted_iota(I32, (HI, n), 0).astype(F32) == high_row
-        rows = []
+                for side in range(2):
+                    spot = pl.ds(side * TABLE_ROWS + comp * 32 + half * CX + x, LAYERS, stride=128)
+                    table[spot, :] = row[:, half * LO + side * 128 : half * LO + side * 128 + 128]
+    copy = pltpu.make_async_copy(fields, fields_any, sem)
+    copy.start()
+    for block in range(CLASSES):
+        spot = slice(block * 256, block * 256 + 256)
+        for side in range(2):
+            lanes = slice(side * 128, side * 128 + 128)
+            at = side * TABLE_ROWS + block * 256
+            tops[spot, lanes], bottoms[spot, lanes] = halves(table[at : at + 256, :])
+    ids = lax.broadcasted_iota(I32, (CLASS_HIGH, 128), 0).astype(F32)
+
+    def step(chunk, carry):
+        fill_low_hot(low_hot, low_ref, chunk)
+
+        def class_step(kind, sums):
+            key = high_ref[chunk] - (kind * CLASS_HIGH).astype(F32)
+            spot = pl.ds(pl.multiple_of(kind * 256, 256), 256)
+            value = dot_nn(tops[spot, :], low_hot[...]) + dot_nn(bottoms[spot, :], low_hot[...])
+            pieces = [[] for comp in range(4)]
+            for r in range(8):
+                member = ids == key[r : r + 1]
+                for comp in range(4):
+                    rows = [
+                        jnp.where(
+                            member[layer * 32 : layer * 32 + 32],
+                            value[layer * 128 + comp * 32 : layer * 128 + comp * 32 + 32, r * 128 : (r + 1) * 128],
+                            0.0,
+                        )
+                        for layer in range(2)
+                    ]
+                    pieces[comp].append(jnp.sum(rows[0] + rows[1], axis=0, keepdims=True))
+            return tuple(total + jnp.concatenate(piece, axis=0) for total, piece in zip(sums, pieces))
+
+        start = (jnp.zeros((8, 128), F32),) * 4
+        sums = lax.fori_loop(bounds_ref[chunk, 0], bounds_ref[chunk, 1], class_step, start)
         for comp in range(4):
-            value = dot_nn(tops[comp], low_hot) + dot_nn(bottoms[comp], low_hot)
-            rows.append(jnp.sum(jnp.where(member, value, 0.0), axis=0, keepdims=True))
-        for sub in range(GATHER_SOURCES):
-            pieces = [
-                row[:, sub * CAP + half * 128 : sub * CAP + (half + 1) * 128] for row in rows for half in range(2)
-            ]
-            start = pl.multiple_of((block * GATHER_SOURCES + sub) * BACK_ROWS, BACK_ROWS)
-            out_ref[pl.ds(start, BACK_ROWS), :] = jnp.concatenate(pieces, axis=0)
+            found[comp, chunk] = sums[comp]
         return carry
 
-    lax.fori_loop(0, OWNERS // GATHER_SOURCES, step, 0)
-
-
-def gather(own, above, below, received):
+    lax.fori_loop(0, CHUNKS, step, 0)
+    for comp in range(4):
+        slots = []
+        for m in range(8):
+            slots += swap_halves(found[comp, m], found[comp, m + 8])
+        tile = jnp.transpose(jnp.concatenate(slots, axis=0))
+        for half in range(2):
+            out_ref[pl.ds(2 * comp + half, OWNERS, stride=BACK_ROWS), :] = tile[half * OWNERS : (half + 1) * OWNERS]
+    copy.wait()
+
+
+def gather(bounds, *arrays):
     vmem = pl.BlockSpec(memory_space=pltpu.VMEM)
     return pl.pallas_call(
         gather_kernel,
@@ -284,12 +417,20 @@
             jax.ShapeDtypeStruct((4, LAYERS, CX, CY), F32),
             jax.ShapeDtypeStruct((OWNERS * BACK_ROWS, 128), F32),
         ),
-        in_specs=[vmem] * 4,
-        out_specs=(vmem, vmem),
-        scratch_shapes=[pltpu.VMEM((4, HI, LO), BF16)] * 2,
+        in_specs=[pl.BlockSpec(memory_space=pltpu.SMEM)] + [vmem] * 5,
+        out_specs=(pl.BlockSpec(memory_space=pltpu.HBM), vmem),
+        scratch_shapes=[
+            pltpu.VMEM((4, LAYERS, CX, CY), F32),
+            pltpu.VMEM((2 * TABLE_ROWS, 128), F32),
+            pltpu.VMEM((TABLE_ROWS, LO), BF16),
+            pltpu.VMEM((TABLE_ROWS, LO), BF16),
+            pltpu.VMEM((LO, CHUNK), BF16),
+            pltpu.VMEM((4, CHUNKS, 8, 128), F32),
+            pltpu.SemaphoreType.DMA,
+        ],
+        compiler_params=pltpu.CompilerParams(vmem_limit_bytes=16 * MIB),
         name="gather",
-        compiler_params=pltpu.CompilerParams(vmem_limit_bytes=16 * MIB),
-    )(own, above, below, received)
+    )(bounds, *arrays)
 
 
 PICK_BLOCK = 1024
@@ -338,7 +479,7 @@
 
 
 def relax_kernel(
-    target_ref, solid_ref, drag_ref, before, after, own_ref, up_ref, down_ref, state, source
+    target_ref, prior_ref, before, after, own_ref, up_ref, down_ref, state, source
 ):
     top, bottom = at_edge("span")
     first, last = at_edge("depth")
@@ -353,10 +494,11 @@
         for x in range(CX):
             row = comp * CX + x
             for half in range(2):
-                spot = pl.ds((half * CX + x) * LAYERS, LAYERS)
-                source[comp, x, :, half * LO : (half + 1) * LO] = target_ref[comp, spot, :]
+                for side in range(2):
+                    at, lanes = target_row(comp, side, half * CX + x), half * LO + side * 128
+                    source[comp, x, :, lanes : lanes + 128] = target_ref[at : at + LAYERS, :]
             source[comp, x, :, CY:WIDE] = unfold_side(row, before, after, is_before, is_after)
-            state[comp, RIM + x, :, 0:CY] = prior_row(solid_ref, drag_ref, row, slice(None))
+            state[comp, RIM + x, :, 0:CY] = prior_ref[row * LAYERS : (row + 1) * LAYERS, :]
             state[comp, RIM + x, :, CY:WIDE] = unfold_side(4 * CX + row, before, after, is_before, is_after)
 
     lane = lax.broadcasted_iota(I32, (LAYERS, WIDE), 1)
@@ -397,7 +539,7 @@
     return pl.pallas_call(
         relax_kernel,
         out_shape=(jax.ShapeDtypeStruct((4 * CX * LAYERS, CY), F32), rim, rim),
-        in_specs=[vmem] * 5,
+        in_specs=[vmem] * 4,
         out_specs=(vmem, vmem, vmem),
         scratch_shapes=[
             pltpu.VMEM((4, CX + 2 * RIM, LAYERS, WIDE), F32),
@@ -418,13 +560,13 @@
     sent, position = pack(part_count, slab, part_cell, part_volume, part_drag)
     received = lax.all_to_all(sent.reshape(OWNERS, 5, 2, 128), "span", 0, 0, tiled=True)
     received = received.reshape(OWNERS * ROWS, 128)
-    target, first, last = deposit(received, prior_solid, prior_drag)
+    target, first, last, prior, high, low, bounds = deposit(received, prior_solid, prior_drag)
     before = shifted(last, "depth", 1)
     after = shifted(first, "depth", -1)
-    own, up, down = relax(target, prior_solid, prior_drag, before, after)
+    own, up, down = relax(target, prior, before, after)
     from_above = shifted(down, "span", 1)
     from_below = shifted(up, "span", -1)
-    fields, returned = gather(own, from_above, from_below, received)
+    fields, returned = gather(bounds, own, from_above, from_below, high, low)
     back = lax.all_to_all(returned.reshape(OWNERS, BACK_ROWS, 128), "span", 0, 0, tiled=True)
     feedback = pick(part_count, slab, position, back.reshape(OWNERS * BACK_ROWS, 128))
     return fields, feedback

time: 130 us -> 115 us (0.88)
  Pallas kernels: 62.1 us -> 38.9 us
  blocking collectives: 47 us -> 52.1 us
  waiting for transfers between devices: 8.84 us -> 10.6 us
    pallas_call x1, Pallas kernels: 24.1 us -> 9.48 us  [gather(): pl.pallas_call(gather_kernel, out_shape=(jax.ShapeDtypeStruct((4, LAYERS,...]
    pallas_call x1, Pallas kernels: 21.2 us -> 9.64 us  [deposit(): pl.pallas_call(deposit_kernel, out_shape=(jax.ShapeDtypeStruct((4 * 2 * H...]
    all_to_all x1, blocking collectives: 20.8 us -> 25.9 us  [on_device(): lax.all_to_all(returned.reshape(OWNERS, BACK_ROWS, 128), 'span', 0, 0, ti...]
    pallas_call x1, Pallas kernels: 6.17 us -> 9.31 us  [pack(): pl.pallas_call(pack_kernel, out_shape=(jax.ShapeDtypeStruct((OWNERS * ROW...]
    ppermute x4, waiting for transfers between devices: 8.84 us -> 10.6 us  [shifted(): lax.ppermute(array, axis, [(i, (i + step) % count) for i in range(count)])]
    unnamed x16 -> x14, local copies, waits for them, and re-layouts: 4.12 us -> 4.12 us
where the time goes in v4:
time: 115 us; the launch traced here: 114 us
  blocking collectives  52.1 us (45%)
  Pallas kernels  38.9 us (34%)
  waiting for transfers between devices  10.6 us (9%)
  starting transfers between devices  6.69 us (6%)
  local copies, waits for them, and re-layouts  4.12 us (4%)
  between operations  1.42 us (1%)
    all_to_all x1, blocking collectives, on_device(): lax.all_to_all(sent.reshape(OWNERS, 5, 2, 128), 'span', 0, 0, tiled=True)  26.2 us
    all_to_all x1, blocking collectives, on_device(): lax.all_to_all(returned.reshape(OWNERS, BACK_ROWS, 128), 'span', 0, 0, ti...  25.9 us
    ppermute x4, waiting for transfers between devices, shifted(): lax.ppermute(array, axis, [(i, (i + step) % count) for i in range(count)])  10.6 us
    pallas_call x1, Pallas kernels, deposit(): pl.pallas_call(deposit_kernel, out_shape=(jax.ShapeDtypeStruct((4 * 2 * H...  9.64 us
    pallas_call x1, Pallas kernels, gather(): pl.pallas_call(gather_kernel, out_shape=(jax.ShapeDtypeStruct((4, LAYERS,...  9.48 us
    pallas_call x1, Pallas kernels, pack(): pl.pallas_call(pack_kernel, out_shape=(jax.ShapeDtypeStruct((OWNERS * ROW...  9.31 us
    ppermute x4, starting transfers between devices, shifted(): lax.ppermute(array, axis, [(i, (i + step) % count) for i in range(count)])  6.69 us
    pallas_call x1, Pallas kernels, relax(): pl.pallas_call(relax_kernel, out_shape=(jax.ShapeDtypeStruct((4 * CX * LA...  6.14 us
  transfers between devices with their start and end apart: 4, of which 3 were waited for; matrix products, arithmetic and copies ran while one was open for 0% of the time, Pallas kernels for 0%

profile of v4, /device:TPU:1, one launch (start us, length us, event | category | flops | bytes accessed | tf_op | source)
XLA Modules:
  0.0 113.9 jit_solution(12831717693800155213)
XLA Ops:
  0.6 0.0 copy-start
  1.4 0.0 copy-start.2
  1.4 0.7 copy-done.2
  2.1 0.0 copy-start.4
  2.1 0.9 copy-done.4
  3.0 0.0 copy-start.5
  3.0 0.8 copy-done.5
  3.8 0.0 copy-start.6
  3.8 0.8 copy-done.6
  4.5 9.3 %pack.1 = (f32[640,128]{1,0:T(8,128)S(1)}, f32[1,8192]{1,0:T(1,128)S(1)}) custom-call(s32[1,1]{1,0:T(1,128)S(6)} %copy.9.count_ref, s32[1,8192]{1,0:T(1,128)S(1)} %bitcast.9, s32[1,8192]{1,0:T(1,128)S(1)} %copy-done.5, f32[1,8192]{1,0:T(1,128)S(1)} %copy-done.6, f32[3,1,8192]{2,1,0:T(1,128)S(1)} %copy-done.4), custom_call_target="tpu_custom_call" | custom-call | tf_op jit(solution)/shard_map/pack/pallas_call | solution.py:170
  13.8 26.2 %all_to_all.10 = f32[64,5,2,128]{3,2,1,0:T(2,128)S(1)} all-to-all(f32[64,5,2,128]{3,2,1,0:T(2,128)S(1)} %bitcast.7), channel_id=1, replica_groups=mesh['span'=64,'depth'=4] {'span'}, dimensions={0} | all-to-all | bytes 655360 | tf_op jit(solution)/shard_map/all_to_all | solution.py:561
  40.1 0.0 copy-done
  40.1 0.0 copy-start.1
  40.1 0.9 copy-done.1
  41.0 9.6 %deposit.1 = (f32[2048,128]{1,0:T(8,128)S(1)}, f32[64,128]{1,0:T(8,128)S(1)}, f32[64,128]{1,0:T(8,128)S(1)}, f32[512,512]{1,0:T(8,128)S(1)}, f32[16,8,128]{2,1,0...) custom-call(f32[640,128]{1,0:T(8,128)S(1)} %bitcast.5, f32[8,16,512]{2,1,0:T(8,128)S(1)} %copy-done.1, ...), custom_call_target="tpu_custom_call" | custom-call | tf_op jit(solution)/shard_map/deposit/pallas_call | solution.py:312
  50.7 1.8 %collective-permute-start = (f32[64,128]{1,0:T(8,128)S(1)}, f32[64,128]{1,0:T(8,128)S(1)}, u32[]{:S(2)}, u32[]{:S(2)}) collective-permute-start(f32[64,128]{1,0:T(8,128)S(1)} %get-tuple-element.20), channel_id=1, source_target_pairs={{0,1},{1,2},{2,3},{3,0},{4,5},{5,6},{6,7},{7,4},{8,9},{9,10},{10,1... | collective-permute-start | bytes 98312 | tf_op jit(solution)/shard_map/ppermute | solution.py:555
  52.4 1.9 %collective-permute-start.1 = (f32[64,128]{1,0:T(8,128)S(1)}, f32[64,128]{1,0:T(8,128)S(1)}, u32[]{:S(2)}, u32[]{:S(2)}) collective-permute-start(f32[64,128]{1,0:T(8,128)S(1)} %get-tuple-element.21), channel_id=1, source_target_pairs={{0,3},{1,0},{2,1},{3,2},{4,7},{5,4},{6,5},{7,6},{8,11},{9,8},{10,9... | collective-permute-start | bytes 98312 | tf_op jit(solution)/shard_map/ppermute | solution.py:555
  54.3 1.8 %collective-permute-done.before = f32[64,128]{1,0:T(8,128)S(1)} collective-permute-done((f32[64,128]{1,0:T(8,128)S(1)}, f32[64,128]{1,0:T(8,128)S(1)}, u32[]{:S(2)}, u32[]{:S(2)}) %collective-permute-start) | collective-permute-done | bytes 32800 | tf_op jit(solution)/shard_map/ppermute | solution.py:555
  56.1 0.0 collective-permute-done.1.after
  56.1 6.1 %relax.1 = (f32[512,512]{1,0:T(8,128)S(1)}, f32[192,512]{1,0:T(8,128)S(1)}, f32[192,512]{1,0:T(8,128)S(1)}) custom-call(f32[2048,128]{1,0:T(8,128)S(1)} %get-tuple-element.18.target_ref, f32[512,512]{1,0:T(8,128)S(1)} %get-tuple-element.19.prior_ref, f32[64,128]{1,0:T(8,128)S(1)} %collective-permute-done.before, f32[64,128]{1,0:T(8,128)S(1)} %collective-permute-done.1.after), custom_call_target="tpu_custom_call" | custom-call | tf_op jit(solution)/shard_map/relax/pallas_call | solution.py:539
  62.2 3.0 %collective-permute-start.2 = (f32[192,512]{1,0:T(8,128)S(1)}, f32[192,512]{1,0:T(8,128)S(1)}, u32[]{:S(2)}, u32[]{:S(2)}) collective-permute-start(f32[192,512]{1,0:T(8,128)S(1)} %get-tuple-element.23), channel_id=1, source_target_pairs={{0,4},{4,8},{8,12},{12,16},{16,20},{20,24},{24,28},{28,32},{32,36}... | collective-permute-start | bytes 1179656 | tf_op jit(solution)/shard_map/ppermute | solution.py:555
  65.3 0.0 collective-permute-start.3
  65.3 4.7 %collective-permute-done.2.above_ref = f32[192,512]{1,0:T(8,128)S(1)} collective-permute-done((f32[192,512]{1,0:T(8,128)S(1)}, f32[192,512]{1,0:T(8,128)S(1)}, u32[]{:S(2)}, u32[]{:S(2)}) %collective-permute-start.2) | collective-permute-done | bytes 393248 | tf_op jit(solution)/shard_map/ppermute | solution.py:555
  70.0 4.1 %collective-permute-done.3.below_ref = f32[192,512]{1,0:T(8,128)S(1)} collective-permute-done((f32[192,512]{1,0:T(8,128)S(1)}, f32[192,512]{1,0:T(8,128)S(1)}, u32[]{:S(2)}, u32[]{:S(2)}) %collective-permute-start.3) | collective-permute-done | bytes 393248 | tf_op jit(solution)/shard_map/ppermute | solution.py:555
  74.1 9.5 %gather.1 = (f32[4,8,16,512]{3,2,1,0:T(8,128)}, f32[512,128]{1,0:T(8,128)S(1)}) custom-call(s32[16,2]{1,0:T(8,128)S(1)} %get-tuple-element.17.bounds_ref, f32[512,512]{1,0:T(8,128)S(1)} %get-tuple-element.22.own_ref, f32[192,512]{1,0:T(8,128)S(1)} %collective-permute-done.2.above_ref, f32[192,512]{1,0:T(8,128)S(1)} %collective-permute-done.3.below_ref, ...), custom_call_target="tpu_custom_call" | custom-call | tf_op jit(solution)/shard_map/gather/pallas_call | solution.py:414
  83.6 0.0 copy-start.3
  83.6 25.9 %all_to_all.11 = f32[64,8,128]{2,1,0:T(8,128)S(1)} all-to-all(f32[64,8,128]{2,1,0:T(8,128)S(1)} %bitcast.8), channel_id=1, replica_groups=mesh['span'=64,'depth'=4] {'span'}, dimensions={0} | all-to-all | bytes 524288 | tf_op jit(solution)/shard_map/all_to_all | solution.py:570
  109.5 0.0 copy-done.3
  109.5 4.4 %pick.1 = f32[4,1,8192]{2,1,0:T(1,128)} custom-call(s32[1,1]{1,0:T(1,128)S(6)} %copy.9.count_ref, s32[1,8192]{1,0:T(1,128)S(1)} %bitcast.10, f32[1,8192]{1,0:T(1,128)S(1)} %get-tuple-element.28.position_ref, f32[512,128]{1,0:T(8,128)S(1)} %bitcast.6), custom_call_target="tpu_custom_call" | custom-call | tf_op jit(solution)/shard_map/pick/pallas_call | solution.py:467
Async XLA Ops:
  0.6 39.4 %copy-start = (f32[3,8,16,512]{3,2,1,0:T(8,128)S(1)}, f32[3,8,16,512]{3,2,1,0:T(8,128)}, u32[]{:S(2)}) copy-start(f32[3,8,16,512]{3,2,1,0:T(8,128)} %drag_any.3) | copy-start | bytes 2359300
  1.4 0.8 copy-start.2
  2.1 0.9 copy-start.4
  3.0 0.8 copy-start.5
  3.8 0.8 copy-start.6
  40.1 1.0 copy-start.1
  50.7 5.4 %collective-permute-start = (f32[64,128]{1,0:T(8,128)S(1)}, f32[64,128]{1,0:T(8,128)S(1)}, u32[]{:S(2)}, u32[]{:S(2)}) collective-permute-start(f32[64,128]{1,0:T(8,128)S(1)} %get-tuple-element.20), channel_id=1, source_target_pairs={{0,1},{1,2},{2,3},{3,0},{4,5},{5,6},{6,7},{7,4},{8,9},{9,10},{10,1... | collective-permute-start | bytes 98312 | tf_op jit(solution)/shard_map/ppermute | solution.py:555
  52.4 3.6 %collective-permute-start.1 = (f32[64,128]{1,0:T(8,128)S(1)}, f32[64,128]{1,0:T(8,128)S(1)}, u32[]{:S(2)}, u32[]{:S(2)}) collective-permute-start(f32[64,128]{1,0:T(8,128)S(1)} %get-tuple-element.21), channel_id=1, source_target_pairs={{0,3},{1,0},{2,1},{3,2},{4,7},{5,4},{6,5},{7,6},{8,11},{9,8},{10,9... | collective-permute-start | bytes 98312 | tf_op jit(solution)/shard_map/ppermute | solution.py:555
  62.2 7.8 %collective-permute-start.2 = (f32[192,512]{1,0:T(8,128)S(1)}, f32[192,512]{1,0:T(8,128)S(1)}, u32[]{:S(2)}, u32[]{:S(2)}) collective-permute-start(f32[192,512]{1,0:T(8,128)S(1)} %get-tuple-element.23), channel_id=1, source_target_pairs={{0,4},{4,8},{8,12},{12,16},{16,20},{20,24},{24,28},{28,32},{32,36}... | collective-permute-start | bytes 1179656 | tf_op jit(solution)/shard_map/ppermute | solution.py:555
  65.3 8.8 %collective-permute-start.3 = (f32[192,512]{1,0:T(8,128)S(1)}, f32[192,512]{1,0:T(8,128)S(1)}, u32[]{:S(2)}, u32[]{:S(2)}) collective-permute-start(f32[192,512]{1,0:T(8,128)S(1)} %get-tuple-element.24), channel_id=1, source_target_pairs={{0,252},{4,0},{8,4},{12,8},{16,12},{20,16},{24,20},{28,24},{32,28}... | collective-permute-start | bytes 1179656 | tf_op jit(solution)/shard_map/ppermute | solution.py:555
  83.6 25.9 %copy-start.3 = (s32[1,8192,1]{1,2,0:T(1,128)S(1)}, s32[1,8192,1]{1,2,0:T(1,128)}, u32[]{:S(2)}) copy-start(s32[1,8192,1]{1,2,0:T(1,128)} %param.7) | copy-start | bytes 98308

commit v5 on v4

--- a/solution.py
+++ b/solution.py
@@ -1,3 +1,5 @@
+import functools
+
 import jax
 import jax.numpy as jnp
 from jax import lax
@@ -16,6 +18,7 @@
 BACK_ROWS = 8
 SWEEPS = 6
 RIM = SWEEPS
+GROUPS, GROUP = 2, 2
 SIDE_ROWS = 2 * 4 * CX // 16 * LAYERS
 PHI_LIMIT = 0.6
 
@@ -112,7 +115,8 @@
         return jnp.where(lane < count, slab_ref[0:1, pl.ds(start, size)], CLASSES * OWNERS)
 
     def classes(start, size):
-        return lax.shift_right_logical(cell_ref[0:1, pl.ds(start, size)], 14)
+        cell = cell_ref[0:1, pl.ds(start, size)]
+        return (lax.shift_right_logical(cell, 8) & 1) * 2 + (lax.shift_right_logical(cell, 12) & 1)
 
     def count_step(block, counts):
         start = pl.multiple_of(block * PACK_BLOCK, PACK_BLOCK)
@@ -189,12 +193,7 @@
 
 
 CHUNKS, CHUNK = 16, 1024
-CLASS_HIGH = 64
-TABLE_ROWS = 4 * HI
-
-
-def target_row(comp, side, block):
-    return (comp * 2 + side) * HI + block * LAYERS
+CLASS_HIGH = HI // CLASSES
 
 
 def swap_halves(first, second):
@@ -205,15 +204,14 @@
     )
 
 
-def fill_low_hot(low_hot, low_ref, chunk):
-    for r in range(8):
-        low_hot[:, r * 128 : (r + 1) * 128] = one_hot(low_ref[chunk, r : r + 1, :], LO)
+def low_hots(low_ref, chunk):
+    return jnp.concatenate([one_hot(low_ref[chunk, r : r + 1, :], LO) for r in range(8)], axis=1)
 
 
 def deposit_kernel(
     recv_ref, solid_any, drag_any,
     out_ref, first_ref, last_ref, prior_ref, high_ref, low_ref, bounds_ref,
-    solid_ref, drag_ref, values, acc, low_hot, left, spreads, sems,
+    solid_ref, drag_ref, values, sems,
 ):
     copies = [
         pltpu.make_async_copy(solid_any, solid_ref, sems.at[0]),
@@ -221,7 +219,7 @@
     ]
     for copy in copies:
         copy.start()
-    acc[...] = jnp.zeros_like(acc)
+    out_ref[...] = jnp.zeros_like(out_ref)
     zero = jnp.zeros((), BF16)
 
     def chunked(comp):
@@ -234,14 +232,12 @@
     for chunk, cell in enumerate(chunked(0)):
         cell = cell.astype(I32)
         layer = lax.shift_right_logical(cell, 13)
-        layer_x = lax.shift_right_logical(cell, 9)
-        layer_xy = lax.shift_right_logical(cell, 8)
-        high = layer * 32 + (layer_xy - layer_x * 2) * 16 + layer_x - layer * 16
+        high = ((lax.shift_right_logical(cell, 8) & 1) * 16 + (lax.shift_right_logical(cell, 9) & 15)) * 8 + layer
         high_ref[chunk] = high.astype(F32)
-        low_ref[chunk] = (cell - layer_xy * 256).astype(F32)
+        low_ref[chunk] = (cell & 255).astype(F32)
         values[0, chunk] = volumes[chunk]
         live = volumes[chunk] > 0.0
-        kind = lax.shift_right_logical(layer, 1).astype(F32)
+        kind = lax.shift_right_logical(high, 6).astype(F32)
         bounds_ref[chunk, 0] = jnp.min(jnp.where(live, kind, float(CLASSES))).astype(I32)
         bounds_ref[chunk, 1] = jnp.max(jnp.where(live, kind, -1.0)).astype(I32) + 1
     for comp in range(1, 4):
@@ -249,48 +245,38 @@
             values[comp, chunk] = value
 
     def step(chunk, carry):
-        fill_low_hot(low_hot, low_ref, chunk)
-        for comp in range(4):
-            value = values[comp, chunk]
-            top = value.astype(BF16).astype(F32)
-            for part, piece in enumerate((top, value - top)):
-                for r in range(8):
-                    row = jnp.broadcast_to(piece[r : r + 1], (16, 128)).astype(BF16)
-                    spreads[comp, :, part * CHUNK + r * 128 : part * CHUNK + (r + 1) * 128] = row
-
         def class_step(kind, carry):
             key = high_ref[chunk] - (kind * CLASS_HIGH).astype(F32)
-            for r in range(8):
-                member = row_is(key[r : r + 1], CLASS_HIGH)
-                for comp in range(4):
-                    for part in range(2):
-                        lanes = slice(part * CHUNK + r * 128, part * CHUNK + (r + 1) * 128)
-                        value = spreads[comp, :, lanes]
-                        value = jnp.broadcast_to(value[None], (CLASS_HIGH // 16, 16, 128)).reshape(CLASS_HIGH, 128)
-                        picked = jnp.where(member, value, zero)
-                        for layer in range(2):
-                            left[pl.ds(layer * 128 + comp * 32, 32), lanes] = picked[layer * 32 : layer * 32 + 32]
-            spot = pl.ds(pl.multiple_of(kind * 256, 256), 256)
-            acc[spot, :] += dot_nt(left[:, 0:CHUNK], low_hot[...]) + dot_nt(left[:, CHUNK : 2 * CHUNK], low_hot[...])
+            members = [row_is(key[r : r + 1], CLASS_HIGH) for r in range(8)]
+            lows = low_hots(low_ref, chunk)
+            left = []
+            for comp in range(4):
+                value = values[comp, chunk]
+                top = value.astype(BF16).astype(F32)
+                left.append(
+                    jnp.concatenate(
+                        [
+                            jnp.where(members[r], spread(piece[r : r + 1], CLASS_HIGH), zero)
+                            for piece in (top, value - top)
+                            for r in range(8)
+                        ],
+                        axis=1,
+                    )
+                )
+            total = dot_nt(jnp.concatenate(left, axis=0), jnp.concatenate([lows, lows], axis=1))
+            spot = pl.ds(pl.multiple_of(kind * CLASS_HIGH, CLASS_HIGH), CLASS_HIGH)
+            for comp in range(4):
+                out_ref[comp, spot, :] += total[comp * CLASS_HIGH : (comp + 1) * CLASS_HIGH, :]
             return carry
 
-        lax.fori_loop(bounds_ref[chunk, 0], bounds_ref[chunk, 1], class_step, 0)
-        return carry
+        return lax.fori_loop(bounds_ref[chunk, 0], bounds_ref[chunk, 1], class_step, carry)
 
     lax.fori_loop(0, CHUNKS, step, 0)
+    out_ref[0] = jnp.minimum(out_ref[0], PHI_LIMIT)
     for copy in copies:
         copy.wait()
-    for comp in range(4):
-        for layer in range(LAYERS):
-            rows = acc[pl.ds(layer * 128 + comp * 32, 32), :]
-            if comp == 0:
-                rows = jnp.minimum(rows, PHI_LIMIT)
-            for side in range(2):
-                spot = pl.ds(target_row(comp, side, 0) + layer, 32, stride=LAYERS)
-                out_ref[spot, :] = rows[:, side * 128 : (side + 1) * 128]
-        for x in range(CX):
-            row = comp * CX + x
-            prior_ref[row * LAYERS : (row + 1) * LAYERS, :] = prior_row(solid_ref, drag_ref, row, slice(None))
+    for row in range(4 * CX):
+        prior_ref[row * LAYERS : (row + 1) * LAYERS, :] = prior_row(solid_ref, drag_ref, row, slice(None))
 
     def pieces(row):
         if row >= 4 * CX:
@@ -298,8 +284,9 @@
             spot = slice(row * LAYERS, (row + 1) * LAYERS)
             return prior_ref[spot, 0:128], prior_ref[spot, CY - 128 : CY]
         comp, x = row // CX, row % CX
-        at = target_row(comp, 0, x), target_row(comp, 1, CX + x)
-        return out_ref[at[0] : at[0] + LAYERS, :], out_ref[at[1] : at[1] + LAYERS, :]
+        first = out_ref[comp, x * LAYERS : (x + 1) * LAYERS, 0:128]
+        last = out_ref[comp, (CX + x) * LAYERS : (CX + x + 1) * LAYERS, LO - 128 : LO]
+        return first, last
 
     fold_sides(pieces, first_ref, last_ref)
 
@@ -312,7 +299,7 @@
     return pl.pallas_call(
         deposit_kernel,
         out_shape=(
-            jax.ShapeDtypeStruct((4 * 2 * HI, 128), F32),
+            jax.ShapeDtypeStruct((4, HI, LO), F32),
             side,
             side,
             jax.ShapeDtypeStruct((4 * CX * LAYERS, CY), F32),
@@ -326,10 +313,6 @@
             pltpu.VMEM((LAYERS, CX, CY), F32),
             pltpu.VMEM((3, LAYERS, CX, CY), F32),
             pltpu.VMEM((4, CHUNKS, 8, 128), F32),
-            pltpu.VMEM((TABLE_ROWS, LO), F32),
-            pltpu.VMEM((LO, CHUNK), BF16),
-            pltpu.VMEM((256, 2 * CHUNK), BF16),
-            pltpu.VMEM((4, 16, 2 * CHUNK), BF16),
             pltpu.SemaphoreType.DMA((2,)),
         ],
         compiler_params=pltpu.CompilerParams(vmem_limit_bytes=16 * MIB),
@@ -337,60 +320,54 @@
     )(received, solid, drag)
 
 
-def gather_kernel(
-    bounds_ref, own_ref, above_ref, below_ref, high_ref, low_ref, fields_any, out_ref,
-    fields, table, tops, bottoms, low_hot, found, sem,
-):
+def gather_kernel(bounds_ref, *refs):
+    own_refs, above_refs, below_refs = refs[0:GROUPS], refs[GROUPS : 2 * GROUPS], refs[2 * GROUPS : 3 * GROUPS]
+    high_ref, low_ref, fields_any, out_ref, fields, tops, bottoms, found, sem = refs[3 * GROUPS :]
     top, bottom = at_edge("span")
 
     def smooth(comp, x):
-        row = own_ref[pl.ds((comp * CX + x) * LAYERS, LAYERS), :]
+        group, comp = comp // GROUP, comp % GROUP
+        row = own_refs[group][pl.ds((comp * CX + x) * LAYERS, LAYERS), :]
         if x < RIM:
-            row = row + jnp.where(top, 0.0, above_ref[pl.ds((comp * RIM + x) * LAYERS, LAYERS), :])
+            spot = pl.ds((comp * RIM + x) * LAYERS, LAYERS)
+            row = row + jnp.where(top, 0.0, above_refs[group][spot, :])
         if x >= CX - RIM:
-            row = row + jnp.where(bottom, 0.0, below_ref[pl.ds((comp * RIM + x - CX + RIM) * LAYERS, LAYERS), :])
+            spot = pl.ds((comp * RIM + x - CX + RIM) * LAYERS, LAYERS)
+            row = row + jnp.where(bottom, 0.0, below_refs[group][spot, :])
         return row
 
-    for x in range(CX):
-        void = 1.0 - smooth(0, x)
+    for pair in range(0, CX, 2):
+        void = [1.0 - smooth(0, x) for x in (pair, pair + 1)]
         for comp in range(4):
-            row = void if comp == 0 else -smooth(comp, x) / void
-            fields[comp, :, x, :] = row
+            rows = void if comp == 0 else [-smooth(comp, x) / v for x, v in zip((pair, pair + 1), void)]
+            for x, row in zip((pair, pair + 1), rows):
+                fields[comp, :, x, :] = row
+            high, low = halves(jnp.concatenate(rows, axis=0))
             for half in range(2):
-                for side in range(2):
-                    spot = pl.ds(side * TABLE_ROWS + comp * 32 + half * CX + x, LAYERS, stride=128)
-                    table[spot, :] = row[:, half * LO + side * 128 : half * LO + side * 128 + 128]
+                spot = pl.ds((half * CX + pair) * LAYERS, 2 * LAYERS)
+                tops[comp, spot, :] = high[:, half * LO : (half + 1) * LO]
+                bottoms[comp, spot, :] = low[:, half * LO : (half + 1) * LO]
     copy = pltpu.make_async_copy(fields, fields_any, sem)
     copy.start()
-    for block in range(CLASSES):
-        spot = slice(block * 256, block * 256 + 256)
-        for side in range(2):
-            lanes = slice(side * 128, side * 128 + 128)
-            at = side * TABLE_ROWS + block * 256
-            tops[spot, lanes], bottoms[spot, lanes] = halves(table[at : at + 256, :])
     ids = lax.broadcasted_iota(I32, (CLASS_HIGH, 128), 0).astype(F32)
 
     def step(chunk, carry):
-        fill_low_hot(low_hot, low_ref, chunk)
-
         def class_step(kind, sums):
             key = high_ref[chunk] - (kind * CLASS_HIGH).astype(F32)
-            spot = pl.ds(pl.multiple_of(kind * 256, 256), 256)
-            value = dot_nn(tops[spot, :], low_hot[...]) + dot_nn(bottoms[spot, :], low_hot[...])
-            pieces = [[] for comp in range(4)]
-            for r in range(8):
-                member = ids == key[r : r + 1]
-                for comp in range(4):
-                    rows = [
-                        jnp.where(
-                            member[layer * 32 : layer * 32 + 32],
-                            value[layer * 128 + comp * 32 : layer * 128 + comp * 32 + 32, r * 128 : (r + 1) * 128],
-                            0.0,
-                        )
-                        for layer in range(2)
-                    ]
-                    pieces[comp].append(jnp.sum(rows[0] + rows[1], axis=0, keepdims=True))
-            return tuple(total + jnp.concatenate(piece, axis=0) for total, piece in zip(sums, pieces))
+            lows = low_hots(low_ref, chunk)
+            spot = pl.ds(pl.multiple_of(kind * CLASS_HIGH, CLASS_HIGH), CLASS_HIGH)
+            members = [ids == key[r : r + 1] for r in range(8)]
+            table = [jnp.concatenate([part[comp, spot, :] for comp in range(4)], axis=0) for part in (tops, bottoms)]
+            value = dot_nn(table[0], lows) + dot_nn(table[1], lows)
+            new = []
+            for comp in range(4):
+                rows = value[comp * CLASS_HIGH : (comp + 1) * CLASS_HIGH]
+                pieces = [
+                    jnp.sum(jnp.where(members[r], rows[:, r * 128 : (r + 1) * 128], 0.0), axis=0, keepdims=True)
+                    for r in range(8)
+                ]
+                new.append(sums[comp] + jnp.concatenate(pieces, axis=0))
+            return tuple(new)
 
         start = (jnp.zeros((8, 128), F32),) * 4
         sums = lax.fori_loop(bounds_ref[chunk, 0], bounds_ref[chunk, 1], class_step, start)
@@ -409,7 +386,7 @@
     copy.wait()
 
 
-def gather(bounds, *arrays):
+def gather(bounds, owns, aboves, belows, high, low):
     vmem = pl.BlockSpec(memory_space=pltpu.VMEM)
     return pl.pallas_call(
         gather_kernel,
@@ -417,20 +394,18 @@
             jax.ShapeDtypeStruct((4, LAYERS, CX, CY), F32),
             jax.ShapeDtypeStruct((OWNERS * BACK_ROWS, 128), F32),
         ),
-        in_specs=[pl.BlockSpec(memory_space=pltpu.SMEM)] + [vmem] * 5,
+        in_specs=[pl.BlockSpec(memory_space=pltpu.SMEM)] + [vmem] * (3 * GROUPS + 2),
         out_specs=(pl.BlockSpec(memory_space=pltpu.HBM), vmem),
         scratch_shapes=[
             pltpu.VMEM((4, LAYERS, CX, CY), F32),
-            pltpu.VMEM((2 * TABLE_ROWS, 128), F32),
-            pltpu.VMEM((TABLE_ROWS, LO), BF16),
-            pltpu.VMEM((TABLE_ROWS, LO), BF16),
-            pltpu.VMEM((LO, CHUNK), BF16),
+            pltpu.VMEM((4, HI, LO), BF16),
+            pltpu.VMEM((4, HI, LO), BF16),
             pltpu.VMEM((4, CHUNKS, 8, 128), F32),
             pltpu.SemaphoreType.DMA,
         ],
         compiler_params=pltpu.CompilerParams(vmem_limit_bytes=16 * MIB),
         name="gather",
-    )(bounds, *arrays)
+    )(bounds, *owns, *aboves, *belows, high, low)
 
 
 PICK_BLOCK = 1024
@@ -476,10 +451,11 @@
 
 
 WIDE = CY + 128
+RELAX_FLOPS = 40_000_000
 
 
 def relax_kernel(
-    target_ref, prior_ref, before, after, own_ref, up_ref, down_ref, state, source
+    base, target_ref, prior_ref, before, after, own_ref, up_ref, down_ref, state, source
 ):
     top, bottom = at_edge("span")
     first, last = at_edge("depth")
@@ -487,16 +463,15 @@
     is_before = (near >= 120) & jnp.logical_not(first)
     is_after = (near < 8) & jnp.logical_not(last)
     blank = jnp.zeros((LAYERS, WIDE), F32)
-    for comp in range(4):
+    for comp in range(GROUP):
         for x in range(RIM):
             state[comp, x] = blank
             state[comp, RIM + CX + x] = blank
         for x in range(CX):
-            row = comp * CX + x
+            row = (base + comp) * CX + x
             for half in range(2):
-                for side in range(2):
-                    at, lanes = target_row(comp, side, half * CX + x), half * LO + side * 128
-                    source[comp, x, :, lanes : lanes + 128] = target_ref[at : at + LAYERS, :]
+                spot = pl.ds((half * CX + x) * LAYERS, LAYERS)
+                source[comp, x, :, half * LO : (half + 1) * LO] = target_ref[base + comp, spot, :]
             source[comp, x, :, CY:WIDE] = unfold_side(row, before, after, is_before, is_after)
             state[comp, RIM + x, :, 0:CY] = prior_ref[row * LAYERS : (row + 1) * LAYERS, :]
             state[comp, RIM + x, :, CY:WIDE] = unfold_side(4 * CX + row, before, after, is_before, is_after)
@@ -523,8 +498,8 @@
                 above, here = here, below
         return carry
 
-    lax.fori_loop(0, 4, comp_step, 0)
-    for comp in range(4):
+    lax.fori_loop(0, GROUP, comp_step, 0)
+    for comp in range(GROUP):
         for x in range(CX):
             own_ref[pl.ds((comp * CX + x) * LAYERS, LAYERS), :] = state[comp, RIM + x, :, 0:CY]
         for x in range(RIM):
@@ -533,20 +508,21 @@
             down_ref[spot, :] = state[comp, RIM + CX + x, :, 0:CY]
 
 
-def relax(*arrays):
+def relax(base, *arrays):
     vmem = pl.BlockSpec(memory_space=pltpu.VMEM)
-    rim = jax.ShapeDtypeStruct((4 * RIM * LAYERS, CY), F32)
+    rim = jax.ShapeDtypeStruct((GROUP * RIM * LAYERS, CY), F32)
     return pl.pallas_call(
-        relax_kernel,
-        out_shape=(jax.ShapeDtypeStruct((4 * CX * LAYERS, CY), F32), rim, rim),
+        functools.partial(relax_kernel, base),
+        out_shape=(jax.ShapeDtypeStruct((GROUP * CX * LAYERS, CY), F32), rim, rim),
         in_specs=[vmem] * 4,
         out_specs=(vmem, vmem, vmem),
         scratch_shapes=[
-            pltpu.VMEM((4, CX + 2 * RIM, LAYERS, WIDE), F32),
-            pltpu.VMEM((4, CX, LAYERS, WIDE), F32),
+            pltpu.VMEM((GROUP, CX + 2 * RIM, LAYERS, WIDE), F32),
+            pltpu.VMEM((GROUP, CX, LAYERS, WIDE), F32),
         ],
-        name="relax",
-        compiler_params=pltpu.CompilerParams(vmem_limit_bytes=16 * MIB),
+        compiler_params=pltpu.CompilerParams(vmem_limit_bytes=12 * MIB),
+        cost_estimate=pl.CostEstimate(flops=RELAX_FLOPS, bytes_accessed=4 * MIB, transcendentals=0),
+        name=f"relax_{base}",
     )(*arrays)
 
 
@@ -557,16 +533,22 @@
 
 def on_device(part_slab, part_cell, part_volume, part_drag, part_count, prior_solid, prior_drag):
     slab = part_slab.reshape(1, PARTS)
-    sent, position = pack(part_count, slab, part_cell, part_volume, part_drag)
+    in_hbm = [pltpu.with_memory_space_constraint(a, pltpu.HBM) for a in (slab, part_cell, part_volume, part_drag)]
+    sent, position = pack(part_count, *in_hbm)
     received = lax.all_to_all(sent.reshape(OWNERS, 5, 2, 128), "span", 0, 0, tiled=True)
     received = received.reshape(OWNERS * ROWS, 128)
-    target, first, last, prior, high, low, bounds = deposit(received, prior_solid, prior_drag)
+    target, first, last, prior, high, low, bounds = deposit(
+        received, *[pltpu.with_memory_space_constraint(a, pltpu.HBM) for a in (prior_solid, prior_drag)]
+    )
     before = shifted(last, "depth", 1)
     after = shifted(first, "depth", -1)
-    own, up, down = relax(target, prior, before, after)
-    from_above = shifted(down, "span", 1)
-    from_below = shifted(up, "span", -1)
-    fields, returned = gather(bounds, own, from_above, from_below, high, low)
+    owns, aboves, belows = [], [], []
+    for group in range(GROUPS):
+        own, up, down = relax(group * GROUP, target, prior, before, after)
+        owns.append(own)
+        aboves.append(shifted(down, "span", 1))
+        belows.append(shifted(up, "span", -1))
+    fields, returned = gather(bounds, owns, aboves, belows, high, low)
     back = lax.all_to_all(returned.reshape(OWNERS, BACK_ROWS, 128), "span", 0, 0, tiled=True)
     feedback = pick(part_count, slab, position, back.reshape(OWNERS * BACK_ROWS, 128))
     return fields, feedback

time: 115 us -> 109 us (0.948)
  waiting for transfers between devices: 10.6 us -> 3.38 us
  starting transfers between devices: 6.69 us -> 13.6 us
  local copies, waits for them, and re-layouts: 4.12 us -> 0.01 us
  Pallas kernels: 38.9 us -> 34.9 us
  blocking collectives: 52.1 us -> 53.5 us
    ppermute x4 -> x6, waiting for transfers between devices: 10.6 us -> 3.38 us  [shifted(): lax.ppermute(array, axis, [(i, (i + step) % count) for i in range(count)])]
    ppermute x4 -> x6, starting transfers between devices: 6.69 us -> 13.6 us  [shifted(): lax.ppermute(array, axis, [(i, (i + step) % count) for i in range(count)])]
    unnamed x14 -> x2, local copies, waits for them, and re-layouts: 4.12 us -> 0.01 us
    pallas_call x1, Pallas kernels: 9.48 us -> 6.96 us  [gather(): pl.pallas_call(gather_kernel, out_shape=(jax.ShapeDtypeStruct((4, LAYERS,...]
    pallas_call x2 -> x3, Pallas kernels: 15.8 us -> 13.6 us  [the longest x1 7.48 us: deposit(): pl.pallas_call(deposit_kernel, out_shape=(jax.ShapeDtypeStruct((4, HI, LO...]
    all_to_all x1, blocking collectives: 25.9 us -> 27.3 us  [on_device(): lax.all_to_all(returned.reshape(OWNERS, BACK_ROWS, 128), 'span', 0, 0, ti...]
  transfers between devices with their start and end apart: 4 -> 6, of which waited for: 3 -> 4; matrix products, arithmetic and copies ran while one was open for 0% -> 0% of each run, Pallas kernels for 0% -> 3%
where the time goes in v5:
time: 109 us; the launch traced here: 107 us
  blocking collectives  53.5 us (49%)
  Pallas kernels  34.9 us (32%)
  starting transfers between devices  13.6 us (12%)
  waiting for transfers between devices  3.38 us (3%)
  between operations  1.34 us (1%)
    all_to_all x1, blocking collectives, on_device(): lax.all_to_all(returned.reshape(OWNERS, BACK_ROWS, 128), 'span', 0, 0, ti...  27.3 us
    all_to_all x1, blocking collectives, on_device(): lax.all_to_all(sent.reshape(OWNERS, 5, 2, 128), 'span', 0, 0, tiled=True)  26.2 us
    ppermute x6, starting transfers between devices, shifted(): lax.ppermute(array, axis, [(i, (i + step) % count) for i in range(count)])  13.6 us
    pallas_call x1, Pallas kernels, pack(): pl.pallas_call(pack_kernel, out_shape=(jax.ShapeDtypeStruct((OWNERS * ROW...  10 us
    pallas_call x1, Pallas kernels, deposit(): pl.pallas_call(deposit_kernel, out_shape=(jax.ShapeDtypeStruct((4, HI, LO...  7.48 us
    pallas_call x1, Pallas kernels, gather(): pl.pallas_call(gather_kernel, out_shape=(jax.ShapeDtypeStruct((4, LAYERS,...  6.96 us
    pallas_call x2, Pallas kernels, relax(): pl.pallas_call(functools.partial(relax_kernel, base), out_shape=(jax.Shap...  6.13 us
    pallas_call x1, Pallas kernels, pick(): pl.pallas_call(pick_kernel, out_shape=jax.ShapeDtypeStruct((4, 1, PARTS),...  4.37 us
  transfers between devices with their start and end apart: 6, of which 4 were waited for; matrix products, arithmetic and copies ran while one was open for 0% of the time, Pallas kernels for 3%

profile of v5, /device:TPU:1, one launch (start us, length us, event | category | flops | bytes accessed | tf_op | source)
XLA Modules:
  0.0 106.7 jit_solution(7425578846603212096)
XLA Ops:
  1.3 10.0 %pack.1 = (f32[640,128]{1,0:T(8,128)S(1)}, f32[1,8192]{1,0:T(1,128)S(1)}) custom-call(s32[1,1]{1,0:T(1,128)S(6)} %copy.9.count_ref, s32[1,8192]{1,0:T(1,128)} %bitcast.9, s32[1,8192]{1,0:T(1,128)} %cell_any.1, f32[1,8192]{1,0:T(1,128)} %volume_any.1, f32[3,1,8192]{2,1,0:T(1,128)} %drag_any.2), custom_call_target="tpu_custom_call" | custom-call | tf_op jit(solution)/shard_map/pack/pallas_call | solution.py:174
  11.3 26.2 %all_to_all.10 = f32[64,5,2,128]{3,2,1,0:T(2,128)S(1)} all-to-all(f32[64,5,2,128]{3,2,1,0:T(2,128)S(1)} %bitcast.7), channel_id=1, replica_groups=mesh['span'=64,'depth'=4] {'span'}, dimensions={0} | all-to-all | bytes 655360 | tf_op jit(solution)/shard_map/all_to_all | solution.py:538
  37.5 7.5 %deposit.1 = (f32[4,256,256]{2,1,0:T(8,128)S(1)}, f32[64,128]{1,0:T(8,128)S(1)}, f32[64,128]{1,0:T(8,128)S(1)}, f32[512,512]{1,0:T(8,128)S(1)}, f32[16,8,128]{2,...) custom-call(f32[640,128]{1,0:T(8,128)S(1)} %bitcast.5, f32[8,16,512]{2,1,0:T(8,128)} %solid_any.1, ...), custom_call_target="tpu_custom_call" | custom-call | tf_op jit(solution)/shard_map/deposit/pallas_call | solution.py:299
  45.0 2.7 %collective-permute-start = (f32[64,128]{1,0:T(8,128)S(1)}, f32[64,128]{1,0:T(8,128)S(1)}, u32[]{:S(2)}, u32[]{:S(2)}) collective-permute-start(f32[64,128]{1,0:T(8,128)S(1)} %get-tuple-element.23), channel_id=1, source_target_pairs={{0,1},{1,2},{2,3},{3,0},{4,5},{5,6},{6,7},{7,4},{8,9},{9,10},{10,1... | collective-permute-start | bytes 98312 | tf_op jit(solution)/shard_map/ppermute | solution.py:531
  47.7 0.5 collective-permute-start.1
  48.1 1.2 %collective-permute-done.before = f32[64,128]{1,0:T(8,128)S(1)} collective-permute-done((f32[64,128]{1,0:T(8,128)S(1)}, f32[64,128]{1,0:T(8,128)S(1)}, u32[]{:S(2)}, u32[]{:S(2)}) %collective-permute-start) | collective-permute-done | bytes 32800 | tf_op jit(solution)/shard_map/ppermute | solution.py:531
  49.3 1.1 %collective-permute-done.1.after = f32[64,128]{1,0:T(8,128)S(1)} collective-permute-done((f32[64,128]{1,0:T(8,128)S(1)}, f32[64,128]{1,0:T(8,128)S(1)}, u32[]{:S(2)}, u32[]{:S(2)}) %collective-permute-start.1) | collective-permute-done | bytes 32800 | tf_op jit(solution)/shard_map/ppermute | solution.py:531
  50.4 3.1 %relax_2.1 = (f32[256,512]{1,0:T(8,128)S(1)}, f32[96,512]{1,0:T(8,128)S(1)}, f32[96,512]{1,0:T(8,128)S(1)}) custom-call(f32[4,256,256]{2,1,0:T(8,128)S(1)} %get-tuple-element.21.target_ref, f32[512,512]{1,0:T(8,128)S(1)} %get-tuple-element.22.prior_ref, f32[64,128]{1,0:T(8,128)S(1)} %collective-permute-done.before, f32[64,128]{1,0:T(8,128)S(1)} %collective-permute-done.1.after), custom_call_target="tpu_custom_call" | custom-call | flops 40000000 | bytes 4194304 | tf_op jit(solution)/shard_map/relax_2/pallas_call | solution.py:514
  53.5 3.3 %collective-permute-start.3 = (f32[96,512]{1,0:T(8,128)S(1)}, f32[96,512]{1,0:T(8,128)S(1)}, u32[]{:S(2)}, u32[]{:S(2)}) collective-permute-start(f32[96,512]{1,0:T(8,128)S(1)} %get-tuple-element.28), channel_id=1, source_target_pairs={{0,4},{4,8},{8,12},{12,16},{16,20},{20,24},{24,28},{28,32},{32,36}... | collective-permute-start | bytes 589832 | tf_op jit(solution)/shard_map/ppermute | solution.py:531
  56.8 2.1 %collective-permute-start.5 = (f32[96,512]{1,0:T(8,128)S(1)}, f32[96,512]{1,0:T(8,128)S(1)}, u32[]{:S(2)}, u32[]{:S(2)}) collective-permute-start(f32[96,512]{1,0:T(8,128)S(1)} %get-tuple-element.30), channel_id=1, source_target_pairs={{0,252},{4,0},{8,4},{12,8},{16,12},{20,16},{24,20},{28,24},{32,28}... | collective-permute-start | bytes 589832 | tf_op jit(solution)/shard_map/ppermute | solution.py:531
  58.8 3.1 %relax_0.1 = (f32[256,512]{1,0:T(8,128)S(1)}, f32[96,512]{1,0:T(8,128)S(1)}, f32[96,512]{1,0:T(8,128)S(1)}) custom-call(f32[4,256,256]{2,1,0:T(8,128)S(1)} %get-tuple-element.21.target_ref, f32[512,512]{1,0:T(8,128)S(1)} %get-tuple-element.22.prior_ref, f32[64,128]{1,0:T(8,128)S(1)} %collective-permute-done.before, f32[64,128]{1,0:T(8,128)S(1)} %collective-permute-done.1.after), custom_call_target="tpu_custom_call" | custom-call | flops 40000000 | bytes 4194304 | tf_op jit(solution)/shard_map/relax_0/pallas_call | solution.py:514
  61.9 0.1 collective-permute-start.2
  62.0 5.1 %collective-permute-start.4 = (f32[96,512]{1,0:T(8,128)S(1)}, f32[96,512]{1,0:T(8,128)S(1)}, u32[]{:S(2)}, u32[]{:S(2)}) collective-permute-start(f32[96,512]{1,0:T(8,128)S(1)} %get-tuple-element.29), channel_id=1, source_target_pairs={{0,252},{4,0},{8,4},{12,8},{16,12},{20,16},{24,20},{28,24},{32,28}... | collective-permute-start | bytes 589832 | tf_op jit(solution)/shard_map/ppermute | solution.py:531
  67.1 0.0 collective-permute-done.3.refs_3_
  67.1 0.0 collective-permute-done.5.refs_5_
  67.1 0.8 collective-permute-done.2.refs_2_
  67.9 0.2 collective-permute-done.4.refs_4_
  68.1 7.0 %gather.1 = (f32[4,8,16,512]{3,2,1,0:T(8,128)}, f32[512,128]{1,0:T(8,128)S(1)}) custom-call(s32[16,2]{1,0:T(8,128)S(1)} %get-tuple-element.20.bounds_ref, f32[256,512]{1,0:T(8,128)S(1)} %get-tuple-element.25.refs_0_, f32[256,512]{1,0:T(8,128)S(1)} %get-tuple-element.26.refs_1_, f32[96,512]{1,0:T(8,128)S(1)} %collective-permute-done.2.refs_2_, ...), custom_call_target="tpu_custom_call" | custom-call | tf_op jit(solution)/shard_map/gather/pallas_call | solution.py:391
  75.1 0.0 copy-start
  75.1 27.3 %all_to_all.11 = f32[64,8,128]{2,1,0:T(8,128)S(1)} all-to-all(f32[64,8,128]{2,1,0:T(8,128)S(1)} %bitcast.8), channel_id=1, replica_groups=mesh['span'=64,'depth'=4] {'span'}, dimensions={0} | all-to-all | bytes 524288 | tf_op jit(solution)/shard_map/all_to_all | solution.py:552
  102.4 0.0 copy-done
  102.4 4.4 %pick.1 = f32[4,1,8192]{2,1,0:T(1,128)} custom-call(s32[1,1]{1,0:T(1,128)S(6)} %copy.9.count_ref, s32[1,8192]{1,0:T(1,128)S(1)} %bitcast.10, f32[1,8192]{1,0:T(1,128)S(1)} %get-tuple-element.34.position_ref, f32[512,128]{1,0:T(8,128)S(1)} %bitcast.6), custom_call_target="tpu_custom_call" | custom-call | tf_op jit(solution)/shard_map/pick/pallas_call | solution.py:442
Async XLA Ops:
  45.0 4.3 %collective-permute-start = (f32[64,128]{1,0:T(8,128)S(1)}, f32[64,128]{1,0:T(8,128)S(1)}, u32[]{:S(2)}, u32[]{:S(2)}) collective-permute-start(f32[64,128]{1,0:T(8,128)S(1)} %get-tuple-element.23), channel_id=1, source_target_pairs={{0,1},{1,2},{2,3},{3,0},{4,5},{5,6},{6,7},{7,4},{8,9},{9,10},{10,1... | collective-permute-start | bytes 98312 | tf_op jit(solution)/shard_map/ppermute | solution.py:531
  47.7 2.8 %collective-permute-start.1 = (f32[64,128]{1,0:T(8,128)S(1)}, f32[64,128]{1,0:T(8,128)S(1)}, u32[]{:S(2)}, u32[]{:S(2)}) collective-permute-start(f32[64,128]{1,0:T(8,128)S(1)} %get-tuple-element.24), channel_id=1, source_target_pairs={{0,3},{1,0},{2,1},{3,2},{4,7},{5,4},{6,5},{7,6},{8,11},{9,8},{10,9... | collective-permute-start | bytes 98312 | tf_op jit(solution)/shard_map/ppermute | solution.py:531
  53.5 13.6 %collective-permute-start.3 = (f32[96,512]{1,0:T(8,128)S(1)}, f32[96,512]{1,0:T(8,128)S(1)}, u32[]{:S(2)}, u32[]{:S(2)}) collective-permute-start(f32[96,512]{1,0:T(8,128)S(1)} %get-tuple-element.28), channel_id=1, source_target_pairs={{0,4},{4,8},{8,12},{12,16},{16,20},{20,24},{24,28},{28,32},{32,36}... | collective-permute-start | bytes 589832 | tf_op jit(solution)/shard_map/ppermute | solution.py:531
  56.8 10.3 %collective-permute-start.5 = (f32[96,512]{1,0:T(8,128)S(1)}, f32[96,512]{1,0:T(8,128)S(1)}, u32[]{:S(2)}, u32[]{:S(2)}) collective-permute-start(f32[96,512]{1,0:T(8,128)S(1)} %get-tuple-element.30), channel_id=1, source_target_pairs={{0,252},{4,0},{8,4},{12,8},{16,12},{20,16},{24,20},{28,24},{32,28}... | collective-permute-start | bytes 589832 | tf_op jit(solution)/shard_map/ppermute | solution.py:531
  61.9 6.0 %collective-permute-start.2 = (f32[96,512]{1,0:T(8,128)S(1)}, f32[96,512]{1,0:T(8,128)S(1)}, u32[]{:S(2)}, u32[]{:S(2)}) collective-permute-start(f32[96,512]{1,0:T(8,128)S(1)} %get-tuple-element.27), channel_id=1, source_target_pairs={{0,4},{4,8},{8,12},{12,16},{16,20},{20,24},{24,28},{28,32},{32,36}... | collective-permute-start | bytes 589832 | tf_op jit(solution)/shard_map/ppermute | solution.py:531
  62.0 6.1 %collective-permute-start.4 = (f32[96,512]{1,0:T(8,128)S(1)}, f32[96,512]{1,0:T(8,128)S(1)}, u32[]{:S(2)}, u32[]{:S(2)}) collective-permute-start(f32[96,512]{1,0:T(8,128)S(1)} %get-tuple-element.29), channel_id=1, source_target_pairs={{0,252},{4,0},{8,4},{12,8},{16,12},{20,16},{24,20},{28,24},{32,28}... | collective-permute-start | bytes 589832 | tf_op jit(solution)/shard_map/ppermute | solution.py:531
  75.1 27.3 %copy-start = (s32[1,8192,1]{1,2,0:T(1,128)S(1)}, s32[1,8192,1]{1,2,0:T(1,128)}, u32[]{:S(2)}) copy-start(s32[1,8192,1]{1,2,0:T(1,128)} %param.7) | copy-start | bytes 98308

commit v6 on v5

--- a/solution.py
+++ b/solution.py
@@ -18,7 +18,7 @@
 BACK_ROWS = 8
 SWEEPS = 6
 RIM = SWEEPS
-GROUPS, GROUP = 2, 2
+GROUPS, GROUP = 1, 4
 SIDE_ROWS = 2 * 4 * CX // 16 * LAYERS
 PHI_LIMIT = 0.6
 
@@ -89,7 +89,7 @@
     return solid_ref[:, x, lanes] if comp == 0 else drag_ref[comp - 1, :, x, lanes]
 
 
-PACK_BLOCK = 1024
+PACK_BLOCK = 4096
 SUB = 256
 CLASSES = 4
 
@@ -107,7 +107,7 @@
     earlier = lax.broadcasted_iota(I32, (SUB, SUB), 0)
     later = lax.broadcasted_iota(I32, (SUB, SUB), 1)
     upper = jnp.where(earlier <= later, 1.0, 0.0).astype(BF16)
-    for copy in copies:
+    for copy in copies[:2]:
         copy.wait()
 
     def live_slab(start, size):
@@ -126,6 +126,8 @@
 
     counts = lax.fori_loop(0, PARTS // PACK_BLOCK, count_step, jnp.zeros((OWNERS, 128), F32))
     numbers = [jnp.broadcast_to(counts[:, kind : kind + 1], (OWNERS, 128)) for kind in range(CLASSES)]
+    for copy in copies[2:]:
+        copy.wait()
     starts, end = [], jnp.zeros((OWNERS, 128), F32)
     for kind in range(CLASSES):
         rest = sum(numbers[kind:])
@@ -194,6 +196,9 @@
 
 CHUNKS, CHUNK = 16, 1024
 CLASS_HIGH = HI // CLASSES
+ABREAST = 4
+ITEMS = CHUNKS * CLASSES + 8
+NOWHERE = 1024
 
 
 def swap_halves(first, second):
@@ -210,8 +215,8 @@
 
 def deposit_kernel(
     recv_ref, solid_any, drag_any,
-    out_ref, first_ref, last_ref, prior_ref, high_ref, low_ref, bounds_ref,
-    solid_ref, drag_ref, values, sems,
+    out_ref, first_ref, last_ref, prior_ref, high_ref, low_ref, items_ref,
+    solid_ref, drag_ref, values, bounds_ref, sems,
 ):
     copies = [
         pltpu.make_async_copy(solid_any, solid_ref, sems.at[0]),
@@ -244,9 +249,28 @@
         for chunk, value in enumerate(chunked(comp + 1)):
             values[comp, chunk] = value
 
-    def step(chunk, carry):
-        def class_step(kind, carry):
-            key = high_ref[chunk] - (kind * CLASS_HIGH).astype(F32)
+    def list_chunk(chunk, count):
+        def list_class(kind, count):
+            items_ref[0, count] = chunk
+            items_ref[1, count] = kind * CLASS_HIGH
+            items_ref[2, count] = kind * CLASS_HIGH
+            return count + 1
+
+        return lax.fori_loop(bounds_ref[chunk, 0], bounds_ref[chunk, 1], list_class, count)
+
+    count = lax.fori_loop(0, CHUNKS, list_chunk, 0)
+    for spare in range(ABREAST):
+        items_ref[0, count + spare] = 0
+        items_ref[1, count + spare] = NOWHERE
+        items_ref[2, count + spare] = 0
+    steps = (count + ABREAST - 1) // ABREAST
+    items_ref[0, ITEMS - 1] = steps
+
+    def step(index, carry):
+        totals = []
+        for item in range(ABREAST):
+            chunk = items_ref[0, index * ABREAST + item]
+            key = high_ref[chunk] - items_ref[1, index * ABREAST + item].astype(F32)
             members = [row_is(key[r : r + 1], CLASS_HIGH) for r in range(8)]
             lows = low_hots(low_ref, chunk)
             left = []
@@ -263,15 +287,14 @@
                         axis=1,
                     )
                 )
-            total = dot_nt(jnp.concatenate(left, axis=0), jnp.concatenate([lows, lows], axis=1))
-            spot = pl.ds(pl.multiple_of(kind * CLASS_HIGH, CLASS_HIGH), CLASS_HIGH)
+            totals.append(dot_nt(jnp.concatenate(left, axis=0), jnp.concatenate([lows, lows], axis=1)))
+        for item in range(ABREAST):
+            spot = pl.ds(pl.multiple_of(items_ref[2, index * ABREAST + item], CLASS_HIGH), CLASS_HIGH)
             for comp in range(4):
-                out_ref[comp, spot, :] += total[comp * CLASS_HIGH : (comp + 1) * CLASS_HIGH, :]
-            return carry
-
-        return lax.fori_loop(bounds_ref[chunk, 0], bounds_ref[chunk, 1], class_step, carry)
-
-    lax.fori_loop(0, CHUNKS, step, 0)
+                out_ref[comp, spot, :] += totals[item][comp * CLASS_HIGH : (comp + 1) * CLASS_HIGH, :]
+        return carry
+
+    lax.fori_loop(0, steps, step, 0)
     out_ref[0] = jnp.minimum(out_ref[0], PHI_LIMIT)
     for copy in copies:
         copy.wait()
@@ -305,7 +328,7 @@
             jax.ShapeDtypeStruct((4 * CX * LAYERS, CY), F32),
             index,
             index,
-            jax.ShapeDtypeStruct((CHUNKS, 2), I32),
+            jax.ShapeDtypeStruct((3, ITEMS), I32),
         ),
         in_specs=[vmem, hbm, hbm],
         out_specs=(vmem,) * 6 + (pl.BlockSpec(memory_space=pltpu.SMEM),),
@@ -313,6 +336,7 @@
             pltpu.VMEM((LAYERS, CX, CY), F32),
             pltpu.VMEM((3, LAYERS, CX, CY), F32),
             pltpu.VMEM((4, CHUNKS, 8, 128), F32),
+            pltpu.SMEM((CHUNKS, 2), I32),
             pltpu.SemaphoreType.DMA((2,)),
         ],
         compiler_params=pltpu.CompilerParams(vmem_limit_bytes=16 * MIB),
@@ -320,7 +344,7 @@
     )(received, solid, drag)
 
 
-def gather_kernel(bounds_ref, *refs):
+def gather_kernel(items_ref, *refs):
     own_refs, above_refs, below_refs = refs[0:GROUPS], refs[GROUPS : 2 * GROUPS], refs[2 * GROUPS : 3 * GROUPS]
     high_ref, low_ref, fields_any, out_ref, fields, tops, bottoms, found, sem = refs[3 * GROUPS :]
     top, bottom = at_edge("span")
@@ -351,11 +375,15 @@
     copy.start()
     ids = lax.broadcasted_iota(I32, (CLASS_HIGH, 128), 0).astype(F32)
 
-    def step(chunk, carry):
-        def class_step(kind, sums):
-            key = high_ref[chunk] - (kind * CLASS_HIGH).astype(F32)
+    found[...] = jnp.zeros_like(found)
+
+    def step(index, carry):
+        news = []
+        for item in range(ABREAST):
+            chunk = items_ref[0, index * ABREAST + item]
+            key = high_ref[chunk] - items_ref[1, index * ABREAST + item].astype(F32)
             lows = low_hots(low_ref, chunk)
-            spot = pl.ds(pl.multiple_of(kind * CLASS_HIGH, CLASS_HIGH), CLASS_HIGH)
+            spot = pl.ds(pl.multiple_of(items_ref[2, index * ABREAST + item], CLASS_HIGH), CLASS_HIGH)
             members = [ids == key[r : r + 1] for r in range(8)]
             table = [jnp.concatenate([part[comp, spot, :] for comp in range(4)], axis=0) for part in (tops, bottoms)]
             value = dot_nn(table[0], lows) + dot_nn(table[1], lows)
@@ -366,16 +394,15 @@
                     jnp.sum(jnp.where(members[r], rows[:, r * 128 : (r + 1) * 128], 0.0), axis=0, keepdims=True)
                     for r in range(8)
                 ]
-                new.append(sums[comp] + jnp.concatenate(pieces, axis=0))
-            return tuple(new)
-
-        start = (jnp.zeros((8, 128), F32),) * 4
-        sums = lax.fori_loop(bounds_ref[chunk, 0], bounds_ref[chunk, 1], class_step, start)
-        for comp in range(4):
-            found[comp, chunk] = sums[comp]
+                new.append(jnp.concatenate(pieces, axis=0))
+            news.append(new)
+        for item in range(ABREAST):
+            chunk = items_ref[0, index * ABREAST + item]
+            for comp in range(4):
+                found[comp, chunk] += news[item][comp]
         return carry
 
-    lax.fori_loop(0, CHUNKS, step, 0)
+    lax.fori_loop(0, items_ref[0, ITEMS - 1], step, 0)
     for comp in range(4):
         slots = []
         for m in range(8):
@@ -386,7 +413,7 @@
     copy.wait()
 
 
-def gather(bounds, owns, aboves, belows, high, low):
+def gather(items, owns, aboves, belows, high, low):
     vmem = pl.BlockSpec(memory_space=pltpu.VMEM)
     return pl.pallas_call(
         gather_kernel,
@@ -405,10 +432,10 @@
         ],
         compiler_params=pltpu.CompilerParams(vmem_limit_bytes=16 * MIB),
         name="gather",
-    )(bounds, *owns, *aboves, *belows, high, low)
-
-
-PICK_BLOCK = 1024
+    )(items, *owns, *aboves, *belows, high, low)
+
+
+PICK_BLOCK = 4096
 
 
 def pick_kernel(count_ref, slab_ref, position_ref, back_ref, out_ref, tops, bottoms):
@@ -537,7 +564,7 @@
     sent, position = pack(part_count, *in_hbm)
     received = lax.all_to_all(sent.reshape(OWNERS, 5, 2, 128), "span", 0, 0, tiled=True)
     received = received.reshape(OWNERS * ROWS, 128)
-    target, first, last, prior, high, low, bounds = deposit(
+    target, first, last, prior, high, low, items = deposit(
         received, *[pltpu.with_memory_space_constraint(a, pltpu.HBM) for a in (prior_solid, prior_drag)]
     )
     before = shifted(last, "depth", 1)
@@ -548,7 +575,7 @@
         owns.append(own)
         aboves.append(shifted(down, "span", 1))
         belows.append(shifted(up, "span", -1))
-    fields, returned = gather(bounds, owns, aboves, belows, high, low)
+    fields, returned = gather(items, owns, aboves, belows, high, low)
     back = lax.all_to_all(returned.reshape(OWNERS, BACK_ROWS, 128), "span", 0, 0, tiled=True)
     feedback = pick(part_count, slab, position, back.reshape(OWNERS * BACK_ROWS, 128))
     return fields, feedback

time: 109 us -> 94.9 us (0.87); the launches traced: 107 us -> 95 us
  starting transfers between devices: 13.6 us -> 6.12 us
  blocking collectives: 53.5 us -> 47.8 us
  waiting for transfers between devices: 3.38 us -> 6.68 us
  Pallas kernels: 34.9 us -> 33.1 us
    ppermute x6 -> x4, starting transfers between devices: 13.6 us -> 6.12 us  [shifted(): lax.ppermute(array, axis, [(i, (i + step) % count) for i in range(count)])]
    all_to_all x1, blocking collectives: 27.3 us -> 21.6 us  [on_device(): lax.all_to_all(returned.reshape(OWNERS, BACK_ROWS, 128), 'span', 0, 0, ti...]
    ppermute x6 -> x4, waiting for transfers between devices: 3.38 us -> 6.68 us  [shifted(): lax.ppermute(array, axis, [(i, (i + step) % count) for i in range(count)])]
    pallas_call x1, Pallas kernels: 10 us -> 7.15 us  [pack(): pl.pallas_call(pack_kernel, out_shape=(jax.ShapeDtypeStruct((OWNERS * ROW...]
    pallas_call x2 -> x1, Pallas kernels: 6.13 us -> 6.16 us  [relax(): pl.pallas_call(functools.partial(relax_kernel, base), out_shape=(jax.Shap...]
  transfers between devices with their start and end apart: 6 -> 4, of which waited for: 4 -> 3; matrix products, arithmetic and copies ran while one was open for 0% -> 0% of each run, Pallas kernels for 3% -> 0%
where the time goes in v6:
time: 94.9 us; the launch traced here: 95 us
  blocking collectives  47.8 us (50%)
  Pallas kernels  33.1 us (35%)
  waiting for transfers between devices  6.68 us (7%)
  starting transfers between devices  6.12 us (6%)
  between operations  1.33 us (1%)
    all_to_all x1, blocking collectives, on_device(): lax.all_to_all(sent.reshape(OWNERS, 5, 2, 128), 'span', 0, 0, tiled=True)  26.2 us
    all_to_all x1, blocking collectives, on_device(): lax.all_to_all(returned.reshape(OWNERS, BACK_ROWS, 128), 'span', 0, 0, ti...  21.6 us
    pallas_call x1, Pallas kernels, deposit(): pl.pallas_call(deposit_kernel, out_shape=(jax.ShapeDtypeStruct((4, HI, LO...  8.38 us
    pallas_call x1, Pallas kernels, gather(): pl.pallas_call(gather_kernel, out_shape=(jax.ShapeDtypeStruct((4, LAYERS,...  7.93 us
    pallas_call x1, Pallas kernels, pack(): pl.pallas_call(pack_kernel, out_shape=(jax.ShapeDtypeStruct((OWNERS * ROW...  7.15 us
    ppermute x4, waiting for transfers between devices, shifted(): lax.ppermute(array, axis, [(i, (i + step) % count) for i in range(count)])  6.68 us
    pallas_call x1, Pallas kernels, relax(): pl.pallas_call(functools.partial(relax_kernel, base), out_shape=(jax.Shap...  6.16 us
    ppermute x4, starting transfers between devices, shifted(): lax.ppermute(array, axis, [(i, (i + step) % count) for i in range(count)])  6.12 us
  transfers between devices with their start and end apart: 4, of which 3 were waited for; matrix products, arithmetic and copies ran while one was open for 0% of the time, Pallas kernels for 0%

profile of v6, /device:TPU:1, one launch (start us, length us, event | category | flops | bytes accessed | tf_op | source)
XLA Modules:
  0.0 95.0 jit_solution(3839925802650567969)
XLA Ops:
  1.3 7.2 %pack.1 = (f32[640,128]{1,0:T(8,128)S(1)}, f32[1,8192]{1,0:T(1,128)S(1)}) custom-call(s32[1,1]{1,0:T(1,128)S(6)} %copy.9.count_ref, s32[1,8192]{1,0:T(1,128)} %bitcast.9, s32[1,8192]{1,0:T(1,128)} %cell_any.1, f32[1,8192]{1,0:T(1,128)} %volume_any.1, f32[3,1,8192]{2,1,0:T(1,128)} %drag_any.2), custom_call_target="tpu_custom_call" | custom-call | tf_op jit(solution)/shard_map/pack/pallas_call | solution.py:176
  8.4 26.2 %all_to_all.10 = f32[64,5,2,128]{3,2,1,0:T(2,128)S(1)} all-to-all(f32[64,5,2,128]{3,2,1,0:T(2,128)S(1)} %bitcast.7), channel_id=1, replica_groups=mesh['span'=64,'depth'=4] {'span'}, dimensions={0} | all-to-all | bytes 655360 | tf_op jit(solution)/shard_map/all_to_all | solution.py:565
  34.6 8.4 %deposit.1 = (f32[4,256,256]{2,1,0:T(8,128)S(1)}, f32[64,128]{1,0:T(8,128)S(1)}, f32[64,128]{1,0:T(8,128)S(1)}, f32[512,512]{1,0:T(8,128)S(1)}, f32[16,8,128]{2,...) custom-call(f32[640,128]{1,0:T(8,128)S(1)} %bitcast.5, f32[8,16,512]{2,1,0:T(8,128)} %solid_any.1, ...), custom_call_target="tpu_custom_call" | custom-call | tf_op jit(solution)/shard_map/deposit/pallas_call | solution.py:322
  43.0 0.1 collective-permute-start
  43.1 2.7 %collective-permute-start.1 = (f32[64,128]{1,0:T(8,128)S(1)}, f32[64,128]{1,0:T(8,128)S(1)}, u32[]{:S(2)}, u32[]{:S(2)}) collective-permute-start(f32[64,128]{1,0:T(8,128)S(1)} %get-tuple-element.21), channel_id=1, source_target_pairs={{0,3},{1,0},{2,1},{3,2},{4,7},{5,4},{6,5},{7,6},{8,11},{9,8},{10,9... | collective-permute-start | bytes 98312 | tf_op jit(solution)/shard_map/ppermute | solution.py:558
  45.8 1.3 %collective-permute-done.before = f32[64,128]{1,0:T(8,128)S(1)} collective-permute-done((f32[64,128]{1,0:T(8,128)S(1)}, f32[64,128]{1,0:T(8,128)S(1)}, u32[]{:S(2)}, u32[]{:S(2)}) %collective-permute-start) | collective-permute-done | bytes 32800 | tf_op jit(solution)/shard_map/ppermute | solution.py:558
  47.1 0.0 collective-permute-done.1.after
  47.1 6.2 %relax_0.1 = (f32[512,512]{1,0:T(8,128)S(1)}, f32[192,512]{1,0:T(8,128)S(1)}, f32[192,512]{1,0:T(8,128)S(1)}) custom-call(f32[4,256,256]{2,1,0:T(8,128)S(1)} %get-tuple-element.18.target_ref, f32[512,512]{1,0:T(8,128)S(1)} %get-tuple-element.19.prior_ref, f32[64,128]{1,0:T(8,128)S(1)} %collective-permute-done.before, f32[64,128]{1,0:T(8,128)S(1)} %collective-permute-done.1.after), custom_call_target="tpu_custom_call" | custom-call | flops 40000000 | bytes 4194304 | tf_op jit(solution)/shard_map/relax_0/pallas_call | solution.py:541
  53.2 1.6 %collective-permute-start.2 = (f32[192,512]{1,0:T(8,128)S(1)}, f32[192,512]{1,0:T(8,128)S(1)}, u32[]{:S(2)}, u32[]{:S(2)}) collective-permute-start(f32[192,512]{1,0:T(8,128)S(1)} %get-tuple-element.23), channel_id=1, source_target_pairs={{0,4},{4,8},{8,12},{12,16},{16,20},{20,24},{24,28},{28,32},{32,36}... | collective-permute-start | bytes 1179656 | tf_op jit(solution)/shard_map/ppermute | solution.py:558
  54.8 1.8 %collective-permute-start.3 = (f32[192,512]{1,0:T(8,128)S(1)}, f32[192,512]{1,0:T(8,128)S(1)}, u32[]{:S(2)}, u32[]{:S(2)}) collective-permute-start(f32[192,512]{1,0:T(8,128)S(1)} %get-tuple-element.24), channel_id=1, source_target_pairs={{0,252},{4,0},{8,4},{12,8},{16,12},{20,16},{24,20},{28,24},{32,28}... | collective-permute-start | bytes 1179656 | tf_op jit(solution)/shard_map/ppermute | solution.py:558
  56.6 2.9 %collective-permute-done.2.refs_1_ = f32[192,512]{1,0:T(8,128)S(1)} collective-permute-done((f32[192,512]{1,0:T(8,128)S(1)}, f32[192,512]{1,0:T(8,128)S(1)}, u32[]{:S(2)}, u32[]{:S(2)}) %collective-permute-start.2) | collective-permute-done | bytes 393248 | tf_op jit(solution)/shard_map/ppermute | solution.py:558
  59.5 2.5 %collective-permute-done.3.refs_2_ = f32[192,512]{1,0:T(8,128)S(1)} collective-permute-done((f32[192,512]{1,0:T(8,128)S(1)}, f32[192,512]{1,0:T(8,128)S(1)}, u32[]{:S(2)}, u32[]{:S(2)}) %collective-permute-start.3) | collective-permute-done | bytes 393248 | tf_op jit(solution)/shard_map/ppermute | solution.py:558
  62.0 7.9 %gather.1 = (f32[4,8,16,512]{3,2,1,0:T(8,128)}, f32[512,128]{1,0:T(8,128)S(1)}) custom-call(s32[3,72]{1,0:T(4,128)S(1)} %get-tuple-element.17.items_ref, f32[512,512]{1,0:T(8,128)S(1)} %get-tuple-element.22.refs_0_, f32[192,512]{1,0:T(8,128)S(1)} %collective-permute-done.2.refs_1_, f32[192,512]{1,0:T(8,128)S(1)} %collective-permute-done.3.refs_2_, ...), custom_call_target="tpu_custom_call" | custom-call | tf_op jit(solution)/shard_map/gather/pallas_call | solution.py:418
  69.9 0.0 copy-start
  69.9 21.6 %all_to_all.11 = f32[64,8,128]{2,1,0:T(8,128)S(1)} all-to-all(f32[64,8,128]{2,1,0:T(8,128)S(1)} %bitcast.8), channel_id=1, replica_groups=mesh['span'=64,'depth'=4] {'span'}, dimensions={0} | all-to-all | bytes 524288 | tf_op jit(solution)/shard_map/all_to_all | solution.py:579
  91.5 0.0 copy-done
  91.5 3.5 %pick.1 = f32[4,1,8192]{2,1,0:T(1,128)} custom-call(s32[1,1]{1,0:T(1,128)S(6)} %copy.9.count_ref, s32[1,8192]{1,0:T(1,128)S(1)} %bitcast.10, f32[1,8192]{1,0:T(1,128)S(1)} %get-tuple-element.28.position_ref, f32[512,128]{1,0:T(8,128)S(1)} %bitcast.6), custom_call_target="tpu_custom_call" | custom-call | tf_op jit(solution)/shard_map/pick/pallas_call | solution.py:469
Async XLA Ops:
  43.0 4.1 %collective-permute-start = (f32[64,128]{1,0:T(8,128)S(1)}, f32[64,128]{1,0:T(8,128)S(1)}, u32[]{:S(2)}, u32[]{:S(2)}) collective-permute-start(f32[64,128]{1,0:T(8,128)S(1)} %get-tuple-element.20), channel_id=1, source_target_pairs={{0,1},{1,2},{2,3},{3,0},{4,5},{5,6},{6,7},{7,4},{8,9},{9,10},{10,1... | collective-permute-start | bytes 98312 | tf_op jit(solution)/shard_map/ppermute | solution.py:558
  43.1 4.0 %collective-permute-start.1 = (f32[64,128]{1,0:T(8,128)S(1)}, f32[64,128]{1,0:T(8,128)S(1)}, u32[]{:S(2)}, u32[]{:S(2)}) collective-permute-start(f32[64,128]{1,0:T(8,128)S(1)} %get-tuple-element.21), channel_id=1, source_target_pairs={{0,3},{1,0},{2,1},{3,2},{4,7},{5,4},{6,5},{7,6},{8,11},{9,8},{10,9... | collective-permute-start | bytes 98312 | tf_op jit(solution)/shard_map/ppermute | solution.py:558
  53.2 6.3 %collective-permute-start.2 = (f32[192,512]{1,0:T(8,128)S(1)}, f32[192,512]{1,0:T(8,128)S(1)}, u32[]{:S(2)}, u32[]{:S(2)}) collective-permute-start(f32[192,512]{1,0:T(8,128)S(1)} %get-tuple-element.23), channel_id=1, source_target_pairs={{0,4},{4,8},{8,12},{12,16},{16,20},{20,24},{24,28},{28,32},{32,36}... | collective-permute-start | bytes 1179656 | tf_op jit(solution)/shard_map/ppermute | solution.py:558
  54.8 7.2 %collective-permute-start.3 = (f32[192,512]{1,0:T(8,128)S(1)}, f32[192,512]{1,0:T(8,128)S(1)}, u32[]{:S(2)}, u32[]{:S(2)}) collective-permute-start(f32[192,512]{1,0:T(8,128)S(1)} %get-tuple-element.24), channel_id=1, source_target_pairs={{0,252},{4,0},{8,4},{12,8},{16,12},{20,16},{24,20},{28,24},{32,28}... | collective-permute-start | bytes 1179656 | tf_op jit(solution)/shard_map/ppermute | solution.py:558
  69.9 21.6 %copy-start = (s32[1,8192,1]{1,2,0:T(1,128)S(1)}, s32[1,8192,1]{1,2,0:T(1,128)}, u32[]{:S(2)}) copy-start(s32[1,8192,1]{1,2,0:T(1,128)} %param.7) | copy-start | bytes 98308

commit v7 on v6

--- a/solution.py
+++ b/solution.py
@@ -18,7 +18,6 @@
 BACK_ROWS = 8
 SWEEPS = 6
 RIM = SWEEPS
-GROUPS, GROUP = 1, 4
 SIDE_ROWS = 2 * 4 * CX // 16 * LAYERS
 PHI_LIMIT = 0.6
 
@@ -344,20 +343,20 @@
     )(received, solid, drag)
 
 
-def gather_kernel(items_ref, *refs):
-    own_refs, above_refs, below_refs = refs[0:GROUPS], refs[GROUPS : 2 * GROUPS], refs[2 * GROUPS : 3 * GROUPS]
-    high_ref, low_ref, fields_any, out_ref, fields, tops, bottoms, found, sem = refs[3 * GROUPS :]
+def gather_kernel(
+    items_ref, own_ref, above_ref, below_ref, high_ref, low_ref, fields_any, out_ref,
+    fields, tops, bottoms, found, sem,
+):
     top, bottom = at_edge("span")
 
     def smooth(comp, x):
-        group, comp = comp // GROUP, comp % GROUP
-        row = own_refs[group][pl.ds((comp * CX + x) * LAYERS, LAYERS), :]
+        row = own_ref[pl.ds((comp * CX + x) * LAYERS, LAYERS), :]
         if x < RIM:
             spot = pl.ds((comp * RIM + x) * LAYERS, LAYERS)
-            row = row + jnp.where(top, 0.0, above_refs[group][spot, :])
+            row = row + jnp.where(top, 0.0, above_ref[spot, :])
         if x >= CX - RIM:
             spot = pl.ds((comp * RIM + x - CX + RIM) * LAYERS, LAYERS)
-            row = row + jnp.where(bottom, 0.0, below_refs[group][spot, :])
+            row = row + jnp.where(bottom, 0.0, below_ref[spot, :])
         return row
 
     for pair in range(0, CX, 2):
@@ -413,7 +412,7 @@
     copy.wait()
 
 
-def gather(items, owns, aboves, belows, high, low):
+def gather(items, *arrays):
     vmem = pl.BlockSpec(memory_space=pltpu.VMEM)
     return pl.pallas_call(
         gather_kernel,
@@ -421,7 +420,7 @@
             jax.ShapeDtypeStruct((4, LAYERS, CX, CY), F32),
             jax.ShapeDtypeStruct((OWNERS * BACK_ROWS, 128), F32),
         ),
-        in_specs=[pl.BlockSpec(memory_space=pltpu.SMEM)] + [vmem] * (3 * GROUPS + 2),
+        in_specs=[pl.BlockSpec(memory_space=pltpu.SMEM)] + [vmem] * 5,
         out_specs=(pl.BlockSpec(memory_space=pltpu.HBM), vmem),
         scratch_shapes=[
             pltpu.VMEM((4, LAYERS, CX, CY), F32),
@@ -432,7 +431,7 @@
         ],
         compiler_params=pltpu.CompilerParams(vmem_limit_bytes=16 * MIB),
         name="gather",
-    )(items, *owns, *aboves, *belows, high, low)
+    )(items, *arrays)
 
 
 PICK_BLOCK = 4096
@@ -481,24 +480,22 @@
 RELAX_FLOPS = 40_000_000
 
 
-def relax_kernel(
-    base, target_ref, prior_ref, before, after, own_ref, up_ref, down_ref, state, source
-):
+def relax_kernel(for_rim, target_ref, prior_ref, before, after, *refs):
+    outs, (state, source) = refs[:-2], refs[-2:]
     top, bottom = at_edge("span")
     first, last = at_edge("depth")
     near = lax.broadcasted_iota(I32, (LAYERS, 128), 1)
     is_before = (near >= 120) & jnp.logical_not(first)
     is_after = (near < 8) & jnp.logical_not(last)
     blank = jnp.zeros((LAYERS, WIDE), F32)
-    for comp in range(GROUP):
-        for x in range(RIM):
-            state[comp, x] = blank
-            state[comp, RIM + CX + x] = blank
+    for comp in range(4):
         for x in range(CX):
-            row = (base + comp) * CX + x
+            if for_rim and RIM <= x < CX - RIM:
+                continue
+            row = comp * CX + x
             for half in range(2):
                 spot = pl.ds((half * CX + x) * LAYERS, LAYERS)
-                source[comp, x, :, half * LO : (half + 1) * LO] = target_ref[base + comp, spot, :]
+                source[comp, x, :, half * LO : (half + 1) * LO] = target_ref[comp, spot, :]
             source[comp, x, :, CY:WIDE] = unfold_side(row, before, after, is_before, is_after)
             state[comp, RIM + x, :, 0:CY] = prior_ref[row * LAYERS : (row + 1) * LAYERS, :]
             state[comp, RIM + x, :, CY:WIDE] = unfold_side(4 * CX + row, before, after, is_before, is_after)
@@ -509,47 +506,60 @@
     above_factor = jnp.where(top, 0.0, factor)
     below_factor = jnp.where(bottom, 0.0, factor)
 
+    def sweep_rows(comp, sweep, low, high):
+        def old(x):
+            return state[comp, x + RIM] if -sweep < x < CX - 1 + sweep else blank
+
+        above, here = old(low - 1), old(low)
+        for x in range(low, high + 1):
+            below = old(x + 1)
+            total = above + below
+            if -sweep < x < CX - 1 + sweep:
+                total = total + pltpu.roll(here, 1, 1) + pltpu.roll(here, WIDE - 1, 1)
+            if 0 <= x < CX:
+                total = total + source[comp, x]
+            scale = above_factor if x < 0 else below_factor if x >= CX else factor
+            state[comp, x + RIM] = total * scale
+            above, here = here, below
+
     def comp_step(comp, carry):
-        for sweep in range(SWEEPS):
-            rim = sweep + 1
-            above, here = blank, blank
-            for x in range(-rim, CX + rim):
-                below = state[comp, x + 1 + RIM] if x + 1 < CX + sweep else blank
-                total = above + below
-                if -sweep <= x < CX + sweep:
-                    total = total + pltpu.roll(here, 1, 1) + pltpu.roll(here, WIDE - 1, 1)
-                if 0 <= x < CX:
-                    total = total + source[comp, x]
-                scale = above_factor if x < 0 else below_factor if x >= CX else factor
-                state[comp, x + RIM] = total * scale
-                above, here = here, below
+        for sweep in range(1, SWEEPS + 1):
+            if for_rim:
+                sweep_rows(comp, sweep, -sweep, RIM - 1 - sweep)
+                sweep_rows(comp, sweep, CX - RIM + sweep, CX - 1 + sweep)
+            else:
+                reach = min(sweep, SWEEPS - sweep)
+                sweep_rows(comp, sweep, -reach, CX - 1 + reach)
         return carry
 
-    lax.fori_loop(0, GROUP, comp_step, 0)
-    for comp in range(GROUP):
-        for x in range(CX):
-            own_ref[pl.ds((comp * CX + x) * LAYERS, LAYERS), :] = state[comp, RIM + x, :, 0:CY]
-        for x in range(RIM):
-            spot = pl.ds((comp * RIM + x) * LAYERS, LAYERS)
-            up_ref[spot, :] = state[comp, x, :, 0:CY]
-            down_ref[spot, :] = state[comp, RIM + CX + x, :, 0:CY]
-
-
-def relax(base, *arrays):
+    lax.fori_loop(0, 4, comp_step, 0)
+    for comp in range(4):
+        if for_rim:
+            for x in range(RIM):
+                spot = pl.ds((comp * RIM + x) * LAYERS, LAYERS)
+                outs[0][spot, :] = state[comp, x, :, 0:CY]
+                outs[1][spot, :] = state[comp, RIM + CX + x, :, 0:CY]
+        else:
+            for x in range(CX):
+                outs[0][pl.ds((comp * CX + x) * LAYERS, LAYERS), :] = state[comp, RIM + x, :, 0:CY]
+
+
+def relax(for_rim, *arrays):
     vmem = pl.BlockSpec(memory_space=pltpu.VMEM)
-    rim = jax.ShapeDtypeStruct((GROUP * RIM * LAYERS, CY), F32)
+    rim = jax.ShapeDtypeStruct((4 * RIM * LAYERS, CY), F32)
+    own = jax.ShapeDtypeStruct((4 * CX * LAYERS, CY), F32)
     return pl.pallas_call(
-        functools.partial(relax_kernel, base),
-        out_shape=(jax.ShapeDtypeStruct((GROUP * CX * LAYERS, CY), F32), rim, rim),
+        functools.partial(relax_kernel, for_rim),
+        out_shape=(rim, rim) if for_rim else own,
         in_specs=[vmem] * 4,
-        out_specs=(vmem, vmem, vmem),
+        out_specs=(vmem, vmem) if for_rim else vmem,
         scratch_shapes=[
-            pltpu.VMEM((GROUP, CX + 2 * RIM, LAYERS, WIDE), F32),
-            pltpu.VMEM((GROUP, CX, LAYERS, WIDE), F32),
+            pltpu.VMEM((4, CX + 2 * RIM, LAYERS, WIDE), F32),
+            pltpu.VMEM((4, CX, LAYERS, WIDE), F32),
         ],
         compiler_params=pltpu.CompilerParams(vmem_limit_bytes=12 * MIB),
         cost_estimate=pl.CostEstimate(flops=RELAX_FLOPS, bytes_accessed=4 * MIB, transcendentals=0),
-        name=f"relax_{base}",
+        name="relax_rim" if for_rim else "relax_own",
     )(*arrays)
 
 
@@ -569,13 +579,12 @@
     )
     before = shifted(last, "depth", 1)
     after = shifted(first, "depth", -1)
-    owns, aboves, belows = [], [], []
-    for group in range(GROUPS):
-        own, up, down = relax(group * GROUP, target, prior, before, after)
-        owns.append(own)
-        aboves.append(shifted(down, "span", 1))
-        belows.append(shifted(up, "span", -1))
-    fields, returned = gather(items, owns, aboves, belows, high, low)
+    arrays = (target, prior, before, after)
+    up, down = relax(True, *arrays)
+    from_above = shifted(down, "span", 1)
+    from_below = shifted(up, "span", -1)
+    own = relax(False, *arrays)
+    fields, returned = gather(items, own, from_above, from_below, high, low)
     back = lax.all_to_all(returned.reshape(OWNERS, BACK_ROWS, 128), "span", 0, 0, tiled=True)
     feedback = pick(part_count, slab, position, back.reshape(OWNERS * BACK_ROWS, 128))
     return fields, feedback

time: 94.9 us -> 93.2 us (0.982)
  blocking collectives: 47.8 us -> 50.9 us
  waiting for transfers between devices: 6.68 us -> 3.78 us
  starting transfers between devices: 6.12 us -> 4.05 us
    all_to_all x1, blocking collectives: 21.6 us -> 24.7 us  [on_device(): lax.all_to_all(returned.reshape(OWNERS, BACK_ROWS, 128), 'span', 0, 0, ti...]
    ppermute x4, waiting for transfers between devices: 6.68 us -> 3.78 us  [shifted(): lax.ppermute(array, axis, [(i, (i + step) % count) for i in range(count)])]
    pallas_call x1 -> x2, Pallas kernels: 6.16 us -> 8.41 us  [relax(): pl.pallas_call(functools.partial(relax_kernel, for_rim), out_shape=(rim,...]
    ppermute x4, starting transfers between devices: 6.12 us -> 4.05 us  [shifted(): lax.ppermute(array, axis, [(i, (i + step) % count) for i in range(count)])]
    pallas_call x1, Pallas kernels: 8.38 us -> 6.99 us  [deposit(): pl.pallas_call(deposit_kernel, out_shape=(jax.ShapeDtypeStruct((4, HI, LO...]
    pallas_call x1, Pallas kernels: 7.93 us -> 6.63 us  [gather(): pl.pallas_call(gather_kernel, out_shape=(jax.ShapeDtypeStruct((4, LAYERS,...]
  transfers between devices with their start and end apart: 4 -> 4, of which waited for: 3 -> 3; matrix products, arithmetic and copies ran while one was open for 0% -> 0% of each run, Pallas kernels for 0% -> 6%
where the time goes in v7:
time: 93.2 us; the launch traced here: 92.8 us
  blocking collectives  50.9 us (55%)
  Pallas kernels  32.6 us (35%)
  starting transfers between devices  4.05 us (4%)
  waiting for transfers between devices  3.78 us (4%)
  between operations  1.34 us (1%)
    all_to_all x1, blocking collectives, on_device(): lax.all_to_all(sent.reshape(OWNERS, 5, 2, 128), 'span', 0, 0, tiled=True)  26.2 us
    all_to_all x1, blocking collectives, on_device(): lax.all_to_all(returned.reshape(OWNERS, BACK_ROWS, 128), 'span', 0, 0, ti...  24.7 us
    pallas_call x2, Pallas kernels, relax(): pl.pallas_call(functools.partial(relax_kernel, for_rim), out_shape=(rim,...  8.41 us
    pallas_call x1, Pallas kernels, pack(): pl.pallas_call(pack_kernel, out_shape=(jax.ShapeDtypeStruct((OWNERS * ROW...  7.15 us
    pallas_call x1, Pallas kernels, deposit(): pl.pallas_call(deposit_kernel, out_shape=(jax.ShapeDtypeStruct((4, HI, LO...  6.99 us
    pallas_call x1, Pallas kernels, gather(): pl.pallas_call(gather_kernel, out_shape=(jax.ShapeDtypeStruct((4, LAYERS,...  6.63 us
    ppermute x4, starting transfers between devices, shifted(): lax.ppermute(array, axis, [(i, (i + step) % count) for i in range(count)])  4.05 us
    ppermute x4, waiting for transfers between devices, shifted(): lax.ppermute(array, axis, [(i, (i + step) % count) for i in range(count)])  3.78 us
  transfers between devices with their start and end apart: 4, of which 3 were waited for; matrix products, arithmetic and copies ran while one was open for 0% of the time, Pallas kernels for 6%

profile of v7, /device:TPU:1, one launch (start us, length us, event | category | flops | bytes accessed | tf_op | source)
XLA Modules:
  0.0 92.8 jit_solution(15396067045364037188)
XLA Ops:
  1.3 7.2 %pack.1 = (f32[640,128]{1,0:T(8,128)S(1)}, f32[1,8192]{1,0:T(1,128)S(1)}) custom-call(s32[1,1]{1,0:T(1,128)S(6)} %copy.9.count_ref, s32[1,8192]{1,0:T(1,128)} %bitcast.9, s32[1,8192]{1,0:T(1,128)} %cell_any.1, f32[1,8192]{1,0:T(1,128)} %volume_any.1, f32[3,1,8192]{2,1,0:T(1,128)} %drag_any.2), custom_call_target="tpu_custom_call" | custom-call | tf_op jit(solution)/shard_map/pack/pallas_call | solution.py:175
  8.4 26.2 %all_to_all.10 = f32[64,5,2,128]{3,2,1,0:T(2,128)S(1)} all-to-all(f32[64,5,2,128]{3,2,1,0:T(2,128)S(1)} %bitcast.7), channel_id=1, replica_groups=mesh['span'=64,'depth'=4] {'span'}, dimensions={0} | all-to-all | bytes 655360 | tf_op jit(solution)/shard_map/all_to_all | solution.py:575
  34.6 7.0 %deposit.1 = (f32[4,256,256]{2,1,0:T(8,128)S(1)}, f32[64,128]{1,0:T(8,128)S(1)}, f32[64,128]{1,0:T(8,128)S(1)}, f32[512,512]{1,0:T(8,128)S(1)}, f32[16,8,128]{2,...) custom-call(f32[640,128]{1,0:T(8,128)S(1)} %bitcast.5, f32[8,16,512]{2,1,0:T(8,128)} %solid_any.1, ...), custom_call_target="tpu_custom_call" | custom-call | tf_op jit(solution)/shard_map/deposit/pallas_call | solution.py:321
  41.6 1.3 %collective-permute-start = (f32[64,128]{1,0:T(8,128)S(1)}, f32[64,128]{1,0:T(8,128)S(1)}, u32[]{:S(2)}, u32[]{:S(2)}) collective-permute-start(f32[64,128]{1,0:T(8,128)S(1)} %get-tuple-element.19), channel_id=1, source_target_pairs={{0,1},{1,2},{2,3},{3,0},{4,5},{5,6},{6,7},{7,4},{8,9},{9,10},{10,1... | collective-permute-start | bytes 98312 | tf_op jit(solution)/shard_map/ppermute | solution.py:568
  42.9 1.5 %collective-permute-start.1 = (f32[64,128]{1,0:T(8,128)S(1)}, f32[64,128]{1,0:T(8,128)S(1)}, u32[]{:S(2)}, u32[]{:S(2)}) collective-permute-start(f32[64,128]{1,0:T(8,128)S(1)} %get-tuple-element.20), channel_id=1, source_target_pairs={{0,3},{1,0},{2,1},{3,2},{4,7},{5,4},{6,5},{7,6},{8,11},{9,8},{10,9... | collective-permute-start | bytes 98312 | tf_op jit(solution)/shard_map/ppermute | solution.py:568
  44.4 1.3 %collective-permute-done.before = f32[64,128]{1,0:T(8,128)S(1)} collective-permute-done((f32[64,128]{1,0:T(8,128)S(1)}, f32[64,128]{1,0:T(8,128)S(1)}, u32[]{:S(2)}, u32[]{:S(2)}) %collective-permute-start) | collective-permute-done | bytes 32800 | tf_op jit(solution)/shard_map/ppermute | solution.py:568
  45.7 0.3 collective-permute-done.1.after
  46.0 3.1 %relax_rim.1 = (f32[192,512]{1,0:T(8,128)S(1)}, f32[192,512]{1,0:T(8,128)S(1)}) custom-call(f32[4,256,256]{2,1,0:T(8,128)S(1)} %get-tuple-element.17.target_ref, f32[512,512]{1,0:T(8,128)S(1)} %get-tuple-element.18.prior_ref, f32[64,128]{1,0:T(8,128)S(1)} %collective-permute-done.before, f32[64,128]{1,0:T(8,128)S(1)} %collective-permute-done.1.after), custom_call_target="tpu_custom_call" | custom-call | flops 40000000 | bytes 4194304 | tf_op jit(solution)/shard_map/relax_rim/pallas_call | solution.py:551
  49.1 1.3 %collective-permute-start.2 = (f32[192,512]{1,0:T(8,128)S(1)}, f32[192,512]{1,0:T(8,128)S(1)}, u32[]{:S(2)}, u32[]{:S(2)}) collective-permute-start(f32[192,512]{1,0:T(8,128)S(1)} %get-tuple-element.21), channel_id=1, source_target_pairs={{0,4},{4,8},{8,12},{12,16},{16,20},{20,24},{24,28},{28,32},{32,36}... | collective-permute-start | bytes 1179656 | tf_op jit(solution)/shard_map/ppermute | solution.py:568
  50.4 0.0 collective-permute-start.3
  50.4 5.3 %relax_own.1.own_ref = f32[512,512]{1,0:T(8,128)S(1)} custom-call(f32[4,256,256]{2,1,0:T(8,128)S(1)} %get-tuple-element.17.target_ref, f32[512,512]{1,0:T(8,128)S(1)} %get-tuple-element.18.prior_ref, f32[64,128]{1,0:T(8,128)S(1)} %collective-permute-done.before, f32[64,128]{1,0:T(8,128)S(1)} %collective-permute-done.1.after), custom_call_target="tpu_custom_call" | custom-call | flops 40000000 | bytes 4194304 | tf_op jit(solution)/shard_map/relax_own/pallas_call | solution.py:551
  55.7 0.0 collective-permute-done.2.above_ref
  55.7 2.2 %collective-permute-done.3.below_ref = f32[192,512]{1,0:T(8,128)S(1)} collective-permute-done((f32[192,512]{1,0:T(8,128)S(1)}, f32[192,512]{1,0:T(8,128)S(1)}, u32[]{:S(2)}, u32[]{:S(2)}) %collective-permute-start.3) | collective-permute-done | bytes 393248 | tf_op jit(solution)/shard_map/ppermute | solution.py:568
  57.9 6.6 %gather.1 = (f32[4,8,16,512]{3,2,1,0:T(8,128)}, f32[512,128]{1,0:T(8,128)S(1)}) custom-call(s32[3,72]{1,0:T(4,128)S(1)} %get-tuple-element.16.items_ref, f32[512,512]{1,0:T(8,128)S(1)} %relax_own.1.own_ref, f32[192,512]{1,0:T(8,128)S(1)} %collective-permute-done.2.above_ref, f32[192,512]{1,0:T(8,128)S(1)} %collective-permute-done.3.below_ref, ...), custom_call_target="tpu_custom_call" | custom-call | tf_op jit(solution)/shard_map/gather/pallas_call | solution.py:417
  64.5 0.0 copy-start
  64.6 24.7 %all_to_all.11 = f32[64,8,128]{2,1,0:T(8,128)S(1)} all-to-all(f32[64,8,128]{2,1,0:T(8,128)S(1)} %bitcast.8), channel_id=1, replica_groups=mesh['span'=64,'depth'=4] {'span'}, dimensions={0} | all-to-all | bytes 524288 | tf_op jit(solution)/shard_map/all_to_all | solution.py:588
  89.3 0.0 copy-done
  89.3 3.5 %pick.1 = f32[4,1,8192]{2,1,0:T(1,128)} custom-call(s32[1,1]{1,0:T(1,128)S(6)} %copy.9.count_ref, s32[1,8192]{1,0:T(1,128)S(1)} %bitcast.10, f32[1,8192]{1,0:T(1,128)S(1)} %get-tuple-element.26.position_ref, f32[512,128]{1,0:T(8,128)S(1)} %bitcast.6), custom_call_target="tpu_custom_call" | custom-call | tf_op jit(solution)/shard_map/pick/pallas_call | solution.py:468
Async XLA Ops:
  41.6 4.1 %collective-permute-start = (f32[64,128]{1,0:T(8,128)S(1)}, f32[64,128]{1,0:T(8,128)S(1)}, u32[]{:S(2)}, u32[]{:S(2)}) collective-permute-start(f32[64,128]{1,0:T(8,128)S(1)} %get-tuple-element.19), channel_id=1, source_target_pairs={{0,1},{1,2},{2,3},{3,0},{4,5},{5,6},{6,7},{7,4},{8,9},{9,10},{10,1... | collective-permute-start | bytes 98312 | tf_op jit(solution)/shard_map/ppermute | solution.py:568
  42.9 3.0 %collective-permute-start.1 = (f32[64,128]{1,0:T(8,128)S(1)}, f32[64,128]{1,0:T(8,128)S(1)}, u32[]{:S(2)}, u32[]{:S(2)}) collective-permute-start(f32[64,128]{1,0:T(8,128)S(1)} %get-tuple-element.20), channel_id=1, source_target_pairs={{0,3},{1,0},{2,1},{3,2},{4,7},{5,4},{6,5},{7,6},{8,11},{9,8},{10,9... | collective-permute-start | bytes 98312 | tf_op jit(solution)/shard_map/ppermute | solution.py:568
  49.1 6.6 %collective-permute-start.2 = (f32[192,512]{1,0:T(8,128)S(1)}, f32[192,512]{1,0:T(8,128)S(1)}, u32[]{:S(2)}, u32[]{:S(2)}) collective-permute-start(f32[192,512]{1,0:T(8,128)S(1)} %get-tuple-element.21), channel_id=1, source_target_pairs={{0,4},{4,8},{8,12},{12,16},{16,20},{20,24},{24,28},{28,32},{32,36}... | collective-permute-start | bytes 1179656 | tf_op jit(solution)/shard_map/ppermute | solution.py:568
  50.4 7.5 %collective-permute-start.3 = (f32[192,512]{1,0:T(8,128)S(1)}, f32[192,512]{1,0:T(8,128)S(1)}, u32[]{:S(2)}, u32[]{:S(2)}) collective-permute-start(f32[192,512]{1,0:T(8,128)S(1)} %get-tuple-element.22), channel_id=1, source_target_pairs={{0,252},{4,0},{8,4},{12,8},{16,12},{20,16},{24,20},{28,24},{32,28}... | collective-permute-start | bytes 1179656 | tf_op jit(solution)/shard_map/ppermute | solution.py:568
  64.5 24.8 %copy-start = (s32[1,8192,1]{1,2,0:T(1,128)S(1)}, s32[1,8192,1]{1,2,0:T(1,128)}, u32[]{:S(2)}) copy-start(s32[1,8192,1]{1,2,0:T(1,128)} %param.7) | copy-start | bytes 98308

commit v8 on v7

--- a/solution.py
+++ b/solution.py
@@ -90,7 +90,7 @@
 
 PACK_BLOCK = 4096
 SUB = 256
-CLASSES = 4
+CLASSES = 8
 
 
 def pack_kernel(
@@ -115,7 +115,7 @@
 
     def classes(start, size):
         cell = cell_ref[0:1, pl.ds(start, size)]
-        return (lax.shift_right_logical(cell, 8) & 1) * 2 + (lax.shift_right_logical(cell, 12) & 1)
+        return (lax.shift_right_logical(cell, 8) & 1) * 4 + (lax.shift_right_logical(cell, 11) & 3)
 
     def count_step(block, counts):
         start = pl.multiple_of(block * PACK_BLOCK, PACK_BLOCK)
@@ -140,7 +140,10 @@
             spot = pl.ds(start, SUB)
             slab = live_slab(start, SUB)
             member = row_is(slab.astype(F32), OWNERS)
-            sorted_one = one_hot((slab + classes(start, SUB) * OWNERS).astype(F32), CLASSES * OWNERS)
+            order = slab + classes(start, SUB) * OWNERS
+            sorted_one = jnp.concatenate(
+                [one_hot((order - base).astype(F32), 256) for base in range(0, CLASSES * OWNERS, 256)], axis=0
+            )
             ranks = dot_nn(sorted_one, upper)
             place = ranks + jnp.concatenate([offset, offset], axis=1)
             position = jnp.sum(place * sorted_one.astype(F32), axis=0, keepdims=True) - 1.0
@@ -195,8 +198,8 @@
 
 CHUNKS, CHUNK = 16, 1024
 CLASS_HIGH = HI // CLASSES
-ABREAST = 4
-ITEMS = CHUNKS * CLASSES + 8
+ABREAST = 8
+ITEMS = CHUNKS * CLASSES + 16
 NOWHERE = 1024
 
 
@@ -241,7 +244,7 @@
         low_ref[chunk] = (cell & 255).astype(F32)
         values[0, chunk] = volumes[chunk]
         live = volumes[chunk] > 0.0
-        kind = lax.shift_right_logical(high, 6).astype(F32)
+        kind = lax.shift_right_logical(high, 5).astype(F32)
         bounds_ref[chunk, 0] = jnp.min(jnp.where(live, kind, float(CLASSES))).astype(I32)
         bounds_ref[chunk, 1] = jnp.max(jnp.where(live, kind, -1.0)).astype(I32) + 1
     for comp in range(1, 4):
@@ -276,17 +279,24 @@
             for comp in range(4):
                 value = values[comp, chunk]
                 top = value.astype(BF16).astype(F32)
-                left.append(
-                    jnp.concatenate(
-                        [
-                            jnp.where(members[r], spread(piece[r : r + 1], CLASS_HIGH), zero)
-                            for piece in (top, value - top)
-                            for r in range(8)
-                        ],
-                        axis=1,
+                for piece in (top, value - top):
+                    left.append(
+                        jnp.concatenate(
+                            [jnp.where(members[r], spread(piece[r : r + 1], CLASS_HIGH), zero) for r in range(8)],
+                            axis=1,
+                        )
                     )
+            total = dot_nt(jnp.concatenate(left, axis=0), lows)
+            totals.append(
+                jnp.concatenate(
+                    [
+                        total[2 * comp * CLASS_HIGH : (2 * comp + 1) * CLASS_HIGH]
+                        + total[(2 * comp + 1) * CLASS_HIGH : (2 * comp + 2) * CLASS_HIGH]
+                        for comp in range(4)
+                    ],
+                    axis=0,
                 )
-            totals.append(dot_nt(jnp.concatenate(left, axis=0), jnp.concatenate([lows, lows], axis=1)))
+            )
         for item in range(ABREAST):
             spot = pl.ds(pl.multiple_of(items_ref[2, index * ABREAST + item], CLASS_HIGH), CLASS_HIGH)
             for comp in range(4):
@@ -384,8 +394,9 @@
             lows = low_hots(low_ref, chunk)
             spot = pl.ds(pl.multiple_of(items_ref[2, index * ABREAST + item], CLASS_HIGH), CLASS_HIGH)
             members = [ids == key[r : r + 1] for r in range(8)]
-            table = [jnp.concatenate([part[comp, spot, :] for comp in range(4)], axis=0) for part in (tops, bottoms)]
-            value = dot_nn(table[0], lows) + dot_nn(table[1], lows)
+            table = jnp.concatenate([part[comp, spot, :] for part in (tops, bottoms) for comp in range(4)], axis=0)
+            value = dot_nn(table, lows)
+            value = value[: 4 * CLASS_HIGH] + value[4 * CLASS_HIGH :]
             new = []
             for comp in range(4):
                 rows = value[comp * CLASS_HIGH : (comp + 1) * CLASS_HIGH]

time: 93.2 us -> 91.2 us (0.979)
  blocking collectives: 50.9 us -> 48 us
  Pallas kernels: 32.6 us -> 34.4 us
    all_to_all x1, blocking collectives: 24.7 us -> 21.8 us  [on_device(): lax.all_to_all(returned.reshape(OWNERS, BACK_ROWS, 128), 'span', 0, 0, ti...]
    pallas_call x1, Pallas kernels: 7.15 us -> 8.95 us  [pack(): pl.pallas_call(pack_kernel, out_shape=(jax.ShapeDtypeStruct((OWNERS * ROW...]
  transfers between devices with their start and end apart: 4 -> 4, of which waited for: 3 -> 2; matrix products, arithmetic and copies ran while one was open for 0% -> 0% of each run, Pallas kernels for 6% -> 6%
where the time goes in v8:
time: 91.2 us; the launch traced here: 90.4 us
  blocking collectives  48 us (53%)
  Pallas kernels  34.4 us (38%)
  starting transfers between devices  3.34 us (4%)
  waiting for transfers between devices  3.28 us (4%)
  between operations  1.34 us (1%)
    all_to_all x1, blocking collectives, on_device(): lax.all_to_all(sent.reshape(OWNERS, 5, 2, 128), 'span', 0, 0, tiled=True)  26.2 us
    all_to_all x1, blocking collectives, on_device(): lax.all_to_all(returned.reshape(OWNERS, BACK_ROWS, 128), 'span', 0, 0, ti...  21.8 us
    pallas_call x1, Pallas kernels, pack(): pl.pallas_call(pack_kernel, out_shape=(jax.ShapeDtypeStruct((OWNERS * ROW...  8.95 us
    pallas_call x2, Pallas kernels, relax(): pl.pallas_call(functools.partial(relax_kernel, for_rim), out_shape=(rim,...  8.41 us
    pallas_call x1, Pallas kernels, deposit(): pl.pallas_call(deposit_kernel, out_shape=(jax.ShapeDtypeStruct((4, HI, LO...  7.13 us
    pallas_call x1, Pallas kernels, gather(): pl.pallas_call(gather_kernel, out_shape=(jax.ShapeDtypeStruct((4, LAYERS,...  6.47 us
    pallas_call x1, Pallas kernels, pick(): pl.pallas_call(pick_kernel, out_shape=jax.ShapeDtypeStruct((4, 1, PARTS),...  3.47 us
    ppermute x4, starting transfers between devices, shifted(): lax.ppermute(array, axis, [(i, (i + step) % count) for i in range(count)])  3.34 us
  transfers between devices with their start and end apart: 4, of which 2 were waited for; matrix products, arithmetic and copies ran while one was open for 0% of the time, Pallas kernels for 6%

profile of v8, /device:TPU:1, one launch (start us, length us, event | category | flops | bytes accessed | tf_op | source)
XLA Modules:
  0.0 90.4 jit_solution(1448930937386114143)
XLA Ops:
  1.3 8.9 %pack.1 = (f32[640,128]{1,0:T(8,128)S(1)}, f32[1,8192]{1,0:T(1,128)S(1)}) custom-call(s32[1,1]{1,0:T(1,128)S(6)} %copy.9.count_ref, s32[1,8192]{1,0:T(1,128)} %bitcast.9, s32[1,8192]{1,0:T(1,128)} %cell_any.1, f32[1,8192]{1,0:T(1,128)} %volume_any.1, f32[3,1,8192]{2,1,0:T(1,128)} %drag_any.2), custom_call_target="tpu_custom_call" | custom-call | tf_op jit(solution)/shard_map/pack/pallas_call | solution.py:178
  10.2 26.2 %all_to_all.10 = f32[64,5,2,128]{3,2,1,0:T(2,128)S(1)} all-to-all(f32[64,5,2,128]{3,2,1,0:T(2,128)S(1)} %bitcast.7), channel_id=1, replica_groups=mesh['span'=64,'depth'=4] {'span'}, dimensions={0} | all-to-all | bytes 655360 | tf_op jit(solution)/shard_map/all_to_all | solution.py:586
  36.4 7.1 %deposit.1 = (f32[4,256,256]{2,1,0:T(8,128)S(1)}, f32[64,128]{1,0:T(8,128)S(1)}, f32[64,128]{1,0:T(8,128)S(1)}, f32[512,512]{1,0:T(8,128)S(1)}, f32[16,8,128]{2,...) custom-call(f32[640,128]{1,0:T(8,128)S(1)} %bitcast.5, f32[8,16,512]{2,1,0:T(8,128)} %solid_any.1, ...), custom_call_target="tpu_custom_call" | custom-call | tf_op jit(solution)/shard_map/deposit/pallas_call | solution.py:331
  43.6 1.3 %collective-permute-start = (f32[64,128]{1,0:T(8,128)S(1)}, f32[64,128]{1,0:T(8,128)S(1)}, u32[]{:S(2)}, u32[]{:S(2)}) collective-permute-start(f32[64,128]{1,0:T(8,128)S(1)} %get-tuple-element.19), channel_id=1, source_target_pairs={{0,1},{1,2},{2,3},{3,0},{4,5},{5,6},{6,7},{7,4},{8,9},{9,10},{10,1... | collective-permute-start | bytes 98312 | tf_op jit(solution)/shard_map/ppermute | solution.py:579
  44.9 1.5 %collective-permute-start.1 = (f32[64,128]{1,0:T(8,128)S(1)}, f32[64,128]{1,0:T(8,128)S(1)}, u32[]{:S(2)}, u32[]{:S(2)}) collective-permute-start(f32[64,128]{1,0:T(8,128)S(1)} %get-tuple-element.20), channel_id=1, source_target_pairs={{0,3},{1,0},{2,1},{3,2},{4,7},{5,4},{6,5},{7,6},{8,11},{9,8},{10,9... | collective-permute-start | bytes 98312 | tf_op jit(solution)/shard_map/ppermute | solution.py:579
  46.3 1.3 %collective-permute-done.before = f32[64,128]{1,0:T(8,128)S(1)} collective-permute-done((f32[64,128]{1,0:T(8,128)S(1)}, f32[64,128]{1,0:T(8,128)S(1)}, u32[]{:S(2)}, u32[]{:S(2)}) %collective-permute-start) | collective-permute-done | bytes 32800 | tf_op jit(solution)/shard_map/ppermute | solution.py:579
  47.6 0.0 collective-permute-done.1.after
  47.6 3.1 %relax_rim.1 = (f32[192,512]{1,0:T(8,128)S(1)}, f32[192,512]{1,0:T(8,128)S(1)}) custom-call(f32[4,256,256]{2,1,0:T(8,128)S(1)} %get-tuple-element.17.target_ref, f32[512,512]{1,0:T(8,128)S(1)} %get-tuple-element.18.prior_ref, f32[64,128]{1,0:T(8,128)S(1)} %collective-permute-done.before, f32[64,128]{1,0:T(8,128)S(1)} %collective-permute-done.1.after), custom_call_target="tpu_custom_call" | custom-call | flops 40000000 | bytes 4194304 | tf_op jit(solution)/shard_map/relax_rim/pallas_call | solution.py:562
  50.8 0.1 collective-permute-start.2
  50.9 0.4 collective-permute-start.3
  51.4 5.3 %relax_own.1.own_ref = f32[512,512]{1,0:T(8,128)S(1)} custom-call(f32[4,256,256]{2,1,0:T(8,128)S(1)} %get-tuple-element.17.target_ref, f32[512,512]{1,0:T(8,128)S(1)} %get-tuple-element.18.prior_ref, f32[64,128]{1,0:T(8,128)S(1)} %collective-permute-done.before, f32[64,128]{1,0:T(8,128)S(1)} %collective-permute-done.1.after), custom_call_target="tpu_custom_call" | custom-call | flops 40000000 | bytes 4194304 | tf_op jit(solution)/shard_map/relax_own/pallas_call | solution.py:562
  56.6 0.0 collective-permute-done.2.above_ref
  56.7 2.0 %collective-permute-done.3.below_ref = f32[192,512]{1,0:T(8,128)S(1)} collective-permute-done((f32[192,512]{1,0:T(8,128)S(1)}, f32[192,512]{1,0:T(8,128)S(1)}, u32[]{:S(2)}, u32[]{:S(2)}) %collective-permute-start.3) | collective-permute-done | bytes 393248 | tf_op jit(solution)/shard_map/ppermute | solution.py:579
  58.6 6.5 %gather.1 = (f32[4,8,16,512]{3,2,1,0:T(8,128)}, f32[512,128]{1,0:T(8,128)S(1)}) custom-call(s32[3,144]{1,0:T(4,128)S(1)} %get-tuple-element.16.items_ref, f32[512,512]{1,0:T(8,128)S(1)} %relax_own.1.own_ref, f32[192,512]{1,0:T(8,128)S(1)} %collective-permute-done.2.above_ref, f32[192,512]{1,0:T(8,128)S(1)} %collective-permute-done.3.below_ref, ...), custom_call_target="tpu_custom_call" | custom-call | tf_op jit(solution)/shard_map/gather/pallas_call | solution.py:428
  65.1 0.0 copy-start
  65.1 21.8 %all_to_all.11 = f32[64,8,128]{2,1,0:T(8,128)S(1)} all-to-all(f32[64,8,128]{2,1,0:T(8,128)S(1)} %bitcast.8), channel_id=1, replica_groups=mesh['span'=64,'depth'=4] {'span'}, dimensions={0} | all-to-all | bytes 524288 | tf_op jit(solution)/shard_map/all_to_all | solution.py:599
  86.9 0.0 copy-done
  86.9 3.5 %pick.1 = f32[4,1,8192]{2,1,0:T(1,128)} custom-call(s32[1,1]{1,0:T(1,128)S(6)} %copy.9.count_ref, s32[1,8192]{1,0:T(1,128)S(1)} %bitcast.10, f32[1,8192]{1,0:T(1,128)S(1)} %get-tuple-element.26.position_ref, f32[512,128]{1,0:T(8,128)S(1)} %bitcast.6), custom_call_target="tpu_custom_call" | custom-call | tf_op jit(solution)/shard_map/pick/pallas_call | solution.py:479
Async XLA Ops:
  43.6 4.1 %collective-permute-start = (f32[64,128]{1,0:T(8,128)S(1)}, f32[64,128]{1,0:T(8,128)S(1)}, u32[]{:S(2)}, u32[]{:S(2)}) collective-permute-start(f32[64,128]{1,0:T(8,128)S(1)} %get-tuple-element.19), channel_id=1, source_target_pairs={{0,1},{1,2},{2,3},{3,0},{4,5},{5,6},{6,7},{7,4},{8,9},{9,10},{10,1... | collective-permute-start | bytes 98312 | tf_op jit(solution)/shard_map/ppermute | solution.py:579
  44.9 2.8 %collective-permute-start.1 = (f32[64,128]{1,0:T(8,128)S(1)}, f32[64,128]{1,0:T(8,128)S(1)}, u32[]{:S(2)}, u32[]{:S(2)}) collective-permute-start(f32[64,128]{1,0:T(8,128)S(1)} %get-tuple-element.20), channel_id=1, source_target_pairs={{0,3},{1,0},{2,1},{3,2},{4,7},{5,4},{6,5},{7,6},{8,11},{9,8},{10,9... | collective-permute-start | bytes 98312 | tf_op jit(solution)/shard_map/ppermute | solution.py:579
  50.8 5.9 %collective-permute-start.2 = (f32[192,512]{1,0:T(8,128)S(1)}, f32[192,512]{1,0:T(8,128)S(1)}, u32[]{:S(2)}, u32[]{:S(2)}) collective-permute-start(f32[192,512]{1,0:T(8,128)S(1)} %get-tuple-element.21), channel_id=1, source_target_pairs={{0,4},{4,8},{8,12},{12,16},{16,20},{20,24},{24,28},{28,32},{32,36}... | collective-permute-start | bytes 1179656 | tf_op jit(solution)/shard_map/ppermute | solution.py:579
  50.9 7.7 %collective-permute-start.3 = (f32[192,512]{1,0:T(8,128)S(1)}, f32[192,512]{1,0:T(8,128)S(1)}, u32[]{:S(2)}, u32[]{:S(2)}) collective-permute-start(f32[192,512]{1,0:T(8,128)S(1)} %get-tuple-element.22), channel_id=1, source_target_pairs={{0,252},{4,0},{8,4},{12,8},{16,12},{20,16},{24,20},{28,24},{32,28}... | collective-permute-start | bytes 1179656 | tf_op jit(solution)/shard_map/ppermute | solution.py:579
  65.1 21.8 %copy-start = (s32[1,8192,1]{1,2,0:T(1,128)S(1)}, s32[1,8192,1]{1,2,0:T(1,128)}, u32[]{:S(2)}) copy-start(s32[1,8192,1]{1,2,0:T(1,128)} %param.7) | copy-start | bytes 98308
